TPU v7x, 128 devices: a whole 4x4x4 slice. The times are simulated.
128 devices in a mesh: tp: 16 (over z, y), dp: 8 (over x, core).
Axes of the slice: x: 4, y: 4, z: 4, core: 2. Of those that a mesh axis runs over, the one named last changes fastest.
Arguments:
- x: bfloat16 [8192, 4096], P(('dp', 'tp'))
- w_gate: bfloat16 [4096, 14336], P('dp', 'tp')
- w_up: bfloat16 [4096, 14336], P('dp', 'tp')
- w_down: bfloat16 [14336, 4096], P('tp', 'dp')
- dy: bfloat16 [8192, 4096], P(('dp', 'tp'))
Outputs:
- output 1: bfloat16 [8192, 4096], P(('dp', 'tp'))
- output 2: bfloat16 [8192, 4096], P(('dp', 'tp'))
- output 3: float32 [4096, 14336], P('dp', 'tp')
- output 4: float32 [4096, 14336], P('dp', 'tp')
- output 5: float32 [14336, 4096], P('tp', 'dp')
All inputs are finite; a program needn't handle non-finite values.
Results may differ from a plain program's by a relative error of at most 0.001.
Values are sent between devices in bfloat16 or wider.
A program may use at most 1 GiB of HBM per device.

v0:
```python
import jax
import jax.numpy as jnp
from jax import lax
from jax.sharding import PartitionSpec as P


def solution(mesh):
    nx = mesh.shape["dp"]
    ny = mesh.shape["tp"]
    rows = P(("dp", "tp"), None)
    wsp = P("dp", "tp")
    dsp = P("tp", "dp")
    f32 = jnp.float32
    bf = jnp.bfloat16

    def to_columns(v):
        tl = v.shape[0]
        dl = v.shape[1] // nx
        vr = v.reshape(tl, nx, dl).transpose(1, 0, 2)
        return lax.all_to_all(vr, "dp", 0, 0, tiled=True)

    def from_columns(v):
        tl = v.shape[1]
        dl = v.shape[2]
        vr = lax.all_to_all(v, "dp", 0, 0, tiled=True)
        return vr.transpose(1, 0, 2).reshape(tl, nx * dl)

    def all_tokens(va):
        vg = lax.all_gather(va, "tp", axis=0, tiled=False)
        tl = vg.shape[2]
        dl = vg.shape[3]
        return vg.transpose(1, 0, 2, 3).reshape(nx * ny * tl, dl)

    def combine_tp(q, res):
        dl = q.shape[1]
        tl = q.shape[0] // (nx * ny)
        qs = lax.psum_scatter(q.reshape(nx, ny, tl, dl), "tp", scatter_dimension=1, tiled=True)
        out = res.astype(f32) + qs.reshape(nx, tl, dl)
        return from_columns(out.astype(bf))

    def local(x, w_gate, w_up, w_down, dy):
        fl = w_gate.shape[1]
        w = jnp.concatenate([w_gate, w_up], axis=1)
        xa = to_columns(x)
        xt = all_tokens(xa)
        p = lax.psum_scatter(jnp.dot(xt, w, preferred_element_type=f32), "dp", scatter_dimension=0, tiled=True)
        a = p[:, :fl]
        b = p[:, fl:]
        sig = jax.nn.sigmoid(a)
        sa = a * sig
        h = (sa * b).astype(bf)
        hg = lax.all_gather(h, "dp", axis=0, tiled=True)
        y = combine_tp(jnp.dot(hg, w_down, preferred_element_type=f32), xa)
        dya = to_columns(dy)
        dyt = all_tokens(dya)
        g = lax.psum_scatter(jnp.dot(dyt, w_down.T, preferred_element_type=f32), "dp", scatter_dimension=0, tiled=True)
        da = (g * b * sig * (1.0 + a * (1.0 - sig))).astype(bf)
        db = (g * sa).astype(bf)
        dab = lax.all_gather(jnp.concatenate([da, db], axis=1), "dp", axis=0, tiled=True)
        dx = combine_tp(jnp.dot(dab, w.T, preferred_element_type=f32), dya)
        dw = jnp.dot(xt.T, dab, preferred_element_type=f32)
        dw_down = jnp.dot(hg.T, dyt, preferred_element_type=f32)
        return y, dx, dw[:, :fl], dw[:, fl:], dw_down

    return jax.shard_map(local, mesh=mesh, in_specs=(rows, wsp, wsp, dsp, rows), out_specs=(rows, rows, wsp, wsp, dsp), check_vma=False)
```

profile of v0, /device:TPU:1, one launch (start us, length us, event | category | flops | bytes accessed | tf_op | source)
XLA Modules:
  0.0 1109.6 jit_solution(7239601318528146887)
XLA Ops:
  7.2 0.0 copy-start
  7.2 0.0 copy-start.6
  7.2 0.0 all-gather.13.cloned.1.call-start
  7.2 1.3 copy.70
  8.6 0.2 copy.58
  8.7 14.9 %all_to_all.20 = bf16[8,64,512]{2,1,0:T(8,128)(2,1)} all-to-all(bf16[8,64,512]{2,1,0:T(8,128)(2,1)S(1)} %copy.58), channel_id=1, replica_groups=mesh['tp'=16,'dp'=8] {'dp'}, dimensions={0} | all-to-all | bytes 1048576 | tf_op jit(solution)/shard_map/all_to_all | solution.py:20
  23.6 0.0 all-gather.13.cloned.1.call-update
  23.7 0.0 all-gather.11.cloned.1.call-start
  23.7 0.0 copy-done.6
  23.7 0.2 copy.69
  23.9 0.2 copy.53
  24.1 13.4 %all_to_all.21 = bf16[8,64,512]{2,1,0:T(8,128)(2,1)} all-to-all(bf16[8,64,512]{2,1,0:T(8,128)(2,1)S(1)} %copy.53), channel_id=1, replica_groups=mesh['tp'=16,'dp'=8] {'dp'}, dimensions={0} | all-to-all | bytes 1048576 | tf_op jit(solution)/shard_map/all_to_all | solution.py:20
  37.5 0.0 all-gather.11.cloned.1.call-update
  37.5 0.0 reduce-scatter.11.cloned.1.call-start
  37.6 57.7 %all-gather.13.cloned.1.call-done = bf16[128,64,512]{2,1,0:T(8,128)(2,1)} async-done(((bf16[8,64,512]{2,1,0:T(8,128)(2,1)}), bf16[128,64,512]{2,1,0:T(8,128)(2,1)}) %all-gather.13.cloned.1.call-update) | async-done | bytes 8388624 | tf_op jit(solution)/shard_map/all_gather | solution.py:29
  95.3 7.8 copy.59
  103.1 0.0 copy-done
  103.1 16.9 %fusion.5 = f32[8192,896]{0,1:T(8,128)} fusion(bf16[8192,512]{1,0:T(8,128)(2,1)} %bitcast.53, bf16[896,512]{1,0:T(8,128)(2,1)S(1)} %copy-done), kind=kOutput, calls=%fused_computation.16 | convolution fusion | flops 7516192768 | bytes 38666240 | tf_op jit(solution)/shard_map/dot_general | solution.py:56
  120.0 0.0 reduce-scatter.11.cloned.1.call-update
  120.0 0.0 reduce-scatter.9.cloned.1.call-start
  120.1 1.1 copy-done.4
  121.2 1.0 constant_dynamic-update-slice_fusion.1
  122.2 0.0 copy-done.5
  122.2 1.0 constant_dynamic-update-slice_fusion
  123.2 44.6 %all-gather.11.cloned.1.call-done = bf16[128,64,512]{2,1,0:T(8,128)(2,1)} async-done(((bf16[8,64,512]{2,1,0:T(8,128)(2,1)}), bf16[128,64,512]{2,1,0:T(8,128)(2,1)}) %all-gather.11.cloned.1.call-update) | async-done | bytes 8388624 | tf_op jit(solution)/shard_map/all_gather | solution.py:29
  167.8 7.8 copy.54
  175.6 27.6 %convolution_bitcast_fusion = f32[8192,1792]{0,1:T(8,128)} fusion(bf16[512,1792]{1,0:T(8,128)(2,1)} %constant_dynamic-update-slice_fusion, bf16[8192,512]{1,0:T(8,128)(2,1)} %bitcast.51), kind=kOutput, calls=%fused_computation | convolution fusion | flops 15032385536 | bytes 68943872 | tf_op jit(solution)/shard_map/dot_general | solution.py:46
  203.2 0.0 reduce-scatter.9.cloned.1.call-update
  203.2 0.2 all-gather.7.cloned.1.call-start
  203.4 117.4 %reduce-scatter.11.cloned.1.call-done = f32[1024,896]{0,1:T(8,128)} async-done(((f32[8192,896]{0,1:T(8,128)}), f32[1024,896]{0,1:T(8,128)}) %reduce-scatter.11.cloned.1.call-update) | async-done | bytes 3670032 | tf_op jit(solution)/shard_map/reduce_scatter | solution.py:56
  320.8 290.9 %reduce-scatter.9.cloned.1.call-done = f32[1024,1792]{0,1:T(8,128)} async-done(((f32[8192,1792]{0,1:T(8,128)}), f32[1024,1792]{0,1:T(8,128)}) %reduce-scatter.9.cloned.1.call-update) | async-done | bytes 7340048 | tf_op jit(solution)/shard_map/reduce_scatter | solution.py:46
  611.7 6.7 multiply_convert_fusion.1
  618.4 0.0 all-gather.7.cloned.1.call-update
  618.5 0.0 all-gather.9.cloned.1.call-start
  618.5 3.7 pad_maximum_fusion
  622.2 0.0 all-gather.9.cloned.1.call-update
  622.3 0.0 reduce-scatter.13.cloned.1.call-start
  622.3 73.1 %all-gather.7.cloned.1.call-done = bf16[8192,896]{0,1:T(8,128)(2,1)} async-done(((bf16[1024,896]{0,1:T(8,128)(2,1)}), bf16[8192,896]{0,1:T(8,128)(2,1)}) %all-gather.7.cloned.1.call-update) | async-done | bytes 14680080 | tf_op jit(solution)/shard_map/all_gather | solution.py:52
  695.4 12.6 %fusion.4 = f32[8192,512]{1,0:T(8,128)S(1)} fusion(bf16[8192,896]{0,1:T(8,128)(2,1)} %all-gather.7.cloned.1.call-done, bf16[896,512]{1,0:T(8,128)(2,1)S(1)} %copy-done), kind=kOutput, calls=%fused_computation.15 | convolution fusion | flops 7516192768 | bytes 32374784 | tf_op jit(solution)/shard_map/dot_general | solution.py:53
  708.0 12.0 %copy.55 = f32[8,16,64,512]{3,0,2,1:T(8,128)} copy(f32[8,16,64,512]{3,2,1,0:T(8,128)S(1)} %bitcast.50) | data formatting | bytes 33554432 | tf_op jit(solution)/shard_map/reshape | solution.py:37
  720.0 0.0 reduce-scatter.13.cloned.1.call-update
  720.0 0.3 reduce-scatter.15.cloned.1.call-start
  720.2 116.0 %all-gather.9.cloned.1.call-done = bf16[8192,1792]{0,1:T(8,128)(2,1)} async-done(((bf16[1024,1792]{0,1:T(8,128)(2,1)}), bf16[8192,1792]{0,1:T(8,128)(2,1)}) %all-gather.9.cloned.1.call-update) | async-done | bytes 29360144 | tf_op jit(solution)/shard_map/all_gather | solution.py:59
  836.2 24.8 %fusion.6 = f32[8192,512]{1,0:T(8,128)} fusion(bf16[8192,1792]{0,1:T(8,128)(2,1)} %all-gather.9.cloned.1.call-done, bf16[512,1792]{1,0:T(8,128)(2,1)} %constant_dynamic-update-slice_fusion), kind=kOutput, calls=%fused_computation.17 | convolution fusion | flops 15032385536 | bytes 47972352 | tf_op jit(solution)/shard_map/dot_general | solution.py:60
  861.0 18.0 %copy.61 = f32[8,16,64,512]{3,0,2,1:T(8,128)} copy(f32[8,16,64,512]{3,2,1,0:T(8,128)} %bitcast.49) | data formatting | bytes 33554432 | tf_op jit(solution)/shard_map/reshape | solution.py:37
  879.0 0.0 copy-start.3
  879.0 0.0 reduce-scatter.15.cloned.1.call-update
  879.0 71.2 %reduce-scatter.13.cloned.1.call-done = f32[8,1,64,512]{3,0,2,1:T(8,128)} async-done(((f32[8,16,64,512]{3,0,2,1:T(8,128)}), f32[8,1,64,512]{3,0,2,1:T(8,128)}) %reduce-scatter.13.cloned.1.call-update) | async-done | bytes 1048592
  950.2 0.0 copy-done.3
  950.2 2.6 fusion.2
  952.8 5.8 all-to-all-start.1
  958.6 14.3 %fusion.7 = f32[896,512]{1,0:T(8,128)} fusion(bf16[8192,896]{0,1:T(8,128)(2,1)} %all-gather.7.cloned.1.call-done, bf16[8192,512]{1,0:T(8,128)(2,1)} %bitcast.54), kind=kOutput, calls=%fused_computation.18 | convolution fusion | flops 7516192768 | bytes 24903680 | tf_op jit(solution)/shard_map/dot_general | solution.py:62
  972.9 90.8 %reduce-scatter.15.cloned.1.call-done = f32[8,1,64,512]{3,0,2,1:T(8,128)} async-done(((f32[8,16,64,512]{3,0,2,1:T(8,128)}), f32[8,1,64,512]{3,0,2,1:T(8,128)}) %reduce-scatter.15.cloned.1.call-update) | async-done | bytes 1048592
  1063.8 0.0 copy-done.2
  1063.8 2.6 fusion.1
  1066.4 0.0 all-to-all-done.1
  1066.4 5.8 all-to-all-start.3
  1072.2 21.4 %convolution_bitcast_fusion.1 = f32[512,1792]{0,1:T(8,128)S(1)} fusion(bf16[8192,1792]{0,1:T(8,128)(2,1)} %all-gather.9.cloned.1.call-done, bf16[8192,512]{1,0:T(8,128)(2,1)} %bitcast.52), kind=kOutput, calls=%fused_computation.7 | convolution fusion | flops 15032385536 | bytes 41418752 | tf_op jit(solution)/shard_map/dot_general | solution.py:61
  1093.5 1.6 fusion.3
  1095.1 2.8 copy.64
  1097.9 1.7 copy.65
  1099.6 0.8 copy.67
  1100.4 0.0 all-to-all-done.3
  1100.4 1.9 copy.68
  (5 shorter events, 0.0 us)
Async XLA Ops:
  7.2 95.9 %copy-start = (bf16[896,512]{1,0:T(8,128)(2,1)S(1)}, bf16[896,512]{1,0:T(8,128)(2,1)}, u32[]{:S(2)}) copy-start(bf16[896,512]{1,0:T(8,128)(2,1)} %param.8) | copy-start | bytes 2752516
  7.2 16.5 %copy-start.6 = (bf16[64,4096]{1,0:T(8,128)(2,1)S(1)}, bf16[64,4096]{1,0:T(8,128)(2,1)}, u32[]{:S(2)}) copy-start(bf16[64,4096]{1,0:T(8,128)(2,1)} %param.5) | copy-start | bytes 1572868
  7.2 88.1 %all-gather.13.cloned.1.call-start = ((), (), s32[]{:S(2)}) async-start(), calls=%async_computation.13 | async-start | bytes 8912896 | tf_op jit(solution)/shard_map/all_gather | solution.py:29
  23.7 144.1 %all-gather.11.cloned.1.call-start = ((), (), s32[]{:S(2)}) async-start(), calls=%async_computation.12 | async-start | bytes 8912896 | tf_op jit(solution)/shard_map/all_gather | solution.py:29
  37.5 283.3 %reduce-scatter.11.cloned.1.call-start = ((), (), s32[]{:S(2)}) async-start(), calls=%async_computation.10 | async-start | bytes 33030144 | tf_op jit(solution)/shard_map/reduce_scatter | solution.py:56
  120.0 1.2 copy-start.4
  120.0 2.2 copy-start.5
  120.0 491.7 %reduce-scatter.9.cloned.1.call-start = ((), (), s32[]{:S(2)}) async-start(), calls=%async_computation.8 | async-start | bytes 66060288 | tf_op jit(solution)/shard_map/reduce_scatter | solution.py:46
  203.2 492.2 %all-gather.7.cloned.1.call-start = ((), (), s32[]{:S(2)}) async-start(), calls=%async_computation.9 | async-start | bytes 16515072 | tf_op jit(solution)/shard_map/all_gather | solution.py:52
  618.5 217.7 %all-gather.9.cloned.1.call-start = ((), (), s32[]{:S(2)}) async-start(), calls=%async_computation.11 | async-start | bytes 33030144 | tf_op jit(solution)/shard_map/all_gather | solution.py:59
  622.3 328.0 %reduce-scatter.13.cloned.1.call-start = ((), (), s32[]{:S(2)}) async-start(), calls=%async_computation.14 | async-start | bytes 17825792
  720.0 343.8 %reduce-scatter.15.cloned.1.call-start = ((), (), s32[]{:S(2)}) async-start(), calls=%async_computation.15 | async-start | bytes 17825792
  879.0 71.3 %copy-start.3 = (bf16[8,64,512]{2,1,0:T(8,128)(2,1)S(1)}, bf16[8,64,512]{2,1,0:T(8,128)(2,1)}, u32[]{:S(2)}) copy-start(bf16[8,64,512]{2,1,0:T(8,128)(2,1)} %all_to_all.21) | copy-start | bytes 1572868
  952.8 113.6 %all-to-all-start.1 = ((bf16[8,64,512]{2,1,0:T(8,128)(2,1)}), bf16[8,64,512]{2,1,0:T(8,128)(2,1)S(1)}, u32[]{:S(2)}, u32[]{:S(2)}) async-start(bf16[8,64,512]{2,1,0:T(8,128)(2,1)} %fusion.2), calls=%async_computation.2 | async-start | bytes 1048576 | tf_op jit(solution)/shard_map/all_to_all | solution.py:25
  958.6 105.2 %copy-start.2 = (bf16[8,64,512]{2,1,0:T(8,128)(2,1)S(1)}, bf16[8,64,512]{2,1,0:T(8,128)(2,1)}, u32[]{:S(2)}) copy-start(bf16[8,64,512]{2,1,0:T(8,128)(2,1)} %all_to_all.20) | copy-start | bytes 1572868
  1066.4 34.0 %all-to-all-start.3 = ((bf16[8,64,512]{2,1,0:T(8,128)(2,1)}), bf16[8,64,512]{2,1,0:T(8,128)(2,1)}, u32[]{:S(2)}, u32[]{:S(2)}) async-start(bf16[8,64,512]{2,1,0:T(8,128)(2,1)} %fusion.1), calls=%async_computation.5 | async-start | bytes 1048576 | tf_op jit(solution)/shard_map/all_to_all | solution.py:25
  1095.1 7.2 copy-start.1
Sparse Core Ops, SparseCore 0:
  23.8 71.4 all-gather.12
  97.4 70.2 all-gather.10
  170.2 150.5 reduce-scatter.10
  323.2 288.5 reduce-scatter.8
  618.6 76.7 all-gather.6
  696.9 139.2 all-gather.8
  839.6 110.5 reduce-scatter.12
  953.6 110.1 reduce-scatter.14
where the time goes:
time: 1120 us; the launch traced here: 1110 us
  waiting for transfers between devices  862 us (77%)
  matrix products  118 us (11%)
  local copies, waits for them, and re-layouts  59.3 us (5%)
  blocking collectives  28.3 us (3%)
  other arithmetic  15.6 us (1%)
  between operations  14.7 us (1%)
  starting transfers between devices  12.2 us (1%)
    reduce_scatter x1, waiting for transfers between devices, local(): lax.psum_scatter(jnp.dot(xt, w, preferred_element_type=f32), 'dp', scatte...  291 us
    unnamed x10, waiting for transfers between devices  162 us
    reduce_scatter x1, waiting for transfers between devices, local(): lax.psum_scatter(jnp.dot(dyt, w_down.T, preferred_element_type=f32), 'dp'...  117 us
    all_gather x1, waiting for transfers between devices, local(): lax.all_gather(jnp.concatenate([da, db], axis=1), 'dp', axis=0, tiled=True)  116 us
    all_gather x2, waiting for transfers between devices, all_tokens(): vg = lax.all_gather(va, 'tp', axis=0, tiled=False)  102 us
    all_gather x1, waiting for transfers between devices, local(): hg = lax.all_gather(h, 'dp', axis=0, tiled=True)  73.1 us
    reshape x2, local copies, waits for them, and re-layouts, combine_tp(): q.reshape(nx, ny, tl, dl)  29.9 us
    all_to_all x2, blocking collectives, to_columns(): return lax.all_to_all(vr, 'dp', 0, 0, tiled=True)  28.3 us
  transfers between devices with their start and end apart: 10, of which 8 were waited for; matrix products, arithmetic and copies ran while one was open for 16% of the time, Pallas kernels for 0%

commit v1 on v0

v1 whole, which is shorter than its diff:
```python
import functools
import jax
import jax.numpy as jnp
from jax import lax
from jax.experimental import pallas as pl
from jax.experimental.pallas import tpu as pltpu
from jax.sharding import PartitionSpec as P

MESH = pl.DeviceIdType.MESH
HBM = pl.BlockSpec(memory_space=pltpu.HBM)


def place():
    i = lax.axis_index("dp")
    j = lax.axis_index("tp")
    return i // 2, i % 2, j // 4, j % 4


def gather_kernel(x_ref, dy_ref, wg_ref, wu_ref, wd_ref, xg, dyg, wgf, wuf, wdf,
                  xv, dyv, wgv, wuv, wdv, lsem, osem, ssem, rsem):
    x, c, z, y = place()
    xp = (x + 1) % 4
    xm = (x + 3) % 4
    dev = {
        "xp": {"dp": 2 * xp + c}, "xm": {"dp": 2 * xm + c}, "pc": {"dp": 2 * x + 1 - c},
        "yp": {"tp": 4 * z + (y + 1) % 4}, "ym": {"tp": 4 * z + (y + 3) % 4},
        "zp": {"tp": 4 * ((z + 1) % 4) + y}, "zm": {"tp": 4 * ((z + 3) % 4) + y},
    }
    loads = [pltpu.make_async_copy(s, d, lsem.at[k]) for k, (s, d) in enumerate(
        ((x_ref, xv), (wg_ref, wgv), (wu_ref, wuv), (wd_ref, wdv), (dy_ref, dyv)))]
    for l in loads:
        l.start()
    barrier = pltpu.get_barrier_semaphore()
    for d in dev.values():
        pl.semaphore_signal(barrier, inc=1, device_id=d, device_id_type=MESH)
    pl.semaphore_wait(barrier, len(dev))

    sends = []
    count = [0]

    def send(src, dst, to):
        k = count[0]
        count[0] += 1
        r = pltpu.make_async_remote_copy(src_ref=src, dst_ref=dst, send_sem=ssem.at[k], recv_sem=rsem.at[k],
                                         device_id=dev[to], device_id_type=MESH)
        r.start()
        sends.append(r)
        return r

    def wblk(k, xx, cc, half=None):
        i = 2 * xx + cc
        if k < 2:
            r = (wgf, wuf)[k]
            if half is None:
                return r.at[pl.ds(pl.multiple_of(i * 512, 512), 512), :]
            return r.at[pl.ds(pl.multiple_of(i * 512 + half * 256, 256), 256), :]
        if half is None:
            return wdf.at[i]
        return wdf.at[i, pl.ds(half * 448, 448), :]

    gath = (xg, dyg)

    def rows(a, color, p, s, lo=0, n=32):
        zz, yy = (s, p) if color == 0 else (p, s)
        return gath[a].at[pl.ds(pl.multiple_of((zz * 4 + yy) * 64 + color * 32 + lo, 16), n), :]

    prim = ((y, z), (z, y))
    links = (("yp", "ym", "zp", "zm"), ("zp", "zm", "yp", "ym"))
    own = (xv, dyv)
    A = {}
    B = {}

    def start_own(a):
        for col in range(2):
            p, s = prim[col]
            pp, pm, sp, sm = links[col]
            src = own[a].at[pl.ds(col * 32, 32), :]
            dst = rows(a, col, p, s)
            A[a, col] = (send(src, dst, pp), send(src, dst, pm))
            B[a, col, 0] = (send(src, dst, sp), send(src, dst, sm))

    A2 = {}

    def step_a(a):
        for col in range(2):
            p, s = prim[col]
            pp, pm, sp, sm = links[col]
            fromm, fromp = A[a, col]
            fromm.wait_recv()
            q = (p + 3) % 4
            f1 = send(rows(a, col, q, s, 0, 16), rows(a, col, q, s, 0, 16), pp)
            B[a, col, -1] = (send(rows(a, col, q, s), rows(a, col, q, s), sp), send(rows(a, col, q, s), rows(a, col, q, s), sm))
            fromp.wait_recv()
            q = (p + 1) % 4
            f2 = send(rows(a, col, q, s, 16, 16), rows(a, col, q, s, 16, 16), pm)
            B[a, col, 1] = (send(rows(a, col, q, s), rows(a, col, q, s), sp), send(rows(a, col, q, s), rows(a, col, q, s), sm))
            A2[a, col] = (f1, f2)

    def step_a2(a):
        for col in range(2):
            p, s = prim[col]
            pp, pm, sp, sm = links[col]
            f1, f2 = A2[a, col]
            f1.wait_recv()
            f2.wait_recv()
            q = (p + 2) % 4
            B[a, col, 2] = (send(rows(a, col, q, s), rows(a, col, q, s), sp), send(rows(a, col, q, s), rows(a, col, q, s), sm))

    last = []

    def step_b(a, q):
        for col in range(2):
            p, s = prim[col]
            pp, pm, sp, sm = links[col]
            fromm, fromp = B[a, col, q]
            qq = (p + q + 4) % 4
            fromm.wait_recv()
            r = rows(a, col, qq, (s + 3) % 4, 0, 16)
            last.append(send(r, r, sp))
            fromp.wait_recv()
            r = rows(a, col, qq, (s + 1) % 4, 16, 16)
            last.append(send(r, r, sm))

    W = {}

    def start_w(k):
        src = (wgv, wuv, wdv)[k]
        dst = wblk(k, x, c)
        W[k] = (send(src, dst, "xp"), send(src, dst, "xm"))
        last.append(send(src, dst, "pc"))

    W2 = {}

    def step_w(k):
        fromm, fromp = W[k]
        fromm.wait_recv()
        r = wblk(k, xm, c, 0)
        f1 = send(r, r, "xp")
        r = wblk(k, xm, c)
        last.append(send(r, r, "pc"))
        fromp.wait_recv()
        r = wblk(k, xp, c, 1)
        f2 = send(r, r, "xm")
        r = wblk(k, xp, c)
        last.append(send(r, r, "pc"))
        W2[k] = (f1, f2)

    def step_w2(k):
        f1, f2 = W2[k]
        xo = (x + 2) % 4
        f1.wait_recv()
        r = wblk(k, xo, c, 0)
        last.append(send(r, r, "pc"))
        f2.wait_recv()
        r = wblk(k, xo, c, 1)
        last.append(send(r, r, "pc"))

    outs = []

    def put(src, dst):
        r = pltpu.make_async_copy(src, dst, osem.at[len(outs)])
        r.start()
        outs.append(r)

    loads[0].wait()
    start_own(0)
    for k in range(3):
        loads[1 + k].wait()
        start_w(k)
    loads[4].wait()
    j64 = pl.multiple_of((z * 4 + y) * 64, 64)
    put(xv, xg.at[pl.ds(j64, 64), :])
    put(dyv, dyg.at[pl.ds(j64, 64), :])
    for k in range(3):
        put((wgv, wuv, wdv)[k], wblk(k, x, c))

    step_a(0)
    start_own(1)
    step_a2(0)
    step_b(0, 0)
    step_a(1)
    step_w(0)
    step_b(0, -1)
    step_b(0, 1)
    step_a2(1)
    step_b(0, 2)
    step_w(1)
    step_b(1, 0)
    step_b(1, -1)
    step_w(2)
    step_w2(0)
    step_b(1, 1)
    step_w2(1)
    step_b(1, 2)
    step_w2(2)
    for r in last:
        r.wait_recv()
    for r in sends:
        r.wait_send()
    for r in outs:
        r.wait()


NSEND = 80 + 6 + 6 + 15


def gather(x, dy, wg, wu, wd):
    bf = jnp.bfloat16
    sd = jax.ShapeDtypeStruct
    return pl.pallas_call(
        gather_kernel,
        out_shape=(sd((1024, 4096), bf), sd((1024, 4096), bf), sd((4096, 896), bf), sd((4096, 896), bf), sd((8, 896, 512), bf)),
        in_specs=[HBM] * 5,
        out_specs=(HBM,) * 5,
        scratch_shapes=[
            pltpu.VMEM((64, 4096), bf), pltpu.VMEM((64, 4096), bf), pltpu.VMEM((512, 896), bf), pltpu.VMEM((512, 896), bf),
            pltpu.VMEM((896, 512), bf),
            pltpu.SemaphoreType.DMA((5,)), pltpu.SemaphoreType.DMA((5,)),
            pltpu.SemaphoreType.DMA((NSEND,)), pltpu.SemaphoreType.DMA((NSEND,)),
        ],
        compiler_params=pltpu.CompilerParams(collective_id=1, has_side_effects=True, vmem_limit_bytes=16 * 2**20),
        name="gather",
    )(x, dy, wg, wu, wd)


def solution(mesh):
    rows = P(("dp", "tp"), None)
    wsp = P("dp", "tp")
    dsp = P("tp", "dp")
    f32 = jnp.float32
    bf = jnp.bfloat16

    def local(x, w_gate, w_up, w_down, dy):
        xg, dyg, wg, wu, wd = gather(x, dy, w_gate, w_up, w_down)
        a = jnp.dot(xg, wg, preferred_element_type=f32)
        b = jnp.dot(xg, wu, preferred_element_type=f32)
        sig = jax.nn.sigmoid(a)
        sa = a * sig
        h = (sa * b).astype(bf)
        dyb = dyg.reshape(1024, 8, 512)
        g = lax.dot_general(dyb, wd, (((1, 2), (0, 2)), ((), ())), preferred_element_type=f32)
        da = (g * b * sig * (1.0 + a * (1.0 - sig))).astype(bf)
        db = (g * sa).astype(bf)
        yp = lax.dot_general(h, wd, (((1,), (1,)), ((), ())), preferred_element_type=f32).reshape(1024, 4096)
        yq = lax.psum_scatter(yp, "tp", scatter_dimension=0, tiled=True)
        dwd = lax.psum_scatter(lax.dot_general(h, dyg, (((0,), (0,)), ((), ())), preferred_element_type=f32), "dp", scatter_dimension=1, tiled=True)
        dxp = jnp.dot(da, wg.T, preferred_element_type=f32) + jnp.dot(db, wu.T, preferred_element_type=f32)
        dxq = lax.psum_scatter(dxp, "tp", scatter_dimension=0, tiled=True)
        dwg = lax.psum_scatter(lax.dot_general(xg, da, (((0,), (0,)), ((), ())), preferred_element_type=f32), "dp", scatter_dimension=0, tiled=True)
        dwu = lax.psum_scatter(lax.dot_general(xg, db, (((0,), (0,)), ((), ())), preferred_element_type=f32), "dp", scatter_dimension=0, tiled=True)
        y = (x.astype(f32) + yq).astype(bf)
        dx = (dy.astype(f32) + dxq).astype(bf)
        return y, dx, dwg, dwu, dwd

    return jax.shard_map(local, mesh=mesh, in_specs=(rows, wsp, wsp, dsp, rows), out_specs=(rows, rows, wsp, wsp, dsp), check_vma=False)
```

time: 1120 us -> 680 us (0.61)
  waiting for transfers between devices: 862 us -> 396 us
  Pallas kernels: 0 us -> 102 us
  local copies, waits for them, and re-layouts: 59.3 us -> 23.1 us
  blocking collectives: 28.3 us -> 0 us
  matrix products: 118 us -> 132 us
  starting transfers between devices: 12.2 us -> 0.21 us
  other arithmetic: 15.6 us -> 4.21 us
    all_gather x4 -> x0, waiting for transfers between devices: 291 us -> none  [the longest x1 116 us: local(): lax.all_gather(jnp.concatenate([da, db], axis=1), 'dp', axis=0, tiled=True)]
    unnamed x10 -> x5, waiting for transfers between devices: 162 us -> 0.08 us
    pallas_call x0 -> x1, Pallas kernels: none -> 102 us  [gather(): pl.pallas_call(gather_kernel, out_shape=(sd((1024, 4096), bf), sd((1024,...]
    all_to_all x2 -> x0, blocking collectives: 28.3 us -> none  [to_columns(): return lax.all_to_all(vr, 'dp', 0, 0, tiled=True)]
    transpose x4 -> x0, local copies, waits for them, and re-layouts: 15.9 us -> none  [the longest x2 15.6 us: all_tokens(): return vg.transpose(1, 0, 2, 3).reshape(nx * ny * tl, dl)]
    reshape x4 -> x1, local copies, waits for them, and re-layouts: 32.7 us -> 17.4 us  [local(): lax.dot_general(h, wd, (((1,), (1,)), ((), ())), preferred_element_type=f32)]
    dot_general x6 -> x9, matrix products: 118 us -> 132 us  [the longest x1 19.2 us: local(): jnp.dot(db, wu.T, preferred_element_type=f32)]
    reduce_scatter x2 -> x5, waiting for transfers between devices: 408 us -> 396 us  [the longest x1 111 us: local(): yq = lax.psum_scatter(yp, 'tp', scatter_dimension=0, tiled=True)]
  transfers between devices with their start and end apart: 10 -> 5, of which waited for: 8 -> 5; matrix products, arithmetic and copies ran while one was open for 16% -> 12% of each run, Pallas kernels for 0% -> 0%
where the time goes in v1:
time: 680 us; the launch traced here: 672 us
  waiting for transfers between devices  396 us (58%)
  matrix products  132 us (19%)
  Pallas kernels  102 us (15%)
  local copies, waits for them, and re-layouts  23.1 us (3%)
  between operations  14.3 us (2%)
    reduce_scatter x1, waiting for transfers between devices, local(): yq = lax.psum_scatter(yp, 'tp', scatter_dimension=0, tiled=True)  111 us
    pallas_call x1, Pallas kernels, gather(): pl.pallas_call(gather_kernel, out_shape=(sd((1024, 4096), bf), sd((1024,...  102 us
    reduce_scatter x1, waiting for transfers between devices, local(): lax.psum_scatter(lax.dot_general(h, dyg, (((0,), (0,)), ((), ())), prefer...  85 us
    reduce_scatter x1, waiting for transfers between devices, local(): lax.psum_scatter(lax.dot_general(xg, db, (((0,), (0,)), ((), ())), prefer...  84.9 us
    reduce_scatter x1, waiting for transfers between devices, local(): lax.psum_scatter(lax.dot_general(xg, da, (((0,), (0,)), ((), ())), prefer...  83 us
    reduce_scatter x1, waiting for transfers between devices, local(): dxq = lax.psum_scatter(dxp, 'tp', scatter_dimension=0, tiled=True)  31.7 us
    dot_general x1, matrix products, local(): jnp.dot(db, wu.T, preferred_element_type=f32)  19.2 us
    reshape x1, local copies, waits for them, and re-layouts, local(): lax.dot_general(h, wd, (((1,), (1,)), ((), ())), preferred_element_type=f32)  17.4 us
  transfers between devices with their start and end apart: 5, of which 5 were waited for; matrix products, arithmetic and copies ran while one was open for 12% of the time, Pallas kernels for 0%

profile of v1, /device:TPU:1, one launch (start us, length us, event | category | flops | bytes accessed | tf_op | source)
XLA Modules:
  0.0 671.7 jit_solution(956392102559819598)
XLA Ops:
  7.2 0.0 reduce-scatter.8.cloned.1.call-start
  7.2 0.0 copy-start
  7.2 1.0 copy-done
  8.3 0.0 copy-start.2
  8.3 1.0 copy-done.2
  9.3 0.0 copy-start.4
  9.3 1.2 copy-done.4
  10.5 0.0 copy-start.5
  10.5 1.2 copy-done.5
  11.7 0.0 copy-start.6
  11.7 1.2 copy-done.6
  12.8 102.1 %gather.1 = (bf16[1024,4096]{1,0:T(8,128)(2,1)S(1)}, bf16[1024,4096]{1,0:T(8,128)(2,1)}, bf16[4096,896]{1,0:T(8,128)(2,1)S(1)}, bf16[4096,896]{1,0:T(8,128)(2,1)S(1)}, bf16[8,896,512]{2,1,0:T(8,128)(2,1)S(1)}) custom-call(bf16[64,4096]{1,0:T(8,128)(2,1)S(1)} %copy-done.2, bf16[64,4096]{1,0:T(8,128)(2,1)S(1)} %copy-done, bf16[512,896]{1,0:T(8,128)(2,1)S(1)} %copy-done.4, ...), custom_call_target="tpu_custom_call" | custom-call | tf_op jit(solution)/shard_map/gather/pallas_call | solution.py:210
  114.9 0.0 copy-start.8
  114.9 0.0 copy-start.9
  115.0 0.0 copy-start.7
  115.0 0.0 copy-start.10
  115.0 11.0 %fusion.11 = f32[1024,896]{1,0:T(8,128)} fusion(bf16[1024,4096]{1,0:T(8,128)(2,1)S(1)} %get-tuple-element.10, bf16[4096,896]{1,0:T(8,128)(2,1)S(1)} %get-tuple-element.12), kind=kOutput, calls=%fused_computation.18 | convolution fusion | flops 7516192768 | bytes 19398656 | tf_op jit(solution)/shard_map/dot_general | solution.py:236
  126.0 0.0 copy-done.8
  126.0 0.0 copy-done.9
  126.0 0.0 copy-done.7
  126.0 0.0 copy-done.10
  126.0 10.6 %fusion.10 = f32[1024,896]{1,0:T(8,128)} fusion(bf16[1024,4096]{1,0:T(8,128)(2,1)S(1)} %get-tuple-element.10, bf16[4096,896]{1,0:T(8,128)(2,1)S(1)} %get-tuple-element.11), kind=kOutput, calls=%fused_computation.17 | convolution fusion | flops 7516192768 | bytes 19398656 | tf_op jit(solution)/shard_map/dot_general | solution.py:235
  136.6 17.1 %fusion.6 = (bf16[1024,896]{1,0:T(8,128)(2,1)S(1)}, bf16[1024,896]{1,0:T(8,128)(2,1)}, bf16[1024,896]{1,0:T(8,128)(2,1)S(1)}) fusion(f32[1024,896]{1,0:T(8,128)} %fusion.10, f32[1024,896]{1,0:T(8,128)} %fusion.11, bf16[8,896,512]{2,1,0:T(8,128)(2,1)} %copy-done.8, bf16[128,8,8,512]{3,2,1,0:T(8,128)(2,1)} %bitcast.38), kind=kOutput, calls=%fused_computation.9 | convolution fusion | flops 7529955328 | bytes 28573696 | tf_op jit(solution)/shard_map/dot_general | solution.py:241
  153.8 0.0 copy-start.11
  153.8 15.6 %fusion.12 = f32[1024,4096]{1,0:T(8,128)} fusion(bf16[1024,896]{1,0:T(8,128)(2,1)} %get-tuple-element.16, bf16[4096,896]{1,0:T(8,128)(2,1)} %copy-done.10), kind=kOutput, calls=%fused_computation.19 | convolution fusion | flops 7516192768 | bytes 25952256 | tf_op jit(solution)/shard_map/dot_general | solution.py:247
  169.4 0.0 copy-done.11
  169.4 19.2 %convolution_add_fusion = f32[1024,4096]{1,0:T(8,128)} fusion(f32[1024,4096]{1,0:T(8,128)} %fusion.12, bf16[1024,896]{1,0:T(8,128)(2,1)S(1)} %get-tuple-element.15, bf16[4096,896]{1,0:T(8,128)(2,1)} %copy-done.9), kind=kOutput, calls=%fused_computation.3 | convolution fusion | flops 7520387072 | bytes 42729472 | tf_op jit(solution)/shard_map/dot_general | solution.py:247
  188.6 0.0 reduce-scatter.8.cloned.1.call-update
  188.7 0.0 reduce-scatter.6.cloned.1.call-start
  188.7 14.6 %fusion.8 = f32[1024,8,512]{0,2,1:T(8,128)} fusion(bf16[8,896,512]{2,1,0:T(8,128)(2,1)} %copy-done.8, bf16[1024,896]{1,0:T(8,128)(2,1)S(1)} %get-tuple-element.17), kind=kOutput, calls=%fused_computation.13 | convolution fusion | flops 7516192768 | bytes 25952256 | tf_op jit(solution)/shard_map/dot_general | solution.py:244
  203.3 17.4 %copy.11 = f32[1024,4096]{1,0:T(8,128)} copy(f32[1024,4096]{0,1:T(8,128)} %bitcast.37) | data formatting | bytes 33554432 | tf_op jit(solution)/shard_map/reshape | solution.py:244
  220.8 0.0 reduce-scatter.6.cloned.1.call-update
  220.8 0.0 reduce-scatter.10.cloned.1.call-start
  220.9 15.0 %fusion.13 = f32[4096,896]{1,0:T(8,128)} fusion(bf16[1024,4096]{1,0:T(8,128)(2,1)} %copy-done.7, bf16[1024,896]{1,0:T(8,128)(2,1)} %get-tuple-element.16), kind=kOutput, calls=%fused_computation.20 | convolution fusion | flops 7516192768 | bytes 24903680 | tf_op jit(solution)/shard_map/dot_general | solution.py:249
  235.8 0.0 reduce-scatter.10.cloned.1.call-update
  235.9 0.0 reduce-scatter.12.cloned.1.call-start
  235.9 15.3 %fusion.14 = f32[4096,896]{1,0:T(8,128)} fusion(bf16[1024,4096]{1,0:T(8,128)(2,1)} %copy-done.7, bf16[1024,896]{1,0:T(8,128)(2,1)} %copy-done.11), kind=kOutput, calls=%fused_computation.21 | convolution fusion | flops 7516192768 | bytes 24903680 | tf_op jit(solution)/shard_map/dot_general | solution.py:250
  251.2 0.0 reduce-scatter.12.cloned.1.call-update
  251.2 0.0 reduce-scatter.14.cloned.1.call-start
  251.2 13.3 %fusion.15 = f32[896,4096]{1,0:T(8,128)} fusion(bf16[1024,896]{1,0:T(8,128)(2,1)S(1)} %get-tuple-element.17, bf16[1024,4096]{1,0:T(8,128)(2,1)} %get-tuple-element.14), kind=kOutput, calls=%fused_computation.22 | convolution fusion | flops 7516192768 | bytes 24903680 | tf_op jit(solution)/shard_map/dot_general | solution.py:246
  264.5 0.0 copy-start.1
  264.5 0.0 copy-start.3
  264.5 0.0 reduce-scatter.14.cloned.1.call-update
  264.5 31.7 %reduce-scatter.8.cloned.1.call-done = f32[64,4096]{1,0:T(8,128)} async-done(((f32[1024,4096]{1,0:T(8,128)}), f32[64,4096]{1,0:T(8,128)}) %reduce-scatter.8.cloned.1.call-update) | async-done | bytes 1048592 | tf_op jit(solution)/shard_map/reduce_scatter | solution.py:248
  296.2 0.0 copy-done.1
  296.2 2.1 add_convert_fusion
  298.3 111.4 %reduce-scatter.6.cloned.1.call-done = f32[64,4096]{1,0:T(8,128)} async-done(((f32[1024,4096]{1,0:T(8,128)}), f32[64,4096]{1,0:T(8,128)}) %reduce-scatter.6.cloned.1.call-update) | async-done | bytes 1048592 | tf_op jit(solution)/shard_map/reduce_scatter | solution.py:245
  409.7 0.0 copy-done.3
  409.7 2.1 add_convert_fusion.1
  411.8 83.0 %reduce-scatter.10.cloned.1.call-done = f32[512,896]{1,0:T(8,128)} async-done(((f32[4096,896]{1,0:T(8,128)}), f32[512,896]{1,0:T(8,128)}) %reduce-scatter.10.cloned.1.call-update) | async-done | bytes 1835024 | tf_op jit(solution)/shard_map/reduce_scatter | solution.py:249
  494.8 84.9 %reduce-scatter.12.cloned.1.call-done = f32[512,896]{1,0:T(8,128)} async-done(((f32[4096,896]{1,0:T(8,128)}), f32[512,896]{1,0:T(8,128)}) %reduce-scatter.12.cloned.1.call-update) | async-done | bytes 1835024 | tf_op jit(solution)/shard_map/reduce_scatter | solution.py:250
  579.7 85.0 %reduce-scatter.14.cloned.1.call-done = f32[896,512]{1,0:T(8,128)} async-done(((f32[896,4096]{1,0:T(8,128)}), f32[896,512]{1,0:T(8,128)}) %reduce-scatter.14.cloned.1.call-update) | async-done | bytes 1835024 | tf_op jit(solution)/shard_map/reduce_scatter | solution.py:246
Async XLA Ops:
  7.2 289.0 %reduce-scatter.8.cloned.1.call-start = ((), (), s32[]{:S(2)}) async-start(), calls=%async_computation.6 | async-start | bytes 17825792 | tf_op jit(solution)/shard_map/reduce_scatter | solution.py:248
  7.2 1.0 copy-start
  8.3 1.0 copy-start.2
  9.3 1.2 copy-start.4
  10.5 1.2 copy-start.5
  11.7 1.2 copy-start.6
  114.9 11.1 %copy-start.8 = (bf16[8,896,512]{2,1,0:T(8,128)(2,1)}, bf16[8,896,512]{2,1,0:T(8,128)(2,1)S(1)}, u32[]{:S(2)}) copy-start(bf16[8,896,512]{2,1,0:T(8,128)(2,1)S(1)} %get-tuple-element.13) | copy-start | bytes 22020100
  114.9 11.0 %copy-start.9 = (bf16[4096,896]{1,0:T(8,128)(2,1)}, bf16[4096,896]{1,0:T(8,128)(2,1)S(1)}, u32[]{:S(2)}) copy-start(bf16[4096,896]{1,0:T(8,128)(2,1)S(1)} %get-tuple-element.12) | copy-start | bytes 22020100
  115.0 11.0 %copy-start.7 = (bf16[1024,4096]{1,0:T(8,128)(2,1)}, bf16[1024,4096]{1,0:T(8,128)(2,1)S(1)}, u32[]{:S(2)}) copy-start(bf16[1024,4096]{1,0:T(8,128)(2,1)S(1)} %get-tuple-element.10) | copy-start | bytes 25165828
  115.0 11.0 %copy-start.10 = (bf16[4096,896]{1,0:T(8,128)(2,1)}, bf16[4096,896]{1,0:T(8,128)(2,1)S(1)}, u32[]{:S(2)}) copy-start(bf16[4096,896]{1,0:T(8,128)(2,1)S(1)} %get-tuple-element.11) | copy-start | bytes 22020100
  153.8 15.6 %copy-start.11 = (bf16[1024,896]{1,0:T(8,128)(2,1)}, bf16[1024,896]{1,0:T(8,128)(2,1)S(1)}, u32[]{:S(2)}) copy-start(bf16[1024,896]{1,0:T(8,128)(2,1)S(1)} %get-tuple-element.15) | copy-start | bytes 5505028
  188.7 221.1 %reduce-scatter.6.cloned.1.call-start = ((), (), s32[]{:S(2)}) async-start(), calls=%async_computation.5 | async-start | bytes 17825792 | tf_op jit(solution)/shard_map/reduce_scatter | solution.py:245
  220.8 274.0 %reduce-scatter.10.cloned.1.call-start = ((), (), s32[]{:S(2)}) async-start(), calls=%async_computation.7 | async-start | bytes 16515072 | tf_op jit(solution)/shard_map/reduce_scatter | solution.py:249
  235.9 343.9 %reduce-scatter.12.cloned.1.call-start = ((), (), s32[]{:S(2)}) async-start(), calls=%async_computation.8 | async-start | bytes 16515072 | tf_op jit(solution)/shard_map/reduce_scatter | solution.py:250
  251.2 413.5 %reduce-scatter.14.cloned.1.call-start = ((), (), s32[]{:S(2)}) async-start(), calls=%async_computation.9 | async-start | bytes 16515072 | tf_op jit(solution)/shard_map/reduce_scatter | solution.py:246
  264.5 31.7 %copy-start.1 = (bf16[64,4096]{1,0:T(8,128)(2,1)S(1)}, bf16[64,4096]{1,0:T(8,128)(2,1)}, u32[]{:S(2)}) copy-start(bf16[64,4096]{1,0:T(8,128)(2,1)} %dy_ref.1) | copy-start | bytes 1572868
  264.5 145.2 %copy-start.3 = (bf16[64,4096]{1,0:T(8,128)(2,1)S(1)}, bf16[64,4096]{1,0:T(8,128)(2,1)}, u32[]{:S(2)}) copy-start(bf16[64,4096]{1,0:T(8,128)(2,1)} %x_ref.1) | copy-start | bytes 1572868
Sparse Core Ops, SparseCore 0:
  188.8 107.3 reduce-scatter.7
  299.6 110.0 reduce-scatter.5
  412.7 82.0 reduce-scatter.9
  497.6 82.0 reduce-scatter.11
  582.6 82.0 reduce-scatter.13

commit v2 on v1

--- a/solution.py
+++ b/solution.py
@@ -1,4 +1,3 @@
-import functools
 import jax
 import jax.numpy as jnp
 from jax import lax
@@ -16,7 +15,7 @@
     return i // 2, i % 2, j // 4, j % 4
 
 
-def gather_kernel(x_ref, dy_ref, wg_ref, wu_ref, wd_ref, xg, dyg, wgf, wuf, wdf,
+def gather_kernel(x_ref, dy_ref, wg_ref, wu_ref, wd_ref, xd, wgf, wuf, wdf,
                   xv, dyv, wgv, wuv, wdv, lsem, osem, ssem, rsem):
     x, c, z, y = place()
     xp = (x + 1) % 4
@@ -58,11 +57,9 @@
             return wdf.at[i]
         return wdf.at[i, pl.ds(half * 448, 448), :]
 
-    gath = (xg, dyg)
-
     def rows(a, color, p, s, lo=0, n=32):
         zz, yy = (s, p) if color == 0 else (p, s)
-        return gath[a].at[pl.ds(pl.multiple_of((zz * 4 + yy) * 64 + color * 32 + lo, 16), n), :]
+        return xd.at[a, pl.ds(pl.multiple_of((zz * 4 + yy) * 64 + color * 32 + lo, 16), n), :]
 
     prim = ((y, z), (z, y))
     links = (("yp", "ym", "zp", "zm"), ("zp", "zm", "yp", "ym"))
@@ -169,8 +166,8 @@
         start_w(k)
     loads[4].wait()
     j64 = pl.multiple_of((z * 4 + y) * 64, 64)
-    put(xv, xg.at[pl.ds(j64, 64), :])
-    put(dyv, dyg.at[pl.ds(j64, 64), :])
+    put(xv, xd.at[0, pl.ds(j64, 64), :])
+    put(dyv, xd.at[1, pl.ds(j64, 64), :])
     for k in range(3):
         put((wgv, wuv, wdv)[k], wblk(k, x, c))
 
@@ -209,47 +206,406 @@
     sd = jax.ShapeDtypeStruct
     return pl.pallas_call(
         gather_kernel,
-        out_shape=(sd((1024, 4096), bf), sd((1024, 4096), bf), sd((4096, 896), bf), sd((4096, 896), bf), sd((8, 896, 512), bf)),
+        out_shape=(sd((2, 1024, 4096), bf), sd((4096, 896), bf), sd((4096, 896), bf), sd((8, 896, 512), bf)),
         in_specs=[HBM] * 5,
-        out_specs=(HBM,) * 5,
+        out_specs=(HBM,) * 4,
         scratch_shapes=[
             pltpu.VMEM((64, 4096), bf), pltpu.VMEM((64, 4096), bf), pltpu.VMEM((512, 896), bf), pltpu.VMEM((512, 896), bf),
             pltpu.VMEM((896, 512), bf),
             pltpu.SemaphoreType.DMA((5,)), pltpu.SemaphoreType.DMA((5,)),
             pltpu.SemaphoreType.DMA((NSEND,)), pltpu.SemaphoreType.DMA((NSEND,)),
         ],
-        compiler_params=pltpu.CompilerParams(collective_id=1, has_side_effects=True, vmem_limit_bytes=16 * 2**20),
+        compiler_params=pltpu.CompilerParams(collective_id=1, has_side_effects=True, vmem_limit_bytes=60 * 2**20),
         name="gather",
     )(x, dy, wg, wu, wd)
+
+
+NT = (((1,), (1,)), ((), ()))
+TN = (((0,), (0,)), ((), ()))
+F32 = jnp.float32
+BF = jnp.bfloat16
+
+
+def reduce_kernel(hh, da, db, xd, wg, wu, wd, xo, dyo, dw, yo,
+                  XR, ZR, AP, B, A, XB, XS, WD, WX, ZB, ZS, Z2, res, ov,
+                  s_ld, s_a, s_ap, r_ap, s_b, r_b, s_xs, r_xs, s_zs, r_zs, s_2, r_2, s_w, s_xst, s_zst, s_xo, s_yo):
+    x, c, z, y = place()
+    dev = {
+        "xp": {"dp": 2 * ((x + 1) % 4) + c}, "xm": {"dp": 2 * ((x + 3) % 4) + c}, "pc": {"dp": 2 * x + 1 - c},
+        "yp": {"tp": 4 * z + (y + 1) % 4}, "ym": {"tp": 4 * z + (y + 3) % 4},
+        "zp": {"tp": 4 * ((z + 1) % 4) + y}, "zm": {"tp": 4 * ((z + 3) % 4) + y},
+    }
+    hbm_b = (hh, da, db)
+
+    def remote(src, dst, ss, rs, to):
+        return pltpu.make_async_remote_copy(src_ref=src, dst_ref=dst, send_sem=ss, recv_sem=rs, device_id=dev[to], device_id_type=MESH)
+
+    def add(dst, src, n):
+        def body(r, _):
+            s = pl.ds(pl.multiple_of(r * 32, 32), 32)
+            dst[s, :] = dst[s, :] + src[s, :]
+            return 0
+        lax.fori_loop(0, n // 32, body, 0)
+
+    ld_b = [pltpu.make_async_copy(hbm_b[k], B.at[k, 0], s_ld.at[k]) for k in range(3)]
+    ld_r = [pltpu.make_async_copy(xo, res.at[0], s_ld.at[3]), pltpu.make_async_copy(dyo, res.at[1], s_ld.at[4])]
+
+    def load_w(n):
+        out = []
+        for col in range(2):
+            q = 2 * col + n % 2
+            if n < 2:
+                out.append(pltpu.make_async_copy(wd.at[pl.ds(2 * q, 2)], WD.at[col], s_w.at[col, 0]))
+            else:
+                out.append(pltpu.make_async_copy(wg.at[pl.ds(1024 * q, 1024), :], WX.at[col, 0], s_w.at[col, 1]))
+                out.append(pltpu.make_async_copy(wu.at[pl.ds(1024 * q, 1024), :], WX.at[col, 1], s_w.at[col, 2]))
+        for o in out:
+            o.start()
+        return out
+
+    ld_b[0].start()
+    wl = {0: load_w(0)}
+    for l in ld_b[1:] + ld_r:
+        l.start()
+    wl[2] = load_w(2)
+
+    barrier = pltpu.get_barrier_semaphore()
+    for d in dev.values():
+        pl.semaphore_signal(barrier, inc=1, device_id=d, device_id_type=MESH)
+    pl.semaphore_wait(barrier, len(dev))
+
+    def chunk(idx):
+        return (x + 6 - idx) % 4
+
+    bp = [remote(hbm_b[k], B.at[k, 1], s_b.at[k], r_b.at[k], "pc") for k in range(3)]
+
+    def ap(arr, idx):
+        ch = chunk(idx)
+        return remote(xd.at[arr, :, pl.ds(pl.multiple_of(1024 * ch + 512 * (1 - c), 512), 512)], AP.at[arr, idx], s_ap.at[arr, idx], r_ap.at[arr, idx], "pc")
+
+    bp[0].start()
+    for idx in range(4):
+        ap(1, idx).start()
+    bp[1].start()
+    for idx in range(4):
+        ap(0, idx).start()
+    bp[2].start()
+
+    def load_a(arr, idx):
+        slot = idx % 2
+        ch = chunk(idx)
+        return (pltpu.make_async_copy(xd.at[arr, :, pl.ds(pl.multiple_of(1024 * ch + 512 * c, 512), 512)], A.at[slot, 0], s_a.at[slot, 0]),
+                pltpu.make_async_copy(AP.at[arr, idx], A.at[slot, 1], s_a.at[slot, 1]))
+
+    def start_a(arr, idx):
+        for l in load_a(arr, idx):
+            l.start()
+
+    def wait_ap(arr, idx):
+        ap(arr, idx).wait_recv()
+
+    def dot_x(k, idx):
+        slot = idx % 2
+        for l in load_a(0, idx):
+            l.wait()
+
+        def body(m, _):
+            cols = pl.ds(pl.multiple_of(m * 256, 256), 256)
+            XB[idx, m] = (lax.dot_general(A[slot, 0, :, cols], B[k, 0], TN, preferred_element_type=F32)
+                          + lax.dot_general(A[slot, 1, :, cols], B[k, 1], TN, preferred_element_type=F32))
+            return 0
+        lax.fori_loop(0, 2, body, 0)
+
+    def xmsg(k, t):
+        src = (XB.at[0, 0], XB.at[0, 1], XB.at[1, 1], XB.at[3, 0], XB.at[1, 0], XB.at[3, 1])[t]
+        return remote(src, XR.at[k, t], s_xs.at[t], r_xs.at[k, t], ("xp", "xm")[t % 2])
+
+    def x1(k):
+        if k == 0:
+            bp[0].wait_recv()
+            for idx in range(2):
+                wait_ap(1, idx)
+                start_a(1, idx)
+        else:
+            bp[k].wait_recv()
+            xmsg(k - 1, 0).wait_send()
+            xmsg(k - 1, 1).wait_send()
+        dot_x(k, 0)
+        xmsg(k, 0).start()
+        xmsg(k, 1).start()
+        if k < 2:
+            wait_ap(1 - min(k, 1), 2)
+        start_a(1 - min(k, 1), 2)
+
+    def x2(k):
+        if k > 0:
+            for t in range(2, 6):
+                xmsg(k - 1, t).wait_send()
+            xout(k - 1).wait()
+
+        def body(idx, _):
+            dot_x(k, idx)
+            nxt = (idx + 2) % 4
+            carry = (idx + 2) // 4
+            if k == 0:
+                wait_ap(1 - carry, nxt)
+                start_a(1 - carry, nxt)
+            elif k == 1:
+                @pl.when(idx == 1)
+                def _():
+                    wait_ap(0, nxt)
+                start_a(0, nxt)
+            else:
+                @pl.when(idx == 1)
+                def _():
+                    start_a(0, nxt)
+            return 0
+        lax.fori_loop(1, 4, body, 0)
+        xmsg(k, 2).start()
+        xmsg(k, 3).start()
+
+    def xstage(k, t, slot):
+        return pltpu.make_async_copy(XR.at[k, t], XS.at[slot], s_xst.at[slot])
+
+    def x3(k):
+        for t in range(2):
+            xmsg(k, t).wait_recv()
+            xstage(k, t, t).start()
+        for t in range(2):
+            xstage(k, t, t).wait()
+            add(XB.at[(1, 3)[t], t], XS.at[t], 256)
+            xmsg(k, 4 + t).start()
+
+    def xout(k):
+        return pltpu.make_async_copy(XB.at[2], dw.at[k], s_xo)
+
+    def xf(k):
+        for pair in ((3, 2), (4, 5)):
+            for h, t in enumerate(pair):
+                xmsg(k, t).wait_recv()
+                xstage(k, t, h).start()
+            for h, t in enumerate(pair):
+                xstage(k, t, h).wait()
+                add(XB.at[2, h], XS.at[h], 256)
+        xout(k).start()
+
+    pos = ((z, y), (y, z))
+    link = (("zp", "zm", "yp", "ym"), ("yp", "ym", "zp", "zm"))
+
+    def dots_z(n, lo, hi):
+        m = hi - lo
+
+        def body(i, _):
+            col = i // m
+            idx = lo + i % m
+            p = z + col * (y - z)
+            ch = (p + 6 - idx) % 4
+            s1 = 256 - 192 * col
+            s2 = 64 + 192 * col
+            own = (idx // 2) * (1 - idx // 3)
+            slot = idx + own * 2 * (n % 2)
+
+            def lhs(k):
+                return jnp.concatenate([B[k, 0, pl.ds(pl.multiple_of(ch * s1 + g * s2, 64), 64), :] for g in range(4)], axis=0)
+
+            if n < 2:
+                l = lhs(0)
+                for h in range(2):
+                    ZB[col, slot, h] = jnp.dot(l, WD[col, h], preferred_element_type=F32)
+            else:
+                l = lhs(1)
+                u = lhs(2)
+                for h in range(2):
+                    r = pl.ds(512 * h, 512)
+                    ZB[col, slot, h] = (lax.dot_general(l, WX[col, 0, r, :], NT, preferred_element_type=F32)
+                                        + lax.dot_general(u, WX[col, 1, r, :], NT, preferred_element_type=F32))
+            return 0
+        lax.fori_loop(0, 2 * m, body, 0)
+
+    def zmsg(n, col, t):
+        src = ((0, 0), (0, 1), (1, 1), (3, 0), (1, 0), (3, 1))[t]
+        return remote(ZB.at[col, src[0], src[1]], ZR.at[col, n, t], s_zs.at[col, t], r_zs.at[col, n, t], link[col][t % 2])
+
+    def own(n, col, h):
+        return ZB.at[col, 2 + 2 * (n % 2), h]
+
+    def sub(n, col, h, d):
+        s = (pos[col][1] + d) % 4
+        return ZB.at[col, 2 + 2 * (n % 2), h, pl.ds(pl.multiple_of(s * 64, 64), 64), :]
+
+    def msg2(n, col, t):
+        h, d = ((0, 2), (1, 2), (1, 1), (0, 3), (0, 1), (1, 3))[t]
+        return remote(sub(n, col, h, d), Z2.at[col, n, t], s_2.at[col, n % 2, t], r_2.at[col, n, t], link[col][2 + t % 2])
+
+    def p1(n):
+        if n == 0:
+            ld_b[0].wait()
+        for l in wl[n]:
+            l.wait()
+        if n > 0:
+            for col in range(2):
+                for t in range(2):
+                    zmsg(n - 1, col, t).wait_send()
+        dots_z(n, 0, 1)
+        for t in range(2):
+            for col in range(2):
+                zmsg(n, col, t).start()
+
+    def p2(n):
+        if n > 0:
+            for col in range(2):
+                for t in range(2, 6):
+                    zmsg(n - 1, col, t).wait_send()
+        if n > 1:
+            for col in range(2):
+                for t in range(6):
+                    msg2(n - 2, col, t).wait_send()
+        dots_z(n, 1, 4)
+        for t in range(2, 4):
+            for col in range(2):
+                zmsg(n, col, t).start()
+        if n % 2 == 0:
+            wl[n + 1] = load_w(n + 1)
+
+    def zstage(n, col, t, slot):
+        return pltpu.make_async_copy(ZR.at[col, n, t], ZS.at[col, slot], s_zst.at[col, slot])
+
+    def p4(n):
+        for t in range(2):
+            for col in range(2):
+                zmsg(n, col, t).wait_recv()
+                zstage(n, col, t, t).start()
+        for t in range(2):
+            for col in range(2):
+                zstage(n, col, t, t).wait()
+                add(ZB.at[col, (1, 3)[t], t], ZS.at[col, t], 256)
+                zmsg(n, col, 4 + t).start()
+
+    def f(n):
+        order = ((3, 0), (2, 1), (4, 0), (5, 1))
+        for i, (t, h) in enumerate(order):
+            for col in range(2):
+                zmsg(n, col, t).wait_recv()
+                zstage(n, col, t, i).start()
+        for i, (t, h) in enumerate(order):
+            for col in range(2):
+                zstage(n, col, t, i).wait()
+                add(own(n, col, h), ZS.at[col, i], 256)
+        for t in range(4):
+            for col in range(2):
+                msg2(n, col, t).start()
+
+    def hh2(n):
+        for t in range(2):
+            for col in range(2):
+                msg2(n, col, t).wait_recv()
+                add(sub(n, col, t, (1, 3)[t]), Z2.at[col, n, t], 64)
+                msg2(n, col, 4 + t).start()
+
+    def zf(n):
+        a = n // 2
+        for col in range(2):
+            for h, ts in ((0, (3, 4)), (1, (2, 5))):
+                for t in ts:
+                    msg2(n, col, t).wait_recv()
+                cs = pl.ds(2048 * col + 1024 * (n % 2) + 512 * h, 512)
+                v = sub(n, col, h, 0)[...] + Z2[col, n, ts[0]] + Z2[col, n, ts[1]]
+                ov[a, :, cs] = (res[a, :, cs].astype(F32) + v).astype(BF)
+
+    p1(0)
+    x1(0)
+    p2(0)
+    x2(0)
+    p4(0)
+    x3(0)
+    for l in ld_b[1:] + ld_r:
+        l.wait()
+    p1(1)
+    x1(1)
+    f(0)
+    p2(1)
+    hh2(0)
+    zf(0)
+    p4(1)
+    xf(0)
+    x2(1)
+    p1(2)
+    f(1)
+    p2(2)
+    x3(1)
+    hh2(1)
+    zf(1)
+    p4(2)
+    x1(2)
+    p1(3)
+    f(2)
+    xf(1)
+    x2(2)
+    p2(3)
+    hh2(2)
+    zf(2)
+    p4(3)
+    x3(2)
+    f(3)
+    hh2(3)
+    zf(3)
+    xf(2)
+    out = [pltpu.make_async_copy(ov, yo, s_yo)]
+    out[0].start()
+    for t in range(6):
+        xmsg(2, t).wait_send()
+        for col in range(2):
+            zmsg(3, col, t).wait_send()
+            msg2(2, col, t).wait_send()
+            msg2(3, col, t).wait_send()
+    for k in range(3):
+        bp[k].wait_send()
+    for arr in range(2):
+        for idx in range(4):
+            ap(arr, idx).wait_send()
+    xout(2).wait()
+    out[0].wait()
+
+
+def reduce(h, da, db, xd, wg, wu, wd, xo, dyo):
+    sd = jax.ShapeDtypeStruct
+    dma = pltpu.SemaphoreType.DMA
+    V = pltpu.VMEM
+    return pl.pallas_call(
+        reduce_kernel,
+        out_shape=(sd((3, 2, 256, 896), F32), sd((2, 64, 4096), BF),
+                   sd((3, 6, 256, 896), F32), sd((2, 4, 6, 256, 512), F32), sd((2, 4, 1024, 512), BF)),
+        in_specs=[HBM] * 9,
+        out_specs=(HBM,) * 5,
+        scratch_shapes=[
+            V((3, 2, 1024, 896), BF), V((2, 2, 1024, 512), BF), V((4, 2, 256, 896), F32), V((2, 256, 896), F32),
+            V((2, 2, 896, 512), BF), V((2, 2, 1024, 896), BF), V((2, 5, 2, 256, 512), F32), V((2, 4, 256, 512), F32),
+            V((2, 4, 6, 64, 512), F32), V((2, 64, 4096), BF), V((2, 64, 4096), BF),
+            dma((5,)), dma((2, 2)), dma((2, 4)), dma((2, 4)), dma((3,)), dma((3,)), dma((6,)), dma((3, 6)),
+            dma((2, 6)), dma((2, 4, 6)), dma((2, 2, 6)), dma((2, 4, 6)), dma((2, 3)), dma((2,)), dma((2, 4)), dma, dma,
+        ],
+        compiler_params=pltpu.CompilerParams(collective_id=2, has_side_effects=True, vmem_limit_bytes=67043328),
+        name="reduce",
+    )(h, da, db, xd, wg, wu, wd, xo, dyo)[:2]
 
 
 def solution(mesh):
     rows = P(("dp", "tp"), None)
     wsp = P("dp", "tp")
     dsp = P("tp", "dp")
-    f32 = jnp.float32
-    bf = jnp.bfloat16
 
     def local(x, w_gate, w_up, w_down, dy):
-        xg, dyg, wg, wu, wd = gather(x, dy, w_gate, w_up, w_down)
-        a = jnp.dot(xg, wg, preferred_element_type=f32)
-        b = jnp.dot(xg, wu, preferred_element_type=f32)
+        xd, wg, wu, wd = gather(x, dy, w_gate, w_up, w_down)
+        a = jnp.dot(xd[0], wg, preferred_element_type=F32)
+        b = jnp.dot(xd[0], wu, preferred_element_type=F32)
         sig = jax.nn.sigmoid(a)
         sa = a * sig
-        h = (sa * b).astype(bf)
-        dyb = dyg.reshape(1024, 8, 512)
-        g = lax.dot_general(dyb, wd, (((1, 2), (0, 2)), ((), ())), preferred_element_type=f32)
-        da = (g * b * sig * (1.0 + a * (1.0 - sig))).astype(bf)
-        db = (g * sa).astype(bf)
-        yp = lax.dot_general(h, wd, (((1,), (1,)), ((), ())), preferred_element_type=f32).reshape(1024, 4096)
-        yq = lax.psum_scatter(yp, "tp", scatter_dimension=0, tiled=True)
-        dwd = lax.psum_scatter(lax.dot_general(h, dyg, (((0,), (0,)), ((), ())), preferred_element_type=f32), "dp", scatter_dimension=1, tiled=True)
-        dxp = jnp.dot(da, wg.T, preferred_element_type=f32) + jnp.dot(db, wu.T, preferred_element_type=f32)
-        dxq = lax.psum_scatter(dxp, "tp", scatter_dimension=0, tiled=True)
-        dwg = lax.psum_scatter(lax.dot_general(xg, da, (((0,), (0,)), ((), ())), preferred_element_type=f32), "dp", scatter_dimension=0, tiled=True)
-        dwu = lax.psum_scatter(lax.dot_general(xg, db, (((0,), (0,)), ((), ())), preferred_element_type=f32), "dp", scatter_dimension=0, tiled=True)
-        y = (x.astype(f32) + yq).astype(bf)
-        dx = (dy.astype(f32) + dxq).astype(bf)
-        return y, dx, dwg, dwu, dwd
+        h = (sa * b).astype(BF)
+        g = lax.dot_general(xd[1].reshape(1024, 8, 512), wd, (((1, 2), (0, 2)), ((), ())), preferred_element_type=F32)
+        da = (g * b * sig * (1.0 + a * (1.0 - sig))).astype(BF)
+        db = (g * sa).astype(BF)
+        dw, yo = reduce(h, da, db, xd, wg, wu, wd, x, dy)
+        dw = dw.reshape(3, 512, 896)
+        return yo[0], yo[1], dw[1], dw[2], dw[0].T
 
     return jax.shard_map(local, mesh=mesh, in_specs=(rows, wsp, wsp, dsp, rows), out_specs=(rows, rows, wsp, wsp, dsp), check_vma=False)

time: 680 us -> 383 us (0.56)
  waiting for transfers between devices: 396 us -> 0 us
  Pallas kernels: 102 us -> 303 us
  matrix products: 132 us -> 44 us
  between operations: 14.3 us -> 1.13 us
    reduce_scatter x5 -> x0, waiting for transfers between devices: 396 us -> none  [the longest x1 111 us: local(): yq = lax.psum_scatter(yp, 'tp', scatter_dimension=0, tiled=True)]
    pallas_call x1 -> x2, Pallas kernels: 102 us -> 303 us  [the longest x1 202 us: reduce(): pl.pallas_call(reduce_kernel, out_shape=(sd((3, 2, 256, 896), F32), sd((2...]
    dot_general x9 -> x3, matrix products: 132 us -> 44 us  [the longest x1 20.8 us: local(): lax.dot_general(xd[1].reshape(1024, 8, 512), wd, (((1, 2), (0, 2)), ((),...]
    reshape x1 -> x0, local copies, waits for them, and re-layouts: 17.4 us -> none  [local(): lax.dot_general(h, wd, (((1,), (1,)), ((), ())), preferred_element_type=f32)]
    slice x0 -> x2, local copies, waits for them, and re-layouts: none -> 12.5 us  [the longest x1 7.72 us: local(): xd[1].reshape(1024, 8, 512)]
  transfers between devices with their start and end apart: 5 -> 0, of which waited for: 5 -> 0; matrix products, arithmetic and copies ran while one was open for 12% -> 0% of each run, Pallas kernels for 0% -> 0%
where the time goes in v2:
time: 383 us; the launch traced here: 377 us
  Pallas kernels  303 us (79%)
  matrix products  44 us (11%)
  local copies, waits for them, and re-layouts  28.6 us (7%)
    pallas_call x1, Pallas kernels, reduce(): pl.pallas_call(reduce_kernel, out_shape=(sd((3, 2, 256, 896), F32), sd((2...  202 us
    pallas_call x1, Pallas kernels, gather(): pl.pallas_call(gather_kernel, out_shape=(sd((2, 1024, 4096), bf), sd((409...  101 us
    dot_general x1, matrix products, local(): lax.dot_general(xd[1].reshape(1024, 8, 512), wd, (((1, 2), (0, 2)), ((),...  20.8 us
    dot_general x1, matrix products, local(): a = jnp.dot(xd[0], wg, preferred_element_type=F32)  12.7 us
    unnamed x5, local copies, waits for them, and re-layouts  12.2 us
    dot_general x1, matrix products, local(): b = jnp.dot(xd[0], wu, preferred_element_type=F32)  10.6 us
    slice x1, local copies, waits for them, and re-layouts, local(): xd[1].reshape(1024, 8, 512)  7.72 us

profile of v2, /device:TPU:1, one launch (start us, length us, event | category | flops | bytes accessed | tf_op | source)
XLA Modules:
  0.0 376.8 jit_solution(4578563440147841637)
XLA Ops:
  0.6 101.3 %gather.1 = (bf16[2,1024,4096]{2,1,0:T(8,128)(2,1)}, bf16[4096,896]{1,0:T(8,128)(2,1)}, bf16[4096,896]{1,0:T(8,128)(2,1)}, bf16[8,896,512]{2,1,0:T(8,128)(2,1)}) custom-call(bf16[64,4096]{1,0:T(8,128)(2,1)} %xo.1, bf16[64,4096]{1,0:T(8,128)(2,1)} %dyo.1, bf16[512,896]{1,0:T(8,128)(2,1)} %wg_ref.1, bf16[512,896]{1,0:T(8,128)(2,1)} %wu_ref.1, ...), custom_call_target="tpu_custom_call" | custom-call | tf_op jit(solution)/shard_map/gather/pallas_call | solution.py:207
  102.0 0.0 copy-start
  102.0 0.0 copy-start.1
  102.0 12.7 %fusion.2 = f32[1024,896]{1,0:T(8,128)S(1)} fusion(bf16[4096,896]{1,0:T(8,128)(2,1)} %get-tuple-element.12.wg, bf16[2,1024,4096]{2,1,0:T(8,128)(2,1)} %get-tuple-element.11.xd), kind=kOutput, calls=%fused_computation.2 | convolution fusion | flops 7516192768 | bytes 19398656 | tf_op jit(solution)/shard_map/dot_general | solution.py:599
  114.7 0.0 copy-done
  114.7 0.0 copy-done.1
  114.7 10.6 %fusion = f32[1024,896]{1,0:T(8,128)} fusion(bf16[4096,896]{1,0:T(8,128)(2,1)S(1)} %copy-done.1, bf16[2,1024,4096]{2,1,0:T(8,128)(2,1)S(1)} %copy-done), kind=kOutput, calls=%fused_computation | convolution fusion | flops 7516192768 | bytes 19398656 | tf_op jit(solution)/shard_map/dot_general | solution.py:600
  125.3 7.7 %slice.26 = bf16[1,1024,4096]{2,1,0:T(8,128)(2,1)} slice(bf16[2,1024,4096]{2,1,0:T(8,128)(2,1)} %get-tuple-element.11.xd), slice={[1:2], [0:1024], [0:4096]} | slice | bytes 16777216 | tf_op jit(solution)/shard_map/slice | solution.py:604
  133.0 12.2 %copy.12 = bf16[128,8,8,512]{3,2,1,0:T(8,128)(2,1)} copy(bf16[128,8,8,512]{3,1,2,0:T(8,128)(2,1)} %bitcast.30) | data formatting | bytes 16777216
  145.2 20.8 %fusion.11 = (bf16[1024,896]{1,0:T(8,128)(2,1)}, bf16[1024,896]{1,0:T(8,128)(2,1)}, bf16[1024,896]{1,0:T(8,128)(2,1)}) fusion(f32[1024,896]{1,0:T(8,128)S(1)} %fusion.2, f32[1024,896]{1,0:T(8,128)} %fusion, bf16[8,896,512]{2,1,0:T(8,128)(2,1)} %get-tuple-element.14.wd, bf16[1024,8,512]{2,1,0:T(8,128)(2,1)} %bitcast.31), kind=kOutput, calls=%fused_computation.13 | convolution fusion | flops 7529955328 | bytes 28573696 | tf_op jit(solution)/shard_map/dot_general | solution.py:604
  166.0 201.7 %reduce.1 = (f32[3,2,256,896]{3,2,1,0:T(8,128)}, bf16[2,64,4096]{2,1,0:T(8,128)(2,1)}, f32[3,6,256,896]{3,2,1,0:T(8,128)}, f32[2,4,6,256,512]{4,3,2,1,0:T(8,128)}, bf16[2,4,1024,512]{3,2,1,0:T(8,128)(2,1)}) custom-call(bf16[1024,896]{1,0:T(8,128)(2,1)} %get-tuple-element.19.hh, bf16[1024,896]{1,0:T(8,128)(2,1)} %get-tuple-element.18.da, ...), custom_call_target="tpu_custom_call" | custom-call | tf_op jit(solution)/shard_map/reduce/pallas_call | solution.py:574
  367.7 2.3 slice_bitcast_fusion
  369.9 4.8 %fusion.13 = (f32[1,2,256,896]{3,2,1,0:T(8,128)S(1)}, f32[1,2,256,896]{3,2,1,0:T(8,128)}, f32[1,2,256,896]{3,2,1,0:T(8,128)}) fusion(f32[3,2,256,896]{3,2,1,0:T(8,128)} %get-tuple-element.16), kind=kLoop, calls=%fused_computation.19 | loop fusion | bytes 11010048 | tf_op jit(solution)/shard_map/slice | solution.py:609
  374.7 1.7 copy.11
Async XLA Ops:
  102.0 12.7 %copy-start = (bf16[2,1024,4096]{2,1,0:T(8,128)(2,1)S(1)}, bf16[2,1024,4096]{2,1,0:T(8,128)(2,1)}, u32[]{:S(2)}) copy-start(bf16[2,1024,4096]{2,1,0:T(8,128)(2,1)} %get-tuple-element.11.xd) | copy-start | bytes 50331652
  102.0 12.7 %copy-start.1 = (bf16[4096,896]{1,0:T(8,128)(2,1)S(1)}, bf16[4096,896]{1,0:T(8,128)(2,1)}, u32[]{:S(2)}) copy-start(bf16[4096,896]{1,0:T(8,128)(2,1)} %get-tuple-element.13.wu) | copy-start | bytes 22020100

commit v3 on v0

v3 whole, which is shorter than its diff:
```python
import jax
import jax.numpy as jnp
from jax import lax
from jax.experimental import pallas as pl
from jax.experimental.pallas import tpu as pltpu
from jax.sharding import PartitionSpec as P

MESH = pl.DeviceIdType.MESH
HBM = pl.BlockSpec(memory_space=pltpu.HBM)
NT = (((1,), (1,)), ((), ()))
TN = (((0,), (0,)), ((), ()))
F32 = jnp.float32
BF = jnp.bfloat16
NSEND = 107


def mlp_kernel(x_ref, dy_ref, wg_ref, wu_ref, wd_ref, dw, yo, xd, wgf, wuf, wdf, UV, XR, ZR, AP,
               B, A, XB, XS, WD, WX, ZB, ZS, Z2, US, res, ov,
               ssem, rsem, s_ld, s_put, s_c, s_a, s_ap, r_ap, s_b, r_b, s_xs, r_xs, s_zs, r_zs, s_2, r_2, s_w, s_xst, s_zst, s_xo, s_yo, s_uv, s_us):
    i = lax.axis_index("dp")
    j = lax.axis_index("tp")
    x, c, z, y = i // 2, i % 2, j // 4, j % 4
    xp, xm, xq, c1 = (x + 1) % 4, (x + 3) % 4, (x + 2) % 4, 1 - c
    dev = {
        "xp": {"dp": 2 * xp + c}, "xm": {"dp": 2 * xm + c}, "pc": {"dp": 2 * x + c1},
        "yp": {"tp": 4 * z + (y + 1) % 4}, "ym": {"tp": 4 * z + (y + 3) % 4},
        "zp": {"tp": 4 * ((z + 1) % 4) + y}, "zm": {"tp": 4 * ((z + 3) % 4) + y},
    }
    pos = ((z, y), (y, z))
    link = (("zp", "zm", "yp", "ym"), ("yp", "ym", "zp", "zm"))

    def remote(src, dst, ss, rs, to):
        return pltpu.make_async_remote_copy(src_ref=src, dst_ref=dst, send_sem=ss, recv_sem=rs, device_id=dev[to], device_id_type=MESH)

    def add(dst, src, n):
        def body(r, _):
            s = pl.ds(pl.multiple_of(r * 32, 32), 32)
            dst[s, :] = dst[s, :] + src[s, :]
            return 0
        lax.fori_loop(0, n // 32, body, 0)

    sends = []

    def send(src, dst, to):
        k = len(sends)
        r = remote(src, dst, ssem.at[k], rsem.at[k], to)
        r.start()
        sends.append(r)
        return r

    def wblk(k, xx, cc, half=None):
        ii = 2 * xx + cc
        if k < 2:
            r = (wgf, wuf)[k]
            if half is None:
                return r.at[pl.ds(pl.multiple_of(ii * 512, 512), 512), :]
            return r.at[pl.ds(pl.multiple_of(ii * 512 + half * 256, 256), 256), :]
        if half is None:
            return wdf.at[ii]
        return wdf.at[ii, pl.ds(half * 448, 448), :]

    def rows(a, col, s, p, lo=0, n=32):
        zz, yy = (p, s) if col == 0 else (s, p)
        return xd.at[a, pl.ds(pl.multiple_of((zz * 4 + yy) * 64 + col * 32 + lo, 16), n), :]

    GA = {}
    GA2 = {}
    GB = {}
    tail = {0: [], 1: []}

    def geo(col):
        sec, prim = pos[col]
        sp, sm, pp, pm = link[col]
        return prim, sec, pp, pm, sp, sm

    def start_own(a):
        for col in range(2):
            p, s, pp, pm, sp, sm = geo(col)
            src = res.at[a, pl.ds(col * 32, 32), :]
            dst = rows(a, col, p, s)
            GA[a, col] = (send(src, dst, pp), send(src, dst, pm))
            GB[a, col, 0] = (send(src, dst, sp), send(src, dst, sm))

    def step_a(a):
        for col in range(2):
            p, s, pp, pm, sp, sm = geo(col)
            out = []
            for fr, d, lo, fw in ((0, 3, 0, pp), (1, 1, 16, pm)):
                GA[a, col][fr].wait_recv()
                q = (p + d) % 4
                r = rows(a, col, q, s, lo, 16)
                out.append(send(r, r, fw))
                r = rows(a, col, q, s)
                GB[a, col, d] = (send(r, r, sp), send(r, r, sm))
            GA2[a, col] = out

    def step_a2(a):
        for col in range(2):
            p, s, pp, pm, sp, sm = geo(col)
            for m in GA2[a, col]:
                m.wait_recv()
            r = rows(a, col, (p + 2) % 4, s)
            GB[a, col, 2] = (send(r, r, sp), send(r, r, sm))

    def step_b(a, d):
        for col in range(2):
            p, s, pp, pm, sp, sm = geo(col)
            q = (p + d) % 4
            for fr, e, lo, fw in ((0, 3, 0, sp), (1, 1, 16, sm)):
                GB[a, col, d][fr].wait_recv()
                r = rows(a, col, q, (s + e) % 4, lo, 16)
                tail[a].append(send(r, r, fw))

    W1 = {}
    W2 = {}
    WP = {}
    w_in = (wg_ref, wu_ref, wd_ref)

    def start_w(k):
        dst = wblk(k, x, c)
        WP[k, 0] = [send(w_in[k], dst, "pc")]
        W1[k] = (send(w_in[k], dst, "xp"), send(w_in[k], dst, "xm"))

    def step_w(k):
        out = []
        for fr, xx, d, half, fw in ((0, xm, 3, 0, "xp"), (1, xp, 1, 1, "xm")):
            W1[k][fr].wait_recv()
            r = wblk(k, xx, c, half)
            out.append(send(r, r, fw))
            r = wblk(k, xx, c)
            WP[k, d] = [send(r, r, "pc")]
        W2[k] = out

    def step_w2(k):
        WP[k, 2] = []
        for half in range(2):
            W2[k][half].wait_recv()
            r = wblk(k, xq, c, half)
            WP[k, 2].append(send(r, r, "pc"))

    def wait_wp(k, d):
        for m in WP[k, d]:
            m.wait_recv()

    xpos = {0: x, 1: xp, 2: xq, 3: xm}
    order = ((0, 0), (0, 1), (3, 0), (1, 0), (3, 1), (1, 1), (2, 0), (2, 1))

    def blk(t):
        d, o = order[t]
        return 2 * xpos[d] + (c if o == 0 else c1)

    def a_slot(t):
        s = t % 4
        return A.at[s // 2, s % 2]

    def ld_ab(t):
        d, o = order[t]
        s = t % 4
        ii = blk(t)
        out = [pltpu.make_async_copy(xd.at[0, :, pl.ds(pl.multiple_of(ii * 512, 512), 512)], a_slot(t), s_c.at[s, 0])]
        for k in range(2):
            src = w_in[k] if t == 0 else wblk(k, xpos[d], c if o == 0 else c1)
            out.append(pltpu.make_async_copy(src, WX.at[s % 2, k, pl.ds((s // 2) * 512, 512), :], s_c.at[s, 1 + k]))
        return out

    def start_ab(t):
        d, o = order[t]
        if o == 1:
            for k in range(2):
                wait_wp(k, d)
        for l in ld_ab(t):
            l.start()

    def ab(t):
        for l in ld_ab(t):
            l.wait()
        s = t % 4

        def body(m, _):
            r = pl.ds(pl.multiple_of(m * 256, 256), 256)
            lhs = A[s // 2, s % 2, r, :]
            for k in range(2):
                v = jnp.dot(lhs, WX[s % 2, k, pl.ds((s // 2) * 512, 512), :], preferred_element_type=F32)
                if t == 0:
                    XB[2 * k + m // 2, m % 2] = v
                else:
                    XB[2 * k + m // 2, m % 2] += v
            return 0
        lax.fori_loop(0, 4, body, 0)

    def h_pass():
        def body(q, _):
            m = q // 8
            r = pl.ds(pl.multiple_of((q % 8) * 32, 32), 32)
            a = XB[m // 2, m % 2, r, :]
            b = XB[2 + m // 2, m % 2, r, :]
            sig = jax.nn.sigmoid(a)
            sa = a * sig
            XB[m // 2, m % 2, r, :] = b * sig * (1.0 + a * (1.0 - sig))
            XB[2 + m // 2, m % 2, r, :] = sa
            B[0, 0, pl.ds(pl.multiple_of(q * 32, 32), 32), :] = (sa * b).astype(BF)
            return 0
        lax.fori_loop(0, 32, body, 0)

    uv_put = pltpu.make_async_copy(XB, UV, s_uv)

    def ld_g(t):
        d, o = order[t]
        s = t % 4
        ii = blk(t)
        src = wd_ref if t == 0 else wdf.at[ii]
        return [pltpu.make_async_copy(xd.at[1, :, pl.ds(pl.multiple_of(ii * 512, 512), 512)], a_slot(t), s_c.at[s, 0]),
                pltpu.make_async_copy(src, WX.at[s % 2, s // 2, pl.ds(0, 896), pl.ds(0, 512)], s_c.at[s, 1])]

    def start_g(t):
        for l in ld_g(t):
            l.start()

    def gg(t):
        for l in ld_g(t):
            l.wait()
        s = t % 4

        def body(m, _):
            r = pl.ds(pl.multiple_of(m * 256, 256), 256)
            v = lax.dot_general(A[s // 2, s % 2, r, :], WX[s % 2, s // 2, pl.ds(0, 896), pl.ds(0, 512)], NT, preferred_element_type=F32)
            if t == 0:
                XS[m] = v
            else:
                XS[m] += v
            return 0
        lax.fori_loop(0, 4, body, 0)

    def us_load(q, k):
        m = q // 2
        return pltpu.make_async_copy(UV.at[2 * k + m // 2, m % 2, pl.ds(pl.multiple_of((q % 2) * 128, 128), 128), :], US.at[q % 2, k], s_us.at[q % 2, k])

    def dadb():
        for k in range(2):
            us_load(0, k).start()

        def body(q, _):
            @pl.when(q < 7)
            def _():
                for k in range(2):
                    us_load(q + 1, k).start()
            for k in range(2):
                us_load(q, k).wait()

            def inner(e, _):
                r = pl.ds(pl.multiple_of(e * 32, 32), 32)
                g = XS[q // 2, pl.ds(pl.multiple_of((q % 2) * 128 + e * 32, 32), 32), :]
                o = pl.ds(pl.multiple_of(q * 128 + e * 32, 32), 32)
                for k in range(2):
                    B[1 + k, 0, o, :] = (g * US[q % 2, k, r, :]).astype(BF)
                return 0
            lax.fori_loop(0, 4, inner, 0)
            return 0
        lax.fori_loop(0, 8, body, 0)

    def chunk(idx):
        return (x + 6 - idx) % 4

    bp = [remote(B.at[k, 0], B.at[k, 1], s_b.at[k], r_b.at[k], "pc") for k in range(3)]

    def ap(arr, idx):
        return remote(xd.at[arr, :, pl.ds(pl.multiple_of(1024 * chunk(idx) + 512 * c1, 512), 512)], AP.at[arr, idx], s_ap.at[arr, idx], r_ap.at[arr, idx], "pc")

    def load_a(arr, idx):
        slot = idx % 2
        return (pltpu.make_async_copy(xd.at[arr, :, pl.ds(pl.multiple_of(1024 * chunk(idx) + 512 * c, 512), 512)], A.at[slot, 0], s_a.at[slot, 0]),
                pltpu.make_async_copy(AP.at[arr, idx], A.at[slot, 1], s_a.at[slot, 1]))

    def start_a(arr, idx):
        for l in load_a(arr, idx):
            l.start()

    def dot_x(k, idx):
        slot = idx % 2
        for l in load_a(0, idx):
            l.wait()

        def body(m, _):
            cols = pl.ds(pl.multiple_of(m * 256, 256), 256)
            XB[idx, m] = (lax.dot_general(A[slot, 0, :, cols], B[k, 0], TN, preferred_element_type=F32)
                          + lax.dot_general(A[slot, 1, :, cols], B[k, 1], TN, preferred_element_type=F32))
            return 0
        lax.fori_loop(0, 2, body, 0)

    def xmsg(k, t):
        src = (XB.at[0, 0], XB.at[0, 1], XB.at[1, 1], XB.at[3, 0], XB.at[1, 0], XB.at[3, 1])[t]
        return remote(src, XR.at[k, t], s_xs.at[t], r_xs.at[k, t], ("xp", "xm")[t % 2])

    def x1(k):
        arr = 1 - min(k, 1)
        if k < 2:
            for idx in range(2):
                ap(arr, idx).wait_recv()
                start_a(arr, idx)
        bp[k].wait_recv()
        if k == 0:
            uv_put.wait()
        else:
            xmsg(k - 1, 0).wait_send()
            xmsg(k - 1, 1).wait_send()
        dot_x(k, 0)
        xmsg(k, 0).start()
        xmsg(k, 1).start()
        if k < 2:
            ap(arr, 2).wait_recv()
        start_a(arr, 2)

    def x2(k):
        arr = 1 - min(k, 1)
        if k > 0:
            for t in range(2, 6):
                xmsg(k - 1, t).wait_send()
            xout(k - 1).wait()

        def body(idx, _):
            dot_x(k, idx)
            if k == 1:
                @pl.when(idx == 1)
                def _():
                    ap(arr, 3).wait_recv()
                start_a(0, (idx + 2) % 4)
            else:
                @pl.when(idx == 1)
                def _():
                    if k == 0:
                        ap(arr, 3).wait_recv()
                    start_a(arr, 3)
            return 0
        lax.fori_loop(1, 4, body, 0)
        xmsg(k, 2).start()
        xmsg(k, 3).start()

    def xstage(k, t, slot):
        return pltpu.make_async_copy(XR.at[k, t], XS.at[slot], s_xst.at[slot])

    def x3(k):
        for t in range(2):
            xmsg(k, t).wait_recv()
            xstage(k, t, t).start()
        for t in range(2):
            xstage(k, t, t).wait()
            add(XB.at[(1, 3)[t], t], XS.at[t], 256)
            xmsg(k, 4 + t).start()

    def xout(k):
        return pltpu.make_async_copy(XB.at[2], dw.at[k], s_xo)

    def xf(k):
        todo = ((3, 0), (2, 1), (4, 0), (5, 1))
        for n, (t, h) in enumerate(todo):
            xmsg(k, t).wait_recv()
            xstage(k, t, n).start()
        for n, (t, h) in enumerate(todo):
            xstage(k, t, n).wait()
            add(XB.at[2, h], XS.at[n], 256)
        xout(k).start()

    def pair(n, col):
        return ((0, 3), (1, 2))[col][n % 2]

    def load_w(n):
        out = []
        for col in range(2):
            d = pair(n, col)
            q = xpos[d]
            if n < 2:
                if d == 0:
                    out.append(pltpu.make_async_copy(wd_ref, WD.at[col, c], s_w.at[col, 0]))
                    out.append(pltpu.make_async_copy(wdf.at[2 * x + c1], WD.at[col, c1], s_w.at[col, 1]))
                else:
                    out.append(pltpu.make_async_copy(wdf.at[pl.ds(2 * q, 2)], WD.at[col], s_w.at[col, 0]))
            else:
                for k in range(2):
                    full = (wgf, wuf)[k]
                    if d == 0:
                        out.append(pltpu.make_async_copy(w_in[k], WX.at[col, k, pl.ds(pl.multiple_of(512 * c, 512), 512), :], s_w.at[col, 2 * k]))
                        out.append(pltpu.make_async_copy(full.at[pl.ds(pl.multiple_of(1024 * x + 512 * c1, 512), 512), :],
                                                         WX.at[col, k, pl.ds(pl.multiple_of(512 * c1, 512), 512), :], s_w.at[col, 2 * k + 1]))
                    else:
                        out.append(pltpu.make_async_copy(full.at[pl.ds(pl.multiple_of(1024 * q, 1024), 1024), :], WX.at[col, k], s_w.at[col, 2 * k]))
        for o in out:
            o.start()
        return out

    wl = {}

    def dots_z(n, lo, hi):
        m = hi - lo

        def body(q, _):
            col = q // m
            idx = lo + q % m
            p = z + col * (y - z)
            ch = (p + 6 - idx) % 4
            s1 = 256 - 192 * col
            s2 = 64 + 192 * col
            own = (idx // 2) * (1 - idx // 3)
            slot = idx + own * 2 * (n % 2)

            def lhs(k):
                return jnp.concatenate([B[k, 0, pl.ds(pl.multiple_of(ch * s1 + g * s2, 64), 64), :] for g in range(4)], axis=0)

            if n < 2:
                l = lhs(0)
                for h in range(2):
                    ZB[col, slot, h] = jnp.dot(l, WD[col, h], preferred_element_type=F32)
            else:
                l = lhs(1)
                u = lhs(2)
                for h in range(2):
                    r = pl.ds(512 * h, 512)
                    ZB[col, slot, h] = (lax.dot_general(l, WX[col, 0, r, :], NT, preferred_element_type=F32)
                                        + lax.dot_general(u, WX[col, 1, r, :], NT, preferred_element_type=F32))
            return 0
        lax.fori_loop(0, 2 * m, body, 0)

    def zmsg(n, col, t):
        src = ((0, 0), (0, 1), (1, 1), (3, 0), (1, 0), (3, 1))[t]
        return remote(ZB.at[col, src[0], src[1]], ZR.at[col, n, t], s_zs.at[col, t], r_zs.at[col, n, t], link[col][t % 2])

    def own(n, col, h):
        return ZB.at[col, 2 + 2 * (n % 2), h]

    def sub(n, col, h, d):
        s = (pos[col][1] + d) % 4
        return ZB.at[col, 2 + 2 * (n % 2), h, pl.ds(pl.multiple_of(s * 64, 64), 64), :]

    def msg2(n, col, t):
        h, d = ((0, 2), (1, 2), (1, 1), (0, 3), (0, 1), (1, 3))[t]
        return remote(sub(n, col, h, d), Z2.at[col, n % 2, t], s_2.at[col, n % 2, t], r_2.at[col, n, t], link[col][2 + t % 2])

    def p1(n):
        for l in wl[n]:
            l.wait()
        if n > 0:
            for col in range(2):
                for t in range(2):
                    zmsg(n - 1, col, t).wait_send()
        dots_z(n, 0, 1)
        for t in range(2):
            for col in range(2):
                zmsg(n, col, t).start()

    def p2(n):
        if n > 0:
            for col in range(2):
                for t in range(2, 6):
                    zmsg(n - 1, col, t).wait_send()
        if n > 1:
            for col in range(2):
                for t in range(6):
                    msg2(n - 2, col, t).wait_send()
        dots_z(n, 1, 4)
        for t in range(2, 4):
            for col in range(2):
                zmsg(n, col, t).start()

    def zstage(n, col, t, slot):
        return pltpu.make_async_copy(ZR.at[col, n, t], ZS.at[col, slot], s_zst.at[col, slot])

    def p4(n):
        for t in range(2):
            for col in range(2):
                zmsg(n, col, t).wait_recv()
                zstage(n, col, t, t).start()
        for t in range(2):
            for col in range(2):
                zstage(n, col, t, t).wait()
                add(ZB.at[col, (1, 3)[t], t], ZS.at[col, t], 256)
                zmsg(n, col, 4 + t).start()

    def f(n):
        todo = ((3, 0), (2, 1), (4, 0), (5, 1))
        for e, (t, h) in enumerate(todo):
            for col in range(2):
                zmsg(n, col, t).wait_recv()
                zstage(n, col, t, e).start()
        for e, (t, h) in enumerate(todo):
            for col in range(2):
                zstage(n, col, t, e).wait()
                add(own(n, col, h), ZS.at[col, e], 256)
        for t in range(4):
            for col in range(2):
                msg2(n, col, t).start()

    def hh2(n):
        for t in range(2):
            for col in range(2):
                msg2(n, col, t).wait_recv()
                add(sub(n, col, t, (1, 3)[t]), Z2.at[col, n % 2, t], 64)
                msg2(n, col, 4 + t).start()

    def zf(n):
        a = n // 2
        for col in range(2):
            q = xpos[pair(n, col)]
            for h, ts in ((0, (3, 4)), (1, (2, 5))):
                for t in ts:
                    msg2(n, col, t).wait_recv()
                cs = pl.ds(pl.multiple_of(1024 * q + 512 * h, 512), 512)
                v = sub(n, col, h, 0)[...] + Z2[col, n % 2, ts[0]] + Z2[col, n % 2, ts[1]]
                ov[a, :, cs] = (res[a, :, cs].astype(F32) + v).astype(BF)

    own_ld = [pltpu.make_async_copy(r, res.at[k], s_ld.at[k]) for k, r in enumerate((x_ref, dy_ref))]
    for l in own_ld:
        l.start()
    barrier = pltpu.get_barrier_semaphore()
    for d in dev.values():
        pl.semaphore_signal(barrier, inc=1, device_id=d, device_id_type=MESH)
    pl.semaphore_wait(barrier, len(dev))
    own_ld[0].wait()
    start_own(0)
    start_w(0)
    start_w(1)
    own_ld[1].wait()
    put = pltpu.make_async_copy(res, xd.at[:, pl.ds(pl.multiple_of(j * 64, 64), 64), :], s_put)
    put.start()
    step_a(0)
    step_b(0, 0)
    step_a2(0)
    step_w(0)
    step_b(0, 3)
    start_own(1)
    step_b(0, 1)
    step_b(0, 2)
    step_w(1)
    start_w(2)
    put.wait()
    for m in tail[0]:
        m.wait_recv()
    for idx in range(4):
        ap(0, idx).start()
    start_ab(0)
    start_ab(1)
    ab(0)
    step_a(1)
    start_ab(2)
    ab(1)
    step_b(1, 0)
    step_w2(0)
    start_ab(3)
    ab(2)
    step_a2(1)
    start_ab(4)
    ab(3)
    step_b(1, 3)
    start_ab(5)
    ab(4)
    step_w2(1)
    start_ab(6)
    ab(5)
    step_b(1, 1)
    start_ab(7)
    ab(6)
    ab(7)
    step_b(1, 2)
    h_pass()
    bp[0].start()
    uv_put.start()
    step_w(2)
    wait_wp(2, 0)
    wait_wp(2, 1)
    wl[0] = load_w(0)
    p1(0)
    for m in tail[1]:
        m.wait_recv()
    for idx in range(4):
        ap(1, idx).start()
    x1(0)
    step_w2(2)
    p2(0)
    wait_wp(2, 3)
    wait_wp(2, 2)
    wl[1] = load_w(1)
    p4(0)
    x2(0)
    for t in range(3):
        start_g(t)
    for t in range(8):
        gg(t)
        if t + 3 < 8:
            start_g(t + 3)
        if t == 3:
            p1(1)
    f(0)
    dadb()
    bp[1].start()
    bp[2].start()
    wl[2] = load_w(2)
    x3(0)
    p2(1)
    x1(1)
    hh2(0)
    zf(0)
    p4(1)
    xf(0)
    x2(1)
    p1(2)
    f(1)
    p2(2)
    wl[3] = load_w(3)
    x3(1)
    hh2(1)
    zf(1)
    p4(2)
    x1(2)
    p1(3)
    f(2)
    xf(1)
    x2(2)
    p2(3)
    hh2(2)
    zf(2)
    p4(3)
    x3(2)
    f(3)
    hh2(3)
    zf(3)
    out = pltpu.make_async_copy(ov, yo, s_yo)
    out.start()
    xf(2)
    for r in sends:
        r.wait_send()
    for t in range(6):
        xmsg(2, t).wait_send()
        for col in range(2):
            zmsg(3, col, t).wait_send()
            msg2(2, col, t).wait_send()
            msg2(3, col, t).wait_send()
    for k in range(3):
        bp[k].wait_send()
    for arr in range(2):
        for idx in range(4):
            ap(arr, idx).wait_send()
    xout(2).wait()
    out.wait()


def mlp(x, dy, wg, wu, wd):
    sd = jax.ShapeDtypeStruct
    dma = pltpu.SemaphoreType.DMA
    V = pltpu.VMEM
    return pl.pallas_call(
        mlp_kernel,
        out_shape=(sd((3, 2, 256, 896), F32), sd((2, 64, 4096), BF),
                   sd((2, 1024, 4096), BF), sd((4096, 896), BF), sd((4096, 896), BF), sd((8, 896, 512), BF), sd((4, 2, 256, 896), F32),
                   sd((3, 6, 256, 896), F32), sd((2, 4, 6, 256, 512), F32), sd((2, 4, 1024, 512), BF)),
        in_specs=[HBM] * 5,
        out_specs=(HBM,) * 10,
        scratch_shapes=[
            V((3, 2, 1024, 896), BF), V((2, 2, 1024, 512), BF), V((4, 2, 256, 896), F32), V((4, 256, 896), F32),
            V((2, 2, 896, 512), BF), V((2, 2, 1024, 896), BF), V((2, 5, 2, 256, 512), F32), V((2, 4, 256, 512), F32),
            V((2, 2, 6, 64, 512), F32), V((2, 2, 128, 896), F32), V((2, 64, 4096), BF), V((2, 64, 4096), BF),
            dma((NSEND,)), dma((NSEND,)), dma((2,)), dma, dma((4, 3)),
            dma((2, 2)), dma((2, 4)), dma((2, 4)), dma((3,)), dma((3,)), dma((6,)), dma((3, 6)),
            dma((2, 6)), dma((2, 4, 6)), dma((2, 2, 6)), dma((2, 4, 6)), dma((2, 4)), dma((4,)), dma((2, 4)), dma, dma, dma, dma((2, 2)),
        ],
        compiler_params=pltpu.CompilerParams(collective_id=1, has_side_effects=True, vmem_limit_bytes=67043328),
        name="mlp",
    )(x, dy, wg, wu, wd)[:2]


def solution(mesh):
    rows = P(("dp", "tp"), None)
    wsp = P("dp", "tp")
    dsp = P("tp", "dp")

    def local(x, w_gate, w_up, w_down, dy):
        dw, yo = mlp(x, dy, w_gate, w_up, w_down)
        dw = dw.reshape(3, 512, 896)
        return yo[0], yo[1], dw[1], dw[2], dw[0].T

    return jax.shard_map(local, mesh=mesh, in_specs=(rows, wsp, wsp, dsp, rows), out_specs=(rows, rows, wsp, wsp, dsp), check_vma=False)
```

time: 1120 us -> 325 us (0.29)
  waiting for transfers between devices: 862 us -> 0 us
  Pallas kernels: 0 us -> 313 us
  matrix products: 118 us -> 0 us
  local copies, waits for them, and re-layouts: 59.3 us -> 8.73 us
  blocking collectives: 28.3 us -> 0 us
  other arithmetic: 15.6 us -> 0 us
  between operations: 14.7 us -> 0.64 us
  starting transfers between devices: 12.2 us -> 0 us
    reduce_scatter x2 -> x0, waiting for transfers between devices: 408 us -> none  [the longest x1 291 us: local(): lax.psum_scatter(jnp.dot(xt, w, preferred_element_type=f32), 'dp', scatte...]
    pallas_call x0 -> x1, Pallas kernels: none -> 313 us  [mlp(): pl.pallas_call(mlp_kernel, out_shape=(sd((3, 2, 256, 896), F32), sd((2, 6...]
    all_gather x4 -> x0, waiting for transfers between devices: 291 us -> none  [the longest x1 116 us: local(): lax.all_gather(jnp.concatenate([da, db], axis=1), 'dp', axis=0, tiled=True)]
    unnamed x10 -> x0, waiting for transfers between devices: 162 us -> none
    dot_general x6 -> x0, matrix products: 118 us -> none  [the longest x1 27.6 us: local(): jnp.dot(xt, w, preferred_element_type=f32)]
    reshape x4 -> x0, local copies, waits for them, and re-layouts: 32.7 us -> none  [the longest x2 29.9 us: combine_tp(): q.reshape(nx, ny, tl, dl)]
    all_to_all x2 -> x0, blocking collectives: 28.3 us -> none  [to_columns(): return lax.all_to_all(vr, 'dp', 0, 0, tiled=True)]
    transpose x4 -> x0, local copies, waits for them, and re-layouts: 15.9 us -> none  [the longest x2 15.6 us: all_tokens(): return vg.transpose(1, 0, 2, 3).reshape(nx * ny * tl, dl)]
  transfers between devices with their start and end apart: 10 -> 0, of which waited for: 8 -> 0; matrix products, arithmetic and copies ran while one was open for 16% -> 0% of each run, Pallas kernels for 0% -> 0%
where the time goes in v3:
time: 325 us; the launch traced here: 322 us
  Pallas kernels  313 us (96%)
  local copies, waits for them, and re-layouts  8.73 us (3%)
    pallas_call x1, Pallas kernels, mlp(): pl.pallas_call(mlp_kernel, out_shape=(sd((3, 2, 256, 896), F32), sd((2, 6...  313 us

profile of v3, /device:TPU:1, one launch (start us, length us, event | category | flops | bytes accessed | tf_op | source)
XLA Modules:
  0.0 322.1 jit_solution(13010429346671498769)
XLA Ops:
  0.6 312.7 %mlp.1 = (f32[3,2,256,896]{3,2,1,0:T(8,128)}, bf16[2,64,4096]{2,1,0:T(8,128)(2,1)}, bf16[2,1024,4096]{2,1,0:T(8,128)(2,1)}, bf16[4096,896]{1,0:T(8,128)(2,1)}, b...) custom-call(bf16[64,4096]{1,0:T(8,128)(2,1)} %x_ref.1, ...), custom_call_target="tpu_custom_call" | custom-call | tf_op jit(solution)/shard_map/mlp/pallas_call | solution.py:648
  313.4 2.3 slice_bitcast_fusion
  315.6 4.8 %fusion = (f32[1,2,256,896]{3,2,1,0:T(8,128)S(1)}, f32[1,2,256,896]{3,2,1,0:T(8,128)}, f32[1,2,256,896]{3,2,1,0:T(8,128)}) fusion(f32[3,2,256,896]{3,2,1,0:T(8,128)} %get-tuple-element.8), kind=kLoop, calls=%fused_computation.2 | loop fusion | bytes 11010048 | tf_op jit(solution)/shard_map/slice | solution.py:676
  320.4 1.7 copy.10

commit v4 on v3

--- a/solution.py
+++ b/solution.py
@@ -73,74 +73,102 @@
         sp, sm, pp, pm = link[col]
         return prim, sec, pp, pm, sp, sm
 
-    def start_own(a):
+    seen = set()
+
+    def once(m):
+        if id(m) not in seen:
+            seen.add(id(m))
+            m.wait_recv()
+
+    def ga(a):
         for col in range(2):
             p, s, pp, pm, sp, sm = geo(col)
             src = res.at[a, pl.ds(col * 32, 32), :]
-            dst = rows(a, col, p, s)
-            GA[a, col] = (send(src, dst, pp), send(src, dst, pm))
-            GB[a, col, 0] = (send(src, dst, sp), send(src, dst, sm))
-
-    def step_a(a):
+            GA[a, col] = [send(src, rows(a, col, p, s), to) for to in (pp, pm)]
+
+    def gb0(a):
         for col in range(2):
             p, s, pp, pm, sp, sm = geo(col)
-            out = []
+            src = res.at[a, pl.ds(col * 32, 32), :]
+            GB[a, col, 0] = [send(src, rows(a, col, p, s), to) for to in (sp, sm)]
+
+    def ga2(a):
+        for col in range(2):
+            p, s, pp, pm, sp, sm = geo(col)
+            GA2[a, col] = []
             for fr, d, lo, fw in ((0, 3, 0, pp), (1, 1, 16, pm)):
-                GA[a, col][fr].wait_recv()
-                q = (p + d) % 4
-                r = rows(a, col, q, s, lo, 16)
-                out.append(send(r, r, fw))
-                r = rows(a, col, q, s)
-                GB[a, col, d] = (send(r, r, sp), send(r, r, sm))
-            GA2[a, col] = out
-
-    def step_a2(a):
+                once(GA[a, col][fr])
+                r = rows(a, col, (p + d) % 4, s, lo, 16)
+                GA2[a, col].append(send(r, r, fw))
+
+    def gb31(a):
+        for col in range(2):
+            p, s, pp, pm, sp, sm = geo(col)
+            for d in (3, 1):
+                r = rows(a, col, (p + d) % 4, s)
+                GB[a, col, d] = [send(r, r, to) for to in (sp, sm)]
+
+    def gb2(a):
         for col in range(2):
             p, s, pp, pm, sp, sm = geo(col)
             for m in GA2[a, col]:
-                m.wait_recv()
+                once(m)
             r = rows(a, col, (p + 2) % 4, s)
-            GB[a, col, 2] = (send(r, r, sp), send(r, r, sm))
-
-    def step_b(a, d):
+            GB[a, col, 2] = [send(r, r, to) for to in (sp, sm)]
+
+    def gf(a, d):
         for col in range(2):
             p, s, pp, pm, sp, sm = geo(col)
             q = (p + d) % 4
             for fr, e, lo, fw in ((0, 3, 0, sp), (1, 1, 16, sm)):
-                GB[a, col, d][fr].wait_recv()
+                once(GB[a, col, d][fr])
                 r = rows(a, col, q, (s + e) % 4, lo, 16)
                 tail[a].append(send(r, r, fw))
+
+    def gend(a):
+        if a == 0:
+            put.wait()
+        for m in tail[a]:
+            once(m)
+        for idx in range(4):
+            ap(a, idx).start()
 
     W1 = {}
     W2 = {}
     WP = {}
     w_in = (wg_ref, wu_ref, wd_ref)
 
-    def start_w(k):
-        dst = wblk(k, x, c)
-        WP[k, 0] = [send(w_in[k], dst, "pc")]
-        W1[k] = (send(w_in[k], dst, "xp"), send(w_in[k], dst, "xm"))
-
-    def step_w(k):
-        out = []
+    def wpc(k):
+        WP[k, 0] = [send(w_in[k], wblk(k, x, c), "pc")]
+
+    def wown(k):
+        W1[k] = [send(w_in[k], wblk(k, x, c), to) for to in ("xp", "xm")]
+
+    def wf(k):
+        W2[k] = []
         for fr, xx, d, half, fw in ((0, xm, 3, 0, "xp"), (1, xp, 1, 1, "xm")):
-            W1[k][fr].wait_recv()
+            once(W1[k][fr])
             r = wblk(k, xx, c, half)
-            out.append(send(r, r, fw))
+            W2[k].append(send(r, r, fw))
             r = wblk(k, xx, c)
             WP[k, d] = [send(r, r, "pc")]
-        W2[k] = out
-
-    def step_w2(k):
+
+    def wf2(k):
         WP[k, 2] = []
         for half in range(2):
-            W2[k][half].wait_recv()
+            once(W2[k][half])
             r = wblk(k, xq, c, half)
             WP[k, 2].append(send(r, r, "pc"))
 
-    def wait_wp(k, d):
-        for m in WP[k, d]:
-            m.wait_recv()
+    def have(k, d, o):
+        if o == 1:
+            for m in WP[k, d]:
+                once(m)
+        elif d == 2:
+            for m in W2[k]:
+                once(m)
+        elif d:
+            once(W1[k][0 if d == 3 else 1])
 
     xpos = {0: x, 1: xp, 2: xq, 3: xm}
     order = ((0, 0), (0, 1), (3, 0), (1, 0), (3, 1), (1, 1), (2, 0), (2, 1))
@@ -163,11 +191,9 @@
             out.append(pltpu.make_async_copy(src, WX.at[s % 2, k, pl.ds((s // 2) * 512, 512), :], s_c.at[s, 1 + k]))
         return out
 
-    def start_ab(t):
-        d, o = order[t]
-        if o == 1:
-            for k in range(2):
-                wait_wp(k, d)
+    def sab(t):
+        for k in range(2):
+            have(k, *order[t])
         for l in ld_ab(t):
             l.start()
 
@@ -188,7 +214,7 @@
             return 0
         lax.fori_loop(0, 4, body, 0)
 
-    def h_pass():
+    def hp():
         def body(q, _):
             m = q // 8
             r = pl.ds(pl.multiple_of((q % 8) * 32, 32), 32)
@@ -201,6 +227,8 @@
             B[0, 0, pl.ds(pl.multiple_of(q * 32, 32), 32), :] = (sa * b).astype(BF)
             return 0
         lax.fori_loop(0, 32, body, 0)
+        bp[0].start()
+        uv_put.start()
 
     uv_put = pltpu.make_async_copy(XB, UV, s_uv)
 
@@ -212,7 +240,8 @@
         return [pltpu.make_async_copy(xd.at[1, :, pl.ds(pl.multiple_of(ii * 512, 512), 512)], a_slot(t), s_c.at[s, 0]),
                 pltpu.make_async_copy(src, WX.at[s % 2, s // 2, pl.ds(0, 896), pl.ds(0, 512)], s_c.at[s, 1])]
 
-    def start_g(t):
+    def sg(t):
+        have(2, *order[t])
         for l in ld_g(t):
             l.start()
 
@@ -257,33 +286,46 @@
             lax.fori_loop(0, 4, inner, 0)
             return 0
         lax.fori_loop(0, 8, body, 0)
+        bp[1].start()
+        bp[2].start()
 
     def chunk(idx):
         return (x + 6 - idx) % 4
 
     bp = [remote(B.at[k, 0], B.at[k, 1], s_b.at[k], r_b.at[k], "pc") for k in range(3)]
 
+    APM = {}
+
     def ap(arr, idx):
+        if (arr, idx) not in APM:
+            APM[arr, idx] = ap_(arr, idx)
+        return APM[arr, idx]
+
+    def ap_(arr, idx):
         return remote(xd.at[arr, :, pl.ds(pl.multiple_of(1024 * chunk(idx) + 512 * c1, 512), 512)], AP.at[arr, idx], s_ap.at[arr, idx], r_ap.at[arr, idx], "pc")
 
-    def load_a(arr, idx):
-        slot = idx % 2
-        return (pltpu.make_async_copy(xd.at[arr, :, pl.ds(pl.multiple_of(1024 * chunk(idx) + 512 * c, 512), 512)], A.at[slot, 0], s_a.at[slot, 0]),
-                pltpu.make_async_copy(AP.at[arr, idx], A.at[slot, 1], s_a.at[slot, 1]))
-
-    def start_a(arr, idx):
-        for l in load_a(arr, idx):
+    seq = (0, 1, 3, 2)
+
+    def load_a(k, n):
+        arr = 1 - min(k, 1)
+        idx = seq[n]
+        return (pltpu.make_async_copy(xd.at[arr, :, pl.ds(pl.multiple_of(1024 * chunk(idx) + 512 * c, 512), 512)], A.at[n % 2, 0], s_a.at[n % 2, 0]),
+                pltpu.make_async_copy(AP.at[arr, idx], A.at[n % 2, 1], s_a.at[n % 2, 1]))
+
+    def start_a(k, n):
+        once(ap(1 - min(k, 1), seq[n]))
+        for l in load_a(k, n):
             l.start()
 
-    def dot_x(k, idx):
-        slot = idx % 2
-        for l in load_a(0, idx):
+    def dot_x(k, n):
+        slot = n % 2
+        for l in load_a(k, n):
             l.wait()
 
         def body(m, _):
             cols = pl.ds(pl.multiple_of(m * 256, 256), 256)
-            XB[idx, m] = (lax.dot_general(A[slot, 0, :, cols], B[k, 0], TN, preferred_element_type=F32)
-                          + lax.dot_general(A[slot, 1, :, cols], B[k, 1], TN, preferred_element_type=F32))
+            XB[seq[n], m] = (lax.dot_general(A[slot, 0, :, cols], B[k, 0], TN, preferred_element_type=F32)
+                             + lax.dot_general(A[slot, 1, :, cols], B[k, 1], TN, preferred_element_type=F32))
             return 0
         lax.fori_loop(0, 2, body, 0)
 
@@ -291,12 +333,11 @@
         src = (XB.at[0, 0], XB.at[0, 1], XB.at[1, 1], XB.at[3, 0], XB.at[1, 0], XB.at[3, 1])[t]
         return remote(src, XR.at[k, t], s_xs.at[t], r_xs.at[k, t], ("xp", "xm")[t % 2])
 
+    def xl0(k):
+        start_a(k, 0)
+        start_a(k, 1)
+
     def x1(k):
-        arr = 1 - min(k, 1)
-        if k < 2:
-            for idx in range(2):
-                ap(arr, idx).wait_recv()
-                start_a(arr, idx)
         bp[k].wait_recv()
         if k == 0:
             uv_put.wait()
@@ -306,34 +347,26 @@
         dot_x(k, 0)
         xmsg(k, 0).start()
         xmsg(k, 1).start()
-        if k < 2:
-            ap(arr, 2).wait_recv()
-        start_a(arr, 2)
+        start_a(k, 2)
 
     def x2(k):
-        arr = 1 - min(k, 1)
         if k > 0:
             for t in range(2, 6):
                 xmsg(k - 1, t).wait_send()
+        dot_x(k, 1)
+        start_a(k, 3)
+        xmsg(k, 2).start()
+        dot_x(k, 2)
+        if k == 1:
+            start_a(2, 0)
+        xmsg(k, 3).start()
+
+    def x2o(k):
+        if k > 0:
             xout(k - 1).wait()
-
-        def body(idx, _):
-            dot_x(k, idx)
-            if k == 1:
-                @pl.when(idx == 1)
-                def _():
-                    ap(arr, 3).wait_recv()
-                start_a(0, (idx + 2) % 4)
-            else:
-                @pl.when(idx == 1)
-                def _():
-                    if k == 0:
-                        ap(arr, 3).wait_recv()
-                    start_a(arr, 3)
-            return 0
-        lax.fori_loop(1, 4, body, 0)
-        xmsg(k, 2).start()
-        xmsg(k, 3).start()
+        dot_x(k, 3)
+        if k == 1:
+            start_a(2, 1)
 
     def xstage(k, t, slot):
         return pltpu.make_async_copy(XR.at[k, t], XS.at[slot], s_xst.at[slot])
@@ -363,7 +396,11 @@
     def pair(n, col):
         return ((0, 3), (1, 2))[col][n % 2]
 
-    def load_w(n):
+    def lw(n):
+        if n < 2:
+            for col in range(2):
+                have(2, pair(n, col), 0)
+                have(2, pair(n, col), 1)
         out = []
         for col in range(2):
             d = pair(n, col)
@@ -385,16 +422,15 @@
                         out.append(pltpu.make_async_copy(full.at[pl.ds(pl.multiple_of(1024 * q, 1024), 1024), :], WX.at[col, k], s_w.at[col, 2 * k]))
         for o in out:
             o.start()
-        return out
+        wl[n] = out
 
     wl = {}
 
-    def dots_z(n, lo, hi):
-        m = hi - lo
+    def dots_z(n, lo, m):
 
         def body(q, _):
             col = q // m
-            idx = lo + q % m
+            idx = lo + 2 * (q % m)
             p = z + col * (y - z)
             ch = (p + 6 - idx) % 4
             s1 = 256 - 192 * col
@@ -432,7 +468,7 @@
 
     def msg2(n, col, t):
         h, d = ((0, 2), (1, 2), (1, 1), (0, 3), (0, 1), (1, 3))[t]
-        return remote(sub(n, col, h, d), Z2.at[col, n % 2, t], s_2.at[col, n % 2, t], r_2.at[col, n, t], link[col][2 + t % 2])
+        return remote(sub(n, col, h, d), Z2.at[col, n, t], s_2.at[col, n % 2, t], r_2.at[col, n, t], link[col][2 + t % 2])
 
     def p1(n):
         for l in wl[n]:
@@ -451,14 +487,17 @@
             for col in range(2):
                 for t in range(2, 6):
                     zmsg(n - 1, col, t).wait_send()
+        dots_z(n, 1, 2)
+        for t in range(2, 4):
+            for col in range(2):
+                zmsg(n, col, t).start()
+
+    def p2o(n):
         if n > 1:
             for col in range(2):
                 for t in range(6):
                     msg2(n - 2, col, t).wait_send()
-        dots_z(n, 1, 4)
-        for t in range(2, 4):
-            for col in range(2):
-                zmsg(n, col, t).start()
+        dots_z(n, 2, 1)
 
     def zstage(n, col, t, slot):
         return pltpu.make_async_copy(ZR.at[col, n, t], ZS.at[col, slot], s_zst.at[col, slot])
@@ -488,11 +527,11 @@
             for col in range(2):
                 msg2(n, col, t).start()
 
-    def hh2(n):
+    def hh(n):
         for t in range(2):
             for col in range(2):
                 msg2(n, col, t).wait_recv()
-                add(sub(n, col, t, (1, 3)[t]), Z2.at[col, n % 2, t], 64)
+                add(sub(n, col, t, (1, 3)[t]), Z2.at[col, n, t], 64)
                 msg2(n, col, 4 + t).start()
 
     def zf(n):
@@ -503,8 +542,10 @@
                 for t in ts:
                     msg2(n, col, t).wait_recv()
                 cs = pl.ds(pl.multiple_of(1024 * q + 512 * h, 512), 512)
-                v = sub(n, col, h, 0)[...] + Z2[col, n % 2, ts[0]] + Z2[col, n % 2, ts[1]]
+                v = sub(n, col, h, 0)[...] + Z2[col, n, ts[0]] + Z2[col, n, ts[1]]
                 ov[a, :, cs] = (res[a, :, cs].astype(F32) + v).astype(BF)
+        if n == 3:
+            out.start()
 
     own_ld = [pltpu.make_async_copy(r, res.at[k], s_ld.at[k]) for k, r in enumerate((x_ref, dy_ref))]
     for l in own_ld:
@@ -514,116 +555,125 @@
         pl.semaphore_signal(barrier, inc=1, device_id=d, device_id_type=MESH)
     pl.semaphore_wait(barrier, len(dev))
     own_ld[0].wait()
-    start_own(0)
-    start_w(0)
-    start_w(1)
     own_ld[1].wait()
     put = pltpu.make_async_copy(res, xd.at[:, pl.ds(pl.multiple_of(j * 64, 64), 64), :], s_put)
     put.start()
-    step_a(0)
-    step_b(0, 0)
-    step_a2(0)
-    step_w(0)
-    step_b(0, 3)
-    start_own(1)
-    step_b(0, 1)
-    step_b(0, 2)
-    step_w(1)
-    start_w(2)
-    put.wait()
-    for m in tail[0]:
-        m.wait_recv()
-    for idx in range(4):
-        ap(0, idx).start()
-    start_ab(0)
-    start_ab(1)
+    out = pltpu.make_async_copy(ov, yo, s_yo)
+    wpc(0)
+    wown(0)
+    ga(1)
+    wpc(2)
+    ga(0)
+    wown(1)
+    wpc(1)
+    gb0(0)
+    ga2(1)
+    ga2(0)
+    gb31(0)
+    gb2(0)
+    gf(0, 0)
+    wf(0)
+    gf(0, 3)
+    gf(0, 2)
+    wf(1)
+    gf(0, 1)
+    gb2(1)
+    gend(0)
+    wown(2)
+    sab(3)
+    wf2(0)
+    sab(0)
+    sab(2)
+    sab(1)
+    gb0(1)
     ab(0)
-    step_a(1)
-    start_ab(2)
     ab(1)
-    step_b(1, 0)
-    step_w2(0)
-    start_ab(3)
+    gb31(1)
     ab(2)
-    step_a2(1)
-    start_ab(4)
+    wf2(1)
+    sab(4)
     ab(3)
-    step_b(1, 3)
-    start_ab(5)
+    sab(6)
+    sab(5)
+    gf(1, 2)
+    gf(1, 0)
     ab(4)
-    step_w2(1)
-    start_ab(6)
+    sab(7)
     ab(5)
-    step_b(1, 1)
-    start_ab(7)
     ab(6)
+    gf(1, 1)
     ab(7)
-    step_b(1, 2)
-    h_pass()
-    bp[0].start()
-    uv_put.start()
-    step_w(2)
-    wait_wp(2, 0)
-    wait_wp(2, 1)
-    wl[0] = load_w(0)
+    gf(1, 3)
+    wf(2)
+    hp()
+    gend(1)
+    lw(0)
     p1(0)
-    for m in tail[1]:
-        m.wait_recv()
-    for idx in range(4):
-        ap(1, idx).start()
+    xl0(0)
     x1(0)
-    step_w2(2)
+    wf2(2)
+    x2(0)
     p2(0)
-    wait_wp(2, 3)
-    wait_wp(2, 2)
-    wl[1] = load_w(1)
+    x2o(0)
+    sg(1)
+    sg(2)
+    sg(0)
+    gg(0)
+    gg(1)
+    sg(3)
+    gg(2)
+    sg(4)
+    sg(6)
+    gg(3)
+    sg(5)
+    gg(4)
+    gg(5)
+    gg(6)
+    p2o(0)
+    lw(1)
+    sg(7)
     p4(0)
-    x2(0)
-    for t in range(3):
-        start_g(t)
-    for t in range(8):
-        gg(t)
-        if t + 3 < 8:
-            start_g(t + 3)
-        if t == 3:
-            p1(1)
-    f(0)
+    gg(7)
+    p1(1)
+    xl0(1)
     dadb()
-    bp[1].start()
-    bp[2].start()
-    wl[2] = load_w(2)
     x3(0)
     p2(1)
+    f(0)
+    p4(1)
+    p2o(1)
     x1(1)
-    hh2(0)
+    hh(0)
+    x2(1)
+    f(1)
+    lw(2)
+    x3(1)
+    xf(0)
     zf(0)
-    p4(1)
-    xf(0)
-    x2(1)
     p1(2)
-    f(1)
     p2(2)
-    wl[3] = load_w(3)
-    x3(1)
-    hh2(1)
+    hh(1)
+    x1(2)
+    p2o(2)
+    lw(3)
+    p4(2)
     zf(1)
-    p4(2)
-    x1(2)
+    x2o(1)
     p1(3)
+    xf(1)
+    p2(3)
+    x2(2)
+    x3(2)
+    p2o(3)
     f(2)
-    xf(1)
-    x2(2)
-    p2(3)
-    hh2(2)
+    p4(3)
+    hh(2)
+    f(3)
+    x2o(2)
+    hh(3)
     zf(2)
-    p4(3)
-    x3(2)
-    f(3)
-    hh2(3)
+    xf(2)
     zf(3)
-    out = pltpu.make_async_copy(ov, yo, s_yo)
-    out.start()
-    xf(2)
     for r in sends:
         r.wait_send()
     for t in range(6):
@@ -655,7 +705,7 @@
         scratch_shapes=[
             V((3, 2, 1024, 896), BF), V((2, 2, 1024, 512), BF), V((4, 2, 256, 896), F32), V((4, 256, 896), F32),
             V((2, 2, 896, 512), BF), V((2, 2, 1024, 896), BF), V((2, 5, 2, 256, 512), F32), V((2, 4, 256, 512), F32),
-            V((2, 2, 6, 64, 512), F32), V((2, 2, 128, 896), F32), V((2, 64, 4096), BF), V((2, 64, 4096), BF),
+            V((2, 4, 6, 64, 512), F32), V((2, 2, 128, 896), F32), V((2, 64, 4096), BF), V((2, 64, 4096), BF),
             dma((NSEND,)), dma((NSEND,)), dma((2,)), dma, dma((4, 3)),
             dma((2, 2)), dma((2, 4)), dma((2, 4)), dma((3,)), dma((3,)), dma((6,)), dma((3, 6)),
             dma((2, 6)), dma((2, 4, 6)), dma((2, 2, 6)), dma((2, 4, 6)), dma((2, 4)), dma((4,)), dma((2, 4)), dma, dma, dma, dma((2, 2)),
@@ -665,14 +715,46 @@
     )(x, dy, wg, wu, wd)[:2]
 
 
+def place_kernel(dw, yo, y, dx, dg, du, dd, bw, by, bt, s_in, s_out):
+    w_in = [pltpu.make_async_copy(dw.at[k], bw.at[k], s_in.at[k]) for k in range(3)]
+    y_in = [pltpu.make_async_copy(yo.at[k], by.at[k], s_in.at[3 + k]) for k in range(2)]
+    for l in w_in + y_in:
+        l.start()
+    outs = [pltpu.make_async_copy(bw.at[1], dg, s_out.at[1]), pltpu.make_async_copy(bw.at[2], du, s_out.at[2]),
+            pltpu.make_async_copy(by.at[0], y, s_out.at[3]), pltpu.make_async_copy(by.at[1], dx, s_out.at[4])]
+    w_in[0].wait()
+    for h in range(2):
+        bt[:, pl.ds(256 * h, 256)] = bw[0, pl.ds(256 * h, 256), :].T
+    o = pltpu.make_async_copy(bt, dd, s_out.at[0])
+    o.start()
+    for l, e in zip(w_in[1:] + y_in, outs):
+        l.wait()
+        e.start()
+    for e in [o] + outs:
+        e.wait()
+
+
+def place(dw, yo):
+    sd = jax.ShapeDtypeStruct
+    V = pltpu.VMEM
+    return pl.pallas_call(
+        place_kernel,
+        out_shape=(sd((64, 4096), BF), sd((64, 4096), BF), sd((512, 896), F32), sd((512, 896), F32), sd((896, 512), F32)),
+        in_specs=[HBM] * 2,
+        out_specs=(HBM,) * 5,
+        scratch_shapes=[V((3, 512, 896), F32), V((2, 64, 4096), BF), V((896, 512), F32),
+                        pltpu.SemaphoreType.DMA((5,)), pltpu.SemaphoreType.DMA((5,))],
+        compiler_params=pltpu.CompilerParams(vmem_limit_bytes=60 * 2**20),
+        name="place",
+    )(dw.reshape(3, 512, 896), yo)
+
+
 def solution(mesh):
     rows = P(("dp", "tp"), None)
     wsp = P("dp", "tp")
     dsp = P("tp", "dp")
 
     def local(x, w_gate, w_up, w_down, dy):
-        dw, yo = mlp(x, dy, w_gate, w_up, w_down)
-        dw = dw.reshape(3, 512, 896)
-        return yo[0], yo[1], dw[1], dw[2], dw[0].T
+        return place(*mlp(x, dy, w_gate, w_up, w_down))
 
     return jax.shard_map(local, mesh=mesh, in_specs=(rows, wsp, wsp, dsp, rows), out_specs=(rows, rows, wsp, wsp, dsp), check_vma=False)

time: 325 us -> 296 us (0.911)
  Pallas kernels: 313 us -> 295 us
  local copies, waits for them, and re-layouts: 8.73 us -> 0 us
    pallas_call x1, Pallas kernels: 313 us -> 290 us  [mlp(): pl.pallas_call(mlp_kernel, out_shape=(sd((3, 2, 256, 896), F32), sd((2, 6...]
    pallas_call x0 -> x1, Pallas kernels: none -> 4.89 us  [place(): pl.pallas_call(place_kernel, out_shape=(sd((64, 4096), BF), sd((64, 4096)...]
    slice x1 -> x0, local copies, waits for them, and re-layouts: 4.79 us -> none  [local(): return (yo[0], yo[1], dw[1], dw[2], dw[0].T)]
    squeeze x2 -> x0, local copies, waits for them, and re-layouts: 3.94 us -> none  [local(): return (yo[0], yo[1], dw[1], dw[2], dw[0].T)]
where the time goes in v4:
time: 296 us; the launch traced here: 295 us
  Pallas kernels  295 us (100%)
    pallas_call x1, Pallas kernels, mlp(): pl.pallas_call(mlp_kernel, out_shape=(sd((3, 2, 256, 896), F32), sd((2, 6...  290 us

profile of v4, /device:TPU:1, one launch (start us, length us, event | category | flops | bytes accessed | tf_op | source)
XLA Modules:
  0.0 295.4 jit_solution(14136492461721107926)
XLA Ops:
  0.6 289.7 %mlp.1 = (f32[3,2,256,896]{3,2,1,0:T(8,128)}, bf16[2,64,4096]{2,1,0:T(8,128)(2,1)}, bf16[2,1024,4096]{2,1,0:T(8,128)(2,1)}, bf16[4096,896]{1,0:T(8,128)(2,1)}, b...) custom-call(bf16[64,4096]{1,0:T(8,128)(2,1)} %x_ref.1, ...), custom_call_target="tpu_custom_call" | custom-call | tf_op jit(solution)/shard_map/mlp/pallas_call | solution.py:698
  290.3 4.9 %place.1 = (bf16[64,4096]{1,0:T(8,128)(2,1)}, bf16[64,4096]{1,0:T(8,128)(2,1)}, f32[512,896]{1,0:T(8,128)}, f32[512,896]{1,0:T(8,128)}, f32[896,512]{1,0:T(8,128)}) custom-call(f32[3,512,896]{2,1,0:T(8,128)} %bitcast.1, bf16[2,64,4096]{2,1,0:T(8,128)(2,1)} %get-tuple-element.8.yo), custom_call_target="tpu_custom_call" | custom-call | tf_op jit(solution)/shard_map/place/pallas_call | solution.py:740

commit v5 on v4

v5 whole, which is shorter than its diff:
```python
import jax
import jax.numpy as jnp
from jax import lax
from jax.experimental import pallas as pl
from jax.experimental.pallas import tpu as pltpu
from jax.sharding import PartitionSpec as P

MESH = pl.DeviceIdType.MESH
HBM = pl.BlockSpec(memory_space=pltpu.HBM)
NT = (((1,), (1,)), ((), ()))
TN = (((0,), (0,)), ((), ()))
F32 = jnp.float32
BF = jnp.bfloat16
TWO = range(2)
NSEND = 109
RING = 4
PAIR = 2
DM, TG, FB, CB, QB, RW, RH = 4096, 1024, 896, 512, 256, 64, 32
AX, AD = TWO
OWN, NEXT, OPP, PREV = range(4)
WG, WU, WL = range(3)
DOWN, GATE, UP = range(3)
Y0, Y1, X0, X1 = range(4)
B0, B1, B2, B3, B4, B5, B6, B7 = range(8)


def mlp_kernel(x_ref, dy_ref, wg_ref, wu_ref, wd_ref, dw, yo, xd, wgf, wuf, wdf, UV, XR, ZR, AP,
               B, A, XB, XS, WD, WX, ZB, ZS, Z2, US, res, ov,
               ssem, rsem, s_ld, s_put, s_c, s_a, s_ap, r_ap, s_b, r_b, s_xs, r_xs, s_zs, r_zs, s_2, r_2, s_w, s_xst, s_zst, s_xo, s_yo, s_uv, s_us):
    i = lax.axis_index("dp")
    j = lax.axis_index("tp")
    x, c, z, y = i // PAIR, i % PAIR, j // 4, j % RING
    xp, xm, xq, c1 = (x + 1) % RING, (x + 3) % RING, (x + 2) % RING, 1 - c
    dev = {
        "xp": {"dp": 2 * xp + c}, "xm": {"dp": 2 * xm + c}, "pc": {"dp": 2 * x + c1},
        "yp": {"tp": 4 * z + (y + 1) % RING}, "ym": {"tp": 4 * z + (y + 3) % RING},
        "zp": {"tp": 4 * ((z + 1) % RING) + y}, "zm": {"tp": 4 * ((z + 3) % RING) + y},
    }
    pos = ((z, y), (y, z))
    link = (("zp", "zm", "yp", "ym"), ("yp", "ym", "zp", "zm"))

    def remote(src, dst, ss, rs, to):
        return pltpu.make_async_remote_copy(src_ref=src, dst_ref=dst, send_sem=ss, recv_sem=rs, device_id=dev[to], device_id_type=MESH)

    def add(dst, src, n):
        def body(r, _):
            s = pl.ds(pl.multiple_of(r * RH, RH), RH)
            dst[s, :] = dst[s, :] + src[s, :]
            return 0
        lax.fori_loop(0, n // RH, body, 0)

    sends = []

    def send(src, dst, to):
        k = len(sends)
        r = remote(src, dst, ssem.at[k], rsem.at[k], to)
        r.start()
        sends.append(r)
        return r

    def wblk(k, xx, cc, half=None):
        ii = 2 * xx + cc
        if k < 2:
            r = (wgf, wuf)[k]
            if half is None:
                return r.at[pl.ds(pl.multiple_of(ii * CB, CB), CB), :]
            return r.at[pl.ds(pl.multiple_of(ii * CB + half * QB, QB), QB), :]
        if half is None:
            return wdf.at[ii]
        return wdf.at[ii, pl.ds(half * 448, 448), :]

    def rows(a, col, s, p, lo=0, n=RH):
        zz, yy = (p, s) if col == 0 else (s, p)
        return xd.at[a, pl.ds(pl.multiple_of((zz * 4 + yy) * RW + col * RH + lo, 16), n), :]

    GA = {}
    GA2 = {}
    GB = {}
    tail = {0: [], 1: []}

    def geo(col):
        sec, prim = pos[col]
        sp, sm, pp, pm = link[col]
        return prim, sec, pp, pm, sp, sm

    seen = set()

    def once(m):
        if id(m) not in seen:
            seen.add(id(m))
            m.wait_recv()

    def ga(a):
        for col in TWO:
            p, s, pp, pm, sp, sm = geo(col)
            src = res.at[a, pl.ds(col * RH, RH), :]
            GA[a, col] = [send(src, rows(a, col, p, s), to) for to in (pp, pm)]

    def gb0(a):
        for col in TWO:
            p, s, pp, pm, sp, sm = geo(col)
            src = res.at[a, pl.ds(col * RH, RH), :]
            GB[a, col, 0] = [send(src, rows(a, col, p, s), to) for to in (sp, sm)]

    def ga2(a):
        for col in TWO:
            p, s, pp, pm, sp, sm = geo(col)
            GA2[a, col] = []
            for fr, d, lo, fw in ((0, 3, 0, pp), (1, 1, 16, pm)):
                once(GA[a, col][fr])
                r = rows(a, col, (p + d) % RING, s, lo, 16)
                GA2[a, col].append(send(r, r, fw))

    def gb31(a):
        for col in TWO:
            p, s, pp, pm, sp, sm = geo(col)
            for d in (3, 1):
                r = rows(a, col, (p + d) % RING, s)
                GB[a, col, d] = [send(r, r, to) for to in (sp, sm)]

    def gb2(a):
        for col in TWO:
            p, s, pp, pm, sp, sm = geo(col)
            for m in GA2[a, col]:
                once(m)
            r = rows(a, col, (p + 2) % RING, s)
            GB[a, col, 2] = [send(r, r, to) for to in (sp, sm)]

    def gf(a, d):
        for col in TWO:
            p, s, pp, pm, sp, sm = geo(col)
            q = (p + d) % RING
            for fr, e, lo, fw in ((0, 3, 0, sp), (1, 1, 16, sm)):
                once(GB[a, col, d][fr])
                r = rows(a, col, q, (s + e) % RING, lo, 16)
                tail[a].append(send(r, r, fw))

    def gend(a):
        if a == 0:
            put.wait()
        for m in tail[a]:
            once(m)
        for idx in range(4):
            ap(a, idx).start()

    W1 = {}
    W2 = {}
    WP = {}
    w_in = (wg_ref, wu_ref, wd_ref)

    def wpc(k):
        WP[k, 0] = [send(w_in[k], wblk(k, x, c), "pc")]

    def wown(k):
        if k < WL:
            W1[k] = [[send(w_in[k], wblk(k, x, c), to)] for to in ("xp", "xm")]
        else:
            W1[k] = [[], []]
            for first in TWO:
                for fr, to in enumerate(("xp", "xm")):
                    half = (fr + first) % PAIR
                    W1[k][fr].append(send(wd_ref.at[pl.ds(half * 448, 448), :], wblk(k, x, c, half), to))

    def wf(k):
        W2[k] = []
        for fr, xx, d, half, fw in ((0, xm, 3, 0, "xp"), (1, xp, 1, 1, "xm")):
            once(W1[k][fr][0])
            r = wblk(k, xx, c, half)
            W2[k].append(send(r, r, fw))
            if k < 2:
                r = wblk(k, xx, c)
                WP[k, d] = [send(r, r, "pc")]

    def wfp():
        for fr, xx, d in ((0, xm, 3), (1, xp, 1)):
            once(W1[2][fr][1])
            r = wblk(2, xx, c)
            WP[2, d] = [send(r, r, "pc")]

    def wf2(k):
        WP[k, 2] = []
        for half in TWO:
            once(W2[k][half])
            r = wblk(k, xq, c, half)
            WP[k, 2].append(send(r, r, "pc"))

    def have(k, d, o):
        if o == 1:
            for m in WP[k, d]:
                once(m)
        elif d == 2:
            for m in W2[k]:
                once(m)
        elif d:
            for m in W1[k][d == NEXT]:
                once(m)

    xpos = {0: x, 1: xp, 2: xq, 3: xm}
    order = ((0, 0), (0, 1), (3, 0), (1, 0), (3, 1), (1, 1), (2, 0), (2, 1))

    def blk(t):
        d, o = order[t]
        return 2 * xpos[d] + (c if o == 0 else c1)

    def a_slot(t):
        s = t % RING
        return A.at[s // PAIR, s % PAIR]

    def ld_ab(t):
        d, o = order[t]
        s = t % RING
        ii = blk(t)
        out = [pltpu.make_async_copy(xd.at[0, :, pl.ds(pl.multiple_of(ii * CB, CB), CB)], a_slot(t), s_c.at[s, 0])]
        for k in TWO:
            src = w_in[k] if t == 0 else wblk(k, xpos[d], c if o == 0 else c1)
            out.append(pltpu.make_async_copy(src, WX.at[s % PAIR, k, pl.ds((s // PAIR) * CB, CB), :], s_c.at[s, 1 + k]))
        return out

    def sab(t):
        for k in TWO:
            have(k, *order[t])
        for l in ld_ab(t):
            l.start()

    def ab(t):
        for l in ld_ab(t):
            l.wait()
        s = t % RING

        def body(m, _):
            r = pl.ds(pl.multiple_of(m * QB, QB), QB)
            lhs = A[s // PAIR, s % PAIR, r, :]
            for k in TWO:
                v = jnp.dot(lhs, WX[s % PAIR, k, pl.ds((s // PAIR) * CB, CB), :], preferred_element_type=F32)
                if t == 0:
                    XB[2 * k + m // PAIR, m % PAIR] = v
                else:
                    XB[2 * k + m // PAIR, m % PAIR] += v
            return 0
        lax.fori_loop(0, 4, body, 0)

    def hp():
        def body(q, _):
            m = q // 8
            r = pl.ds(pl.multiple_of((q % 8) * RH, RH), RH)
            a = XB[m // PAIR, m % PAIR, r, :]
            b = XB[2 + m // PAIR, m % PAIR, r, :]
            sig = jax.nn.sigmoid(a)
            sa = a * sig
            XB[m // PAIR, m % PAIR, r, :] = b * sig * (1.0 + a * (1.0 - sig))
            XB[2 + m // PAIR, m % PAIR, r, :] = sa
            B[0, 0, pl.ds(pl.multiple_of(q * RH, RH), RH), :] = (sa * b).astype(BF)
            return 0
        lax.fori_loop(0, RH, body, 0)
        bp[0].start()
        uv_put.start()

    uv_put = pltpu.make_async_copy(XB, UV, s_uv)

    def ld_g(t):
        d, o = order[t]
        s = t % RING
        ii = blk(t)
        src = wd_ref if t == 0 else wdf.at[ii]
        return [pltpu.make_async_copy(xd.at[1, :, pl.ds(pl.multiple_of(ii * CB, CB), CB)], a_slot(t), s_c.at[s, 0]),
                pltpu.make_async_copy(src, WX.at[s % PAIR, s // PAIR, pl.ds(0, FB), pl.ds(0, CB)], s_c.at[s, 1])]

    def sg(t):
        have(2, *order[t])
        for l in ld_g(t):
            l.start()

    def gg(t):
        for l in ld_g(t):
            l.wait()
        s = t % RING

        def body(m, _):
            r = pl.ds(pl.multiple_of(m * QB, QB), QB)
            v = lax.dot_general(A[s // PAIR, s % PAIR, r, :], WX[s % PAIR, s // PAIR, pl.ds(0, FB), pl.ds(0, CB)], NT, preferred_element_type=F32)
            if t == 0:
                XS[m] = v
            else:
                XS[m] += v
            return 0
        lax.fori_loop(0, 4, body, 0)

    def us_load(q, k):
        m = q // PAIR
        return pltpu.make_async_copy(UV.at[2 * k + m // PAIR, m % PAIR, pl.ds(pl.multiple_of((q % PAIR) * 128, 128), 128), :], US.at[q % PAIR, k], s_us.at[q % PAIR, k])

    def dadb():
        for k in TWO:
            us_load(0, k).start()

        def body(q, _):
            @pl.when(q < 7)
            def _():
                for k in TWO:
                    us_load(q + 1, k).start()
            for k in TWO:
                us_load(q, k).wait()

            def inner(e, _):
                r = pl.ds(pl.multiple_of(e * RH, RH), RH)
                g = XS[q // PAIR, pl.ds(pl.multiple_of((q % PAIR) * 128 + e * RH, RH), RH), :]
                o = pl.ds(pl.multiple_of(q * 128 + e * RH, RH), RH)
                for k in TWO:
                    B[1 + k, 0, o, :] = (g * US[q % PAIR, k, r, :]).astype(BF)
                return 0
            lax.fori_loop(0, 4, inner, 0)
            return 0
        lax.fori_loop(0, 8, body, 0)
        bp[1].start()
        bp[2].start()

    def chunk(idx):
        return (x + 6 - idx) % RING

    bp = [remote(B.at[k, 0], B.at[k, 1], s_b.at[k], r_b.at[k], "pc") for k in range(3)]

    APM = {}

    def ap(arr, idx):
        if (arr, idx) not in APM:
            APM[arr, idx] = ap_(arr, idx)
        return APM[arr, idx]

    def ap_(arr, idx):
        return remote(xd.at[arr, :, pl.ds(pl.multiple_of(TG * chunk(idx) + CB * c1, CB), CB)], AP.at[arr, idx], s_ap.at[arr, idx], r_ap.at[arr, idx], "pc")

    seq = (0, 1, 3, 2)

    def load_a(k, n):
        arr = 1 - min(k, 1)
        idx = seq[n]
        return (pltpu.make_async_copy(xd.at[arr, :, pl.ds(pl.multiple_of(TG * chunk(idx) + CB * c, CB), CB)], A.at[n % PAIR, 0], s_a.at[n % PAIR, 0]),
                pltpu.make_async_copy(AP.at[arr, idx], A.at[n % PAIR, 1], s_a.at[n % PAIR, 1]))

    def start_a(k, n):
        once(ap(1 - min(k, 1), seq[n]))
        for l in load_a(k, n):
            l.start()

    def dot_x(k, n, split=False):
        slot = n % PAIR
        for l in load_a(k, n):
            l.wait()

        def body(m, _):
            cols = pl.ds(pl.multiple_of(m * QB, QB), QB)
            XB[seq[n], m] = (lax.dot_general(A[slot, 0, :, cols], B[k, 0], TN, preferred_element_type=F32)
                             + lax.dot_general(A[slot, 1, :, cols], B[k, 1], TN, preferred_element_type=F32))
            return 0

        if split:
            for m in TWO:
                body(m, 0)
                xmsg(k, m).start()
        else:
            lax.fori_loop(0, 2, body, 0)

    def xmsg(k, t):
        src = (XB.at[0, 0], XB.at[0, 1], XB.at[1, 1], XB.at[3, 0], XB.at[1, 0], XB.at[3, 1])[t]
        return remote(src, XR.at[k, t], s_xs.at[t], r_xs.at[k, t], ("xp", "xm")[t % PAIR])

    def xl0(k):
        start_a(k, 0)
        start_a(k, 1)

    def x1(k):
        bp[k].wait_recv()
        if k == 0:
            uv_put.wait()
        else:
            xmsg(k - 1, 0).wait_send()
            xmsg(k - 1, 1).wait_send()
        dot_x(k, 0, True)
        start_a(k, 2)

    def x2(k):
        if k > 0:
            for t in range(2, 6):
                xmsg(k - 1, t).wait_send()
        dot_x(k, 1)
        start_a(k, 3)
        xmsg(k, 2).start()
        dot_x(k, 2)
        if k == 1:
            start_a(2, 0)
        xmsg(k, 3).start()

    def x2o(k):
        if k > 0:
            xout(k - 1).wait()
        dot_x(k, 3)
        if k == 1:
            start_a(2, 1)

    def xstage(k, t, slot):
        return pltpu.make_async_copy(XR.at[k, t], XS.at[4 + slot], s_xst.at[slot])

    def x3(k):
        for t in TWO:
            xmsg(k, t).wait_recv()
            xstage(k, t, t).start()
        for t in TWO:
            xstage(k, t, t).wait()
            add(XB.at[(1, 3)[t], t], XS.at[4 + t], QB)
            xmsg(k, 4 + t).start()

    def xout(k):
        return pltpu.make_async_copy(XB.at[2], dw.at[k], s_xo)

    def xadd(k, ts):
        for h, t in enumerate(ts):
            xmsg(k, t).wait_recv()
            xstage(k, t, h).start()
        for h, t in enumerate(ts):
            xstage(k, t, h).wait()
            add(XB.at[2, h], XS.at[4 + h], QB)

    def xfa(k):
        xadd(k, (3, 2))
        if k == 2:
            xout(k).start()

    def xfb(k):
        xadd(k, (4, 5))
        xout(k).start()

    def pair(n, col):
        return ((0, 3), (1, 2))[col][n % PAIR]

    def lw(n):
        if n < 2:
            for col in TWO:
                have(2, pair(n, col), 0)
                have(2, pair(n, col), 1)
        out = []
        for col in TWO:
            d = pair(n, col)
            q = xpos[d]
            if n < 2:
                if d == 0:
                    out.append(pltpu.make_async_copy(wd_ref, WD.at[col, c], s_w.at[col, 0]))
                    out.append(pltpu.make_async_copy(wdf.at[2 * x + c1], WD.at[col, c1], s_w.at[col, 1]))
                else:
                    out.append(pltpu.make_async_copy(wdf.at[pl.ds(2 * q, 2)], WD.at[col], s_w.at[col, 0]))
            else:
                for k in TWO:
                    full = (wgf, wuf)[k]
                    if d == 0:
                        out.append(pltpu.make_async_copy(w_in[k], WX.at[col, k, pl.ds(pl.multiple_of(CB * c, CB), CB), :], s_w.at[col, 2 * k]))
                        out.append(pltpu.make_async_copy(full.at[pl.ds(pl.multiple_of(TG * x + CB * c1, CB), CB), :],
                                                         WX.at[col, k, pl.ds(pl.multiple_of(CB * c1, CB), CB), :], s_w.at[col, 2 * k + 1]))
                    else:
                        out.append(pltpu.make_async_copy(full.at[pl.ds(pl.multiple_of(TG * q, TG), TG), :], WX.at[col, k], s_w.at[col, 2 * k]))
        for o in out:
            o.start()
        wl[n] = out

    wl = {}

    def dots_z(n, lo, m):

        def body(q, _):
            col = q // m
            idx = lo + 2 * (q % m)
            p = z + col * (y - z)
            ch = (p + 6 - idx) % RING
            s1 = QB - 192 * col
            s2 = RW + 192 * col
            own = (idx // PAIR) * (1 - idx // 3)
            slot = idx + own * 2 * (n % PAIR)

            def lhs(k):
                return jnp.concatenate([B[k, 0, pl.ds(pl.multiple_of(ch * s1 + g * s2, RW), RW), :] for g in range(4)], axis=0)

            if n < 2:
                l = lhs(0)
                for h in TWO:
                    ZB[col, slot, h] = jnp.dot(l, WD[col, h], preferred_element_type=F32)
            else:
                l = lhs(1)
                u = lhs(2)
                for h in TWO:
                    r = pl.ds(CB * h, CB)
                    ZB[col, slot, h] = (lax.dot_general(l, WX[col, 0, r, :], NT, preferred_element_type=F32)
                                        + lax.dot_general(u, WX[col, 1, r, :], NT, preferred_element_type=F32))
            return 0
        lax.fori_loop(0, 2 * m, body, 0)

    def zmsg(n, col, t):
        src = ((0, 0), (0, 1), (1, 1), (3, 0), (1, 0), (3, 1))[t]
        return remote(ZB.at[col, src[0], src[1]], ZR.at[col, n, t], s_zs.at[col, t], r_zs.at[col, n, t], link[col][t % PAIR])

    def own(n, col, h):
        return ZB.at[col, 2 + 2 * (n % PAIR), h]

    def sub(n, col, h, d):
        s = (pos[col][1] + d) % RING
        return ZB.at[col, 2 + 2 * (n % PAIR), h, pl.ds(pl.multiple_of(s * RW, RW), RW), :]

    def msg2(n, col, t):
        h, d = ((0, 2), (1, 2), (1, 1), (0, 3), (0, 1), (1, 3))[t]
        return remote(sub(n, col, h, d), Z2.at[col, n, t], s_2.at[col, n % PAIR, t], r_2.at[col, n, t], link[col][2 + t % PAIR])

    def p1(n):
        for l in wl[n]:
            l.wait()
        if n > 0:
            for col in TWO:
                for t in TWO:
                    zmsg(n - 1, col, t).wait_send()
        dots_z(n, 0, 1)
        for t in TWO:
            for col in TWO:
                zmsg(n, col, t).start()

    def p2(n):
        if n > 0:
            for col in TWO:
                for t in range(2, 6):
                    zmsg(n - 1, col, t).wait_send()
        dots_z(n, 1, 2)
        for t in range(2, 4):
            for col in TWO:
                zmsg(n, col, t).start()

    def p2o(n):
        if n > 1:
            for col in TWO:
                for t in range(6):
                    msg2(n - 2, col, t).wait_send()
        dots_z(n, 2, 1)

    def zstage(n, col, t, slot):
        return pltpu.make_async_copy(ZR.at[col, n, t], ZS.at[col, slot], s_zst.at[col, slot])

    def p4(n):
        for t in TWO:
            for col in TWO:
                zmsg(n, col, t).wait_recv()
                zstage(n, col, t, t).start()
        for t in TWO:
            for col in TWO:
                zstage(n, col, t, t).wait()
                add(ZB.at[col, (1, 3)[t], t], ZS.at[col, t], QB)
                zmsg(n, col, 4 + t).start()

    def zadd(n, ts):
        for h, t in enumerate(ts):
            for col in TWO:
                zmsg(n, col, t).wait_recv()
                zstage(n, col, t, h).start()
        for h, t in enumerate(ts):
            for col in TWO:
                zstage(n, col, t, h).wait()
                add(own(n, col, h), ZS.at[col, h], QB)

    def fa(n):
        zadd(n, (3, 2))

    def fb(n):
        zadd(n, (4, 5))
        for t in range(4):
            for col in TWO:
                msg2(n, col, t).start()

    def hh(n):
        for t in TWO:
            for col in TWO:
                msg2(n, col, t).wait_recv()
                add(sub(n, col, t, (1, 3)[t]), Z2.at[col, n, t], RW)
                msg2(n, col, 4 + t).start()

    def zf(n):
        a = n // PAIR
        for col in TWO:
            q = xpos[pair(n, col)]
            for h, ts in ((0, (3, 4)), (1, (2, 5))):
                for t in ts:
                    msg2(n, col, t).wait_recv()
                cs = pl.ds(pl.multiple_of(TG * q + CB * h, CB), CB)
                v = sub(n, col, h, 0)[...] + Z2[col, n, ts[0]] + Z2[col, n, ts[1]]
                ov[a, :, cs] = (res[a, :, cs].astype(F32) + v).astype(BF)
        if n == 3:
            out.start()

    own_ld = [pltpu.make_async_copy(r, res.at[k], s_ld.at[k]) for k, r in enumerate((x_ref, dy_ref))]
    for l in own_ld:
        l.start()
    barrier = pltpu.get_barrier_semaphore()
    for d in dev.values():
        pl.semaphore_signal(barrier, inc=1, device_id=d, device_id_type=MESH)
    pl.semaphore_wait(barrier, len(dev))
    own_ld[0].wait()
    own_ld[1].wait()
    put = pltpu.make_async_copy(res, xd.at[:, pl.ds(pl.multiple_of(j * RW, RW), RW), :], s_put)
    put.start()
    out = pltpu.make_async_copy(ov, yo, s_yo)
    gb0(AX)
    ga(AX)
    wown(WU)
    wpc(WG)
    gf(AX, OWN)
    ga2(AX)
    gb31(AX)
    wown(WG)
    gb2(AX)
    gf(AX, PREV)
    gf(AX, NEXT)
    gf(AX, OPP)
    ga(AD)
    wf(WU)
    gb0(AD)
    wpc(WU)
    gend(AX)
    wf(WG)
    sab(B0)
    sab(B1)
    sab(B3)
    ga2(AD)
    ab(B0)
    gb31(AD)
    gf(AD, OWN)
    wf2(WU)
    sab(B2)
    ab(B1)
    gb2(AD)
    wown(WL)
    sab(B4)
    ab(B2)
    sab(B5)
    ab(B3)
    wf2(WG)
    ab(B4)
    sab(B6)
    ab(B5)
    gf(AD, NEXT)
    gf(AD, PREV)
    sab(B7)
    ab(B6)
    wpc(WL)
    ab(B7)
    hp()
    wf(WL)
    gf(AD, OPP)
    wfp()
    gend(AD)
    xl0(DOWN)
    lw(Y0)
    x1(DOWN)
    x2(DOWN)
    p1(Y0)
    p2(Y0)
    x2o(DOWN)
    wf2(WL)
    sg(B3)
    sg(B2)
    sg(B1)
    sg(B0)
    p2o(Y0)
    lw(Y1)
    gg(B0)
    gg(B1)
    p4(Y0)
    sg(B5)
    gg(B2)
    sg(B6)
    gg(B3)
    sg(B4)
    sg(B7)
    x3(DOWN)
    gg(B4)
    gg(B5)
    gg(B6)
    gg(B7)
    p1(Y1)
    dadb()
    xl0(GATE)
    p2(Y1)
    x1(GATE)
    fa(Y0)
    p2o(Y1)
    lw(X0)
    p4(Y1)
    fb(Y0)
    p1(X0)
    x2(GATE)
    fa(Y1)
    xfa(DOWN)
    x3(GATE)
    hh(Y0)
    fb(Y1)
    xfb(DOWN)
    p2(X0)
    zf(Y0)
    hh(Y1)
    x2o(GATE)
    p2o(X0)
    p4(X0)
    lw(X1)
    xfa(GATE)
    x1(UP)
    zf(Y1)
    p1(X1)
    fa(X0)
    x2(UP)
    p2(X1)
    xfb(GATE)
    p4(X1)
    fb(X0)
    p2o(X1)
    x3(UP)
    x2o(UP)
    fa(X1)
    fb(X1)
    hh(X0)
    hh(X1)
    xfa(UP)
    zf(X0)
    zf(X1)
    for r in sends:
        r.wait_send()
    for t in range(4, 6):
        xmsg(2, t).wait_recv()
    for t in range(6):
        xmsg(2, t).wait_send()
        for col in TWO:
            zmsg(3, col, t).wait_send()
            msg2(2, col, t).wait_send()
            msg2(3, col, t).wait_send()
    for k in range(3):
        bp[k].wait_send()
    for arr in TWO:
        for idx in range(4):
            ap(arr, idx).wait_send()
    xout(2).wait()
    out.wait()


def mlp(x, dy, wg, wu, wd):
    sd = jax.ShapeDtypeStruct
    dma = pltpu.SemaphoreType.DMA
    V = pltpu.VMEM
    o = pl.pallas_call(
        mlp_kernel,
        out_shape=(sd((3, 2, QB, FB), F32), sd((2, RW, DM), BF),
                   sd((2, TG, DM), BF), sd((DM, FB), BF), sd((DM, FB), BF), sd((8, FB, CB), BF), sd((4, 2, QB, FB), F32),
                   sd((3, 6, QB, FB), F32), sd((2, 4, 6, QB, CB), F32), sd((2, 4, TG, CB), BF)),
        in_specs=[HBM] * 5,
        out_specs=(HBM,) * 10,
        scratch_shapes=[
            V((3, 2, TG, FB), BF), V((2, 2, TG, CB), BF), V((4, 2, QB, FB), F32), V((6, QB, FB), F32),
            V((2, 2, FB, CB), BF), V((2, 2, TG, FB), BF), V((2, 5, 2, QB, CB), F32), V((2, 2, QB, CB), F32),
            V((2, 4, 6, RW, CB), F32), V((2, 2, 128, FB), F32), V((2, RW, DM), BF), V((2, RW, DM), BF),
            dma((NSEND,)), dma((NSEND,)), dma((2,)), dma, dma((4, 3)),
            dma((2, 2)), dma((2, 4)), dma((2, 4)), dma((3,)), dma((3,)), dma((6,)), dma((3, 6)),
            dma((2, 6)), dma((2, 4, 6)), dma((2, 2, 6)), dma((2, 4, 6)), dma((2, 4)), dma((4,)), dma((2, 4)), dma, dma, dma, dma((2, 2)),
        ],
        compiler_params=pltpu.CompilerParams(collective_id=1, has_side_effects=True, vmem_limit_bytes=67043328),
        name="mlp",
    )(x, dy, wg, wu, wd)
    return o[0], o[1], o[7]


def place_kernel(dw, yo, xr, y, dx, dg, du, dd, bw, by, bt, br, s_in, s_out):
    w_in = [pltpu.make_async_copy(dw.at[k], bw.at[k], s_in.at[k]) for k in range(3)]
    y_in = [pltpu.make_async_copy(yo.at[k], by.at[k], s_in.at[3 + k]) for k in TWO]
    r_in = pltpu.make_async_copy(xr.at[2, pl.ds(4, 2)], br, s_in.at[5])
    for l in w_in + [r_in] + y_in:
        l.start()
    w_out = [pltpu.make_async_copy(bt, dd, s_out.at[0]), pltpu.make_async_copy(bw.at[1], dg, s_out.at[1]), pltpu.make_async_copy(bw.at[2], du, s_out.at[2])]
    y_out = [pltpu.make_async_copy(by.at[0], y, s_out.at[3]), pltpu.make_async_copy(by.at[1], dx, s_out.at[4])]
    w_in[0].wait()
    for h in TWO:
        bt[:, pl.ds(QB * h, QB)] = bw[0, pl.ds(QB * h, QB), :].T
    w_out[0].start()
    w_in[1].wait()
    w_out[1].start()
    w_in[2].wait()
    r_in.wait()
    for h in TWO:
        bw[2, pl.ds(QB * h, QB), :] += br[h]
    w_out[2].start()
    for l, e in zip(y_in, y_out):
        l.wait()
        e.start()
    for e in w_out + y_out:
        e.wait()


def place(dw, yo, xr):
    sd = jax.ShapeDtypeStruct
    V = pltpu.VMEM
    return pl.pallas_call(
        place_kernel,
        out_shape=(sd((RW, DM), BF), sd((RW, DM), BF), sd((CB, FB), F32), sd((CB, FB), F32), sd((FB, CB), F32)),
        in_specs=[HBM] * 3,
        out_specs=(HBM,) * 5,
        scratch_shapes=[V((3, CB, FB), F32), V((2, RW, DM), BF), V((FB, CB), F32), V((2, QB, FB), F32),
                        pltpu.SemaphoreType.DMA((6,)), pltpu.SemaphoreType.DMA((5,))],
        compiler_params=pltpu.CompilerParams(vmem_limit_bytes=60 * 2**20),
        name="place",
    )(dw.reshape(3, CB, FB), yo, xr)


def solution(mesh):
    rows = P(("dp", "tp"), None)
    wsp = P("dp", "tp")
    dsp = P("tp", "dp")

    def local(x, w_gate, w_up, w_down, dy):
        return place(*mlp(x, dy, w_gate, w_up, w_down))

    return jax.shard_map(local, mesh=mesh, in_specs=(rows, wsp, wsp, dsp, rows), out_specs=(rows, rows, wsp, wsp, dsp), check_vma=False)
```

time: 296 us -> 290 us (0.980)
  Pallas kernels: 295 us -> 288 us
    pallas_call x2, Pallas kernels: 295 us -> 288 us  [the longest x1 283 us: mlp(): pl.pallas_call(mlp_kernel, out_shape=(sd((3, 2, QB, FB), F32), sd((2, RW,...]
where the time goes in v5:
time: 290 us; the launch traced here: 289 us
  Pallas kernels  288 us (99%)
    pallas_call x1, Pallas kernels, mlp(): pl.pallas_call(mlp_kernel, out_shape=(sd((3, 2, QB, FB), F32), sd((2, RW,...  283 us

profile of v5, /device:TPU:1, one launch (start us, length us, event | category | flops | bytes accessed | tf_op | source)
XLA Modules:
  0.0 288.9 jit_solution(11656665208680413467)
XLA Ops:
  0.6 282.8 %mlp.1 = (f32[3,2,256,896]{3,2,1,0:T(8,128)}, bf16[2,64,4096]{2,1,0:T(8,128)(2,1)}, bf16[2,1024,4096]{2,1,0:T(8,128)(2,1)}, bf16[4096,896]{1,0:T(8,128)(2,1)}, b...) custom-call(bf16[64,4096]{1,0:T(8,128)(2,1)} %x_ref.1, ...), custom_call_target="tpu_custom_call" | custom-call | tf_op jit(solution)/shard_map/mlp/pallas_call | solution.py:748
  283.4 5.3 %place.1 = (bf16[64,4096]{1,0:T(8,128)(2,1)}, bf16[64,4096]{1,0:T(8,128)(2,1)}, f32[512,896]{1,0:T(8,128)}, f32[512,896]{1,0:T(8,128)}, f32[896,512]{1,0:T(8,128)}) custom-call(f32[3,512,896]{2,1,0:T(8,128)} %bitcast.1, bf16[2,64,4096]{2,1,0:T(8,128)(2,1)} %get-tuple-element.9.yo, f32[3,6,256,896]{3,2,1,0:T(8,128)} %get-tuple-element.10.xr), custom_call_target="tpu_custom_call" | custom-call | tf_op jit(solution)/shard_map/place/pallas_call | solution.py:798

commit v6 on v5

--- a/solution.py
+++ b/solution.py
@@ -12,11 +12,11 @@
 F32 = jnp.float32
 BF = jnp.bfloat16
 TWO = range(2)
-NSEND = 109
+NSEND = 149
 RING = 4
 PAIR = 2
 DM, TG, FB, CB, QB, RW, RH = 4096, 1024, 896, 512, 256, 64, 32
-AX, AD = TWO
+AX, AD, AE = range(3)
 OWN, NEXT, OPP, PREV = range(4)
 WG, WU, WL = range(3)
 DOWN, GATE, UP = range(3)
@@ -69,14 +69,22 @@
             return wdf.at[ii]
         return wdf.at[ii, pl.ds(half * 448, 448), :]
 
+    ahead = xq // PAIR
+
+    def cols(a):
+        if a == AX:
+            return slice(None)
+        h = ahead if a == AD else 1 - ahead
+        return pl.ds(pl.multiple_of(h * (DM // PAIR), DM // PAIR), DM // PAIR)
+
     def rows(a, col, s, p, lo=0, n=RH):
         zz, yy = (p, s) if col == 0 else (s, p)
-        return xd.at[a, pl.ds(pl.multiple_of((zz * 4 + yy) * RW + col * RH + lo, 16), n), :]
+        return xd.at[min(a, AD), pl.ds(pl.multiple_of((zz * 4 + yy) * RW + col * RH + lo, 16), n), cols(a)]
 
     GA = {}
     GA2 = {}
     GB = {}
-    tail = {0: [], 1: []}
+    tail = ([], [], [])
 
     def geo(col):
         sec, prim = pos[col]
@@ -93,13 +101,13 @@
     def ga(a):
         for col in TWO:
             p, s, pp, pm, sp, sm = geo(col)
-            src = res.at[a, pl.ds(col * RH, RH), :]
+            src = res.at[min(a, AD), pl.ds(col * RH, RH), cols(a)]
             GA[a, col] = [send(src, rows(a, col, p, s), to) for to in (pp, pm)]
 
     def gb0(a):
         for col in TWO:
             p, s, pp, pm, sp, sm = geo(col)
-            src = res.at[a, pl.ds(col * RH, RH), :]
+            src = res.at[min(a, AD), pl.ds(col * RH, RH), cols(a)]
             GB[a, col, 0] = [send(src, rows(a, col, p, s), to) for to in (sp, sm)]
 
     def ga2(a):
@@ -140,8 +148,8 @@
             put.wait()
         for m in tail[a]:
             once(m)
-        for idx in range(4):
-            ap(a, idx).start()
+        for arr, idx in (((AX, 0), (AX, 1), (AX, 3), (AX, 2)), ((AD, 0),), ((AD, 1), (AD, 3), (AD, 2)))[a]:
+            ap(arr, idx).start()
 
     W1 = {}
     W2 = {}
@@ -364,9 +372,8 @@
         src = (XB.at[0, 0], XB.at[0, 1], XB.at[1, 1], XB.at[3, 0], XB.at[1, 0], XB.at[3, 1])[t]
         return remote(src, XR.at[k, t], s_xs.at[t], r_xs.at[k, t], ("xp", "xm")[t % PAIR])
 
-    def xl0(k):
-        start_a(k, 0)
-        start_a(k, 1)
+    def xl(k, n):
+        start_a(k, n)
 
     def x1(k):
         bp[k].wait_recv()
@@ -585,143 +592,160 @@
                 cs = pl.ds(pl.multiple_of(TG * q + CB * h, CB), CB)
                 v = sub(n, col, h, 0)[...] + Z2[col, n, ts[0]] + Z2[col, n, ts[1]]
                 ov[a, :, cs] = (res[a, :, cs].astype(F32) + v).astype(BF)
-        if n == 3:
+        done.append(n)
+        if len(done) == RING:
             out.start()
+
+    def enter():
+        for d in dev.values():
+            pl.semaphore_signal(barrier, inc=1, device_id=d, device_id_type=MESH)
+        pl.semaphore_wait(barrier, len(dev))
 
     own_ld = [pltpu.make_async_copy(r, res.at[k], s_ld.at[k]) for k, r in enumerate((x_ref, dy_ref))]
     for l in own_ld:
         l.start()
     barrier = pltpu.get_barrier_semaphore()
-    for d in dev.values():
-        pl.semaphore_signal(barrier, inc=1, device_id=d, device_id_type=MESH)
-    pl.semaphore_wait(barrier, len(dev))
+    enter()
     own_ld[0].wait()
     own_ld[1].wait()
     put = pltpu.make_async_copy(res, xd.at[:, pl.ds(pl.multiple_of(j * RW, RW), RW), :], s_put)
     put.start()
     out = pltpu.make_async_copy(ov, yo, s_yo)
-    gb0(AX)
+    done = []
+    wpc(WG)
     ga(AX)
     wown(WU)
-    wpc(WG)
-    gf(AX, OWN)
+    gb0(AX)
+    ga(AD)
     ga2(AX)
     gb31(AX)
     wown(WG)
     gb2(AX)
+    ga2(AD)
+    gf(AX, OWN)
+    gf(AX, OPP)
+    gf(AX, NEXT)
     gf(AX, PREV)
-    gf(AX, NEXT)
-    gf(AX, OPP)
-    ga(AD)
     wf(WU)
+    wpc(WU)
+    wpc(WL)
+    wf(WG)
+    ga(AE)
+    gb31(AD)
+    gend(AX)
+    sab(B1)
+    sab(B2)
+    gb2(AD)
+    sab(B0)
+    ab(B0)
+    sab(B3)
+    wown(WL)
+    wf2(WU)
+    gb0(AE)
+    ab(B1)
     gb0(AD)
-    wpc(WU)
-    gend(AX)
-    wf(WG)
-    sab(B0)
-    sab(B1)
-    sab(B3)
-    ga2(AD)
-    ab(B0)
-    gb31(AD)
-    gf(AD, OWN)
-    wf2(WU)
-    sab(B2)
-    ab(B1)
-    gb2(AD)
-    wown(WL)
+    gf(AD, NEXT)
+    sab(B5)
+    ab(B2)
+    ga2(AE)
+    gf(AD, OPP)
     sab(B4)
-    ab(B2)
-    sab(B5)
     ab(B3)
     wf2(WG)
     ab(B4)
+    sab(B7)
     sab(B6)
+    gf(AD, PREV)
+    gf(AD, OWN)
     ab(B5)
-    gf(AD, NEXT)
-    gf(AD, PREV)
-    sab(B7)
+    gb31(AE)
     ab(B6)
-    wpc(WL)
+    gend(AD)
+    gb2(AE)
+    gf(AE, OWN)
+    wf(WL)
     ab(B7)
     hp()
-    wf(WL)
-    gf(AD, OPP)
+    gf(AE, PREV)
+    gf(AE, NEXT)
+    xl(DOWN, 0)
     wfp()
-    gend(AD)
-    xl0(DOWN)
+    gf(AE, OPP)
+    gend(AE)
     lw(Y0)
     x1(DOWN)
+    xl(DOWN, 1)
+    p1(Y0)
     x2(DOWN)
-    p1(Y0)
+    x2o(DOWN)
+    sg(B3)
+    sg(B1)
+    wf2(WL)
+    sg(B0)
     p2(Y0)
-    x2o(DOWN)
-    wf2(WL)
-    sg(B3)
+    gg(B0)
     sg(B2)
-    sg(B1)
-    sg(B0)
+    gg(B1)
+    p4(Y0)
     p2o(Y0)
     lw(Y1)
-    gg(B0)
-    gg(B1)
-    p4(Y0)
+    sg(B4)
     sg(B5)
     gg(B2)
+    gg(B3)
+    p1(Y1)
     sg(B6)
-    gg(B3)
-    sg(B4)
     sg(B7)
+    gg(B4)
     x3(DOWN)
-    gg(B4)
     gg(B5)
     gg(B6)
     gg(B7)
-    p1(Y1)
+    xl(GATE, 0)
+    lw(X0)
     dadb()
-    xl0(GATE)
+    xl(GATE, 1)
     p2(Y1)
+    fa(Y0)
     x1(GATE)
-    fa(Y0)
+    fb(Y0)
     p2o(Y1)
-    lw(X0)
+    hh(Y0)
     p4(Y1)
-    fb(Y0)
+    x2(GATE)
     p1(X0)
-    x2(GATE)
     fa(Y1)
+    fb(Y1)
+    x3(GATE)
+    p2(X0)
+    hh(Y1)
+    zf(Y0)
+    p2o(X0)
+    x1(UP)
+    p4(X0)
     xfa(DOWN)
-    x3(GATE)
-    hh(Y0)
-    fb(Y1)
     xfb(DOWN)
-    p2(X0)
-    zf(Y0)
-    hh(Y1)
+    lw(X1)
     x2o(GATE)
-    p2o(X0)
-    p4(X0)
-    lw(X1)
     xfa(GATE)
-    x1(UP)
+    p1(X1)
+    p2(X1)
+    x2(UP)
     zf(Y1)
-    p1(X1)
     fa(X0)
-    x2(UP)
-    p2(X1)
-    xfb(GATE)
     p4(X1)
+    x3(UP)
     fb(X0)
     p2o(X1)
-    x3(UP)
-    x2o(UP)
     fa(X1)
     fb(X1)
+    xfb(GATE)
     hh(X0)
+    x2o(UP)
     hh(X1)
     xfa(UP)
+    zf(X1)
     zf(X0)
-    zf(X1)
     for r in sends:
         r.wait_send()
     for t in range(4, 6):

time: 290 us -> 285 us (0.983)
  Pallas kernels: 288 us -> 283 us
    pallas_call x1, Pallas kernels: 283 us -> 278 us  [mlp(): pl.pallas_call(mlp_kernel, out_shape=(sd((3, 2, QB, FB), F32), sd((2, RW,...]
where the time goes in v6:
time: 285 us; the launch traced here: 284 us
  Pallas kernels  283 us (99%)
    pallas_call x1, Pallas kernels, mlp(): pl.pallas_call(mlp_kernel, out_shape=(sd((3, 2, QB, FB), F32), sd((2, RW,...  278 us

profile of v6, /device:TPU:1, one launch (start us, length us, event | category | flops | bytes accessed | tf_op | source)
XLA Modules:
  0.0 283.8 jit_solution(9827084766775089298)
XLA Ops:
  0.6 277.7 %mlp.1 = (f32[3,2,256,896]{3,2,1,0:T(8,128)}, bf16[2,64,4096]{2,1,0:T(8,128)(2,1)}, bf16[2,1024,4096]{2,1,0:T(8,128)(2,1)}, bf16[4096,896]{1,0:T(8,128)(2,1)}, b...) custom-call(bf16[64,4096]{1,0:T(8,128)(2,1)} %x_ref.1, ...), custom_call_target="tpu_custom_call" | custom-call | tf_op jit(solution)/shard_map/mlp/pallas_call | solution.py:772
  278.4 5.3 %place.1 = (bf16[64,4096]{1,0:T(8,128)(2,1)}, bf16[64,4096]{1,0:T(8,128)(2,1)}, f32[512,896]{1,0:T(8,128)}, f32[512,896]{1,0:T(8,128)}, f32[896,512]{1,0:T(8,128)}) custom-call(f32[3,512,896]{2,1,0:T(8,128)} %bitcast.1, bf16[2,64,4096]{2,1,0:T(8,128)(2,1)} %get-tuple-element.9.yo, f32[3,6,256,896]{3,2,1,0:T(8,128)} %get-tuple-element.10.xr), custom_call_target="tpu_custom_call" | custom-call | tf_op jit(solution)/shard_map/place/pallas_call | solution.py:822

commit v7 on v6

v7 whole, which is shorter than its diff:
```python
import jax
import jax.numpy as jnp
from jax import lax
from jax.experimental import pallas as pl
from jax.experimental.pallas import tpu as pltpu
from jax.sharding import PartitionSpec as P

MESH = pl.DeviceIdType.MESH
HBM = pl.BlockSpec(memory_space=pltpu.HBM)
NT = (((1,), (1,)), ((), ()))
TN = (((0,), (0,)), ((), ()))
F32 = jnp.float32
BF = jnp.bfloat16
TWO = range(2)
RING = 4
PAIR = 2
HB = 448
FOUR = 128
DM, TG, FB, CB, QB, RW, RH = 4096, 1024, 896, 512, 256, 64, 32
AX, AD, AE = range(3)
OWN, NEXT, OPP, PREV = range(4)
WG, WU, WL = range(3)
DOWN, GATE, UP = range(3)
Y0, Y1, X0, X1 = range(4)
A0, A1, A2 = range(3)
B0, B1, B2, B3, B4, B5, B6, B7 = range(8)


def mlp_kernel(x_ref, dy_ref, wg_ref, wu_ref, wd_ref, dw, yo, xd, wgf, wuf, wdf, UV, XR, ZR, AP,
               B, A, XB, XS, WD, WX, ZB, ZS, Z2, res, ov,
               s_g, r_g, s_v, r_v, s_ap, r_ap, s_b, r_b, s_xs, r_xs, s_zs, r_zs, s_2, r_2, s_c, s_a, s_w, s_us, s_one):
    i = lax.axis_index("dp")
    j = lax.axis_index("tp")
    x, c, z, y = i // PAIR, i % PAIR, j // 4, j % RING
    xp, xm, xq, c1 = (x + 1) % RING, (x + 3) % RING, (x + 2) % RING, 1 - c
    dev = {
        "xp": {"dp": 2 * xp + c}, "xm": {"dp": 2 * xm + c}, "pc": {"dp": 2 * x + c1},
        "yp": {"tp": 4 * z + (y + 1) % RING}, "ym": {"tp": 4 * z + (y + 3) % RING},
        "zp": {"tp": 4 * ((z + 1) % RING) + y}, "zm": {"tp": 4 * ((z + 3) % RING) + y},
    }
    pos = ((z, y), (y, z))
    link = (("zp", "zm", "yp", "ym"), ("yp", "ym", "zp", "zm"))

    def remote(src, dst, ss, rs, to):
        return pltpu.make_async_remote_copy(src_ref=src, dst_ref=dst, send_sem=ss, recv_sem=rs, device_id=dev[to], device_id_type=MESH)

    def wait(ref, sem):
        pltpu.make_async_copy(ref, ref, sem).wait()

    def add(dst, src, n):
        def body(r, _):
            s = pl.ds(pl.multiple_of(r * RH, RH), RH)
            dst[s, :] = dst[s, :] + src[s, :]
            return 0
        lax.fori_loop(0, n // RH, body, 0)

    def send(src, dst, to, ss, rs):
        remote(src, dst, ss, rs, to).start()

    def wblk(k, xx, cc, half=None):
        ii = 2 * xx + cc
        if k < 2:
            r = (wgf, wuf)[k]
            if half is None:
                return r.at[pl.ds(pl.multiple_of(ii * CB, CB), CB), :]
            return r.at[pl.ds(pl.multiple_of(ii * CB + half * QB, QB), QB), :]
        if half is None:
            return wdf.at[ii]
        return wdf.at[ii, pl.ds(half * HB, HB), :]

    ahead = xq // PAIR

    def cols(a):
        if a == AX:
            return slice(None)
        h = ahead if a == AD else 1 - ahead
        return pl.ds(pl.multiple_of(h * (DM // PAIR), DM // PAIR), DM // PAIR)

    def rows(a, col, s, p, lo=0, n=RH):
        zz, yy = (p, s) if col == 0 else (s, p)
        return xd.at[min(a, AD), pl.ds(pl.multiple_of((zz * 4 + yy) * RW + col * RH + lo, 16), n), cols(a)]

    def geo(col):
        sec, prim = pos[col]
        sp, sm, pp, pm = link[col]
        return prim, sec, pp, pm, sp, sm

    def some(a, n):
        return xd.at[min(a, AD), pl.ds(0, n), cols(a)]

    FIRST, ON, LAST = range(4, 7)

    def ga(a):
        for col in TWO:
            p, s, pp, pm, sp, sm = geo(col)
            src = res.at[min(a, AD), pl.ds(col * RH, RH), cols(a)]
            for to in (pp, pm):
                send(src, rows(a, col, p, s), to, s_g.at[a], r_g.at[a, FIRST])

    def gb0(a):
        for col in TWO:
            p, s, pp, pm, sp, sm = geo(col)
            src = res.at[min(a, AD), pl.ds(col * RH, RH), cols(a)]
            for to in (sp, sm):
                send(src, rows(a, col, p, s), to, s_g.at[a], r_g.at[a, OWN])

    def ga2(a):
        wait(some(a, FOUR), r_g.at[a, FIRST])
        for col in TWO:
            p, s, pp, pm, sp, sm = geo(col)
            for d, lo, to in ((PREV, 0, pp), (NEXT, 16, pm)):
                r = rows(a, col, (p + d) % RING, s, lo, 16)
                send(r, r, to, s_g.at[a], r_g.at[a, ON])

    def gb31(a):
        for col in TWO:
            p, s, pp, pm, sp, sm = geo(col)
            for d in (PREV, NEXT):
                r = rows(a, col, (p + d) % RING, s)
                for to in (sp, sm):
                    send(r, r, to, s_g.at[a], r_g.at[a, d])

    def gb2(a):
        wait(some(a, RW), r_g.at[a, ON])
        for col in TWO:
            p, s, pp, pm, sp, sm = geo(col)
            r = rows(a, col, (p + OPP) % RING, s)
            for to in (sp, sm):
                send(r, r, to, s_g.at[a], r_g.at[a, OPP])

    def gf(a, d):
        wait(some(a, FOUR), r_g.at[a, d])
        for col in TWO:
            p, s, pp, pm, sp, sm = geo(col)
            for e, lo, to in ((PREV, 0, sp), (NEXT, 16, sm)):
                r = rows(a, col, (p + d) % RING, (s + e) % RING, lo, 16)
                send(r, r, to, s_g.at[a], r_g.at[a, LAST])

    def gend(a):
        if a == AX:
            put.wait()
        wait(some(a, QB), r_g.at[a, LAST])
        for arr, idx in (((AX, 0), (AX, 1), (AX, 3), (AX, 2)), ((AD, 0),), ((AD, 1), (AD, 3), (AD, 2)))[a]:
            ap(arr, idx).start()

    w_in = (wg_ref, wu_ref, wd_ref)
    LATE = 6
    seen = set()

    def blocks(k, n):
        return wdf.at[pl.ds(0, n)] if k == WL else (wgf, wuf)[k].at[pl.ds(0, n * CB), :]

    def once(k, g, n):
        if (k, g) not in seen:
            seen.add((k, g))
            wait(blocks(k, n), r_v.at[k, g])

    def wpc(k):
        send(w_in[k], wblk(k, x, c), "pc", s_v.at[k], r_v.at[k, OWN])

    def wown(k):
        for fr, to in enumerate(("xp", "xm")):
            if k < WL:
                send(w_in[k], wblk(k, x, c), to, s_v.at[k], r_v.at[k, FIRST])
            else:
                send(wd_ref.at[pl.ds(fr * HB, HB), :], wblk(k, x, c, fr), to, s_v.at[k], r_v.at[k, FIRST])
        if k == WL:
            for fr, to in enumerate(("xp", "xm")):
                send(wd_ref.at[pl.ds((1 - fr) * HB, HB), :], wblk(k, x, c, 1 - fr), to, s_v.at[k], r_v.at[k, LATE])

    def wf(k):
        once(k, FIRST, 1 if k == WL else 2)
        for xx, d, half, to in ((xm, PREV, 0, "xp"), (xp, NEXT, 1, "xm")):
            r = wblk(k, xx, c, half)
            send(r, r, to, s_v.at[k], r_v.at[k, ON])
            if k < WL:
                r = wblk(k, xx, c)
                send(r, r, "pc", s_v.at[k], r_v.at[k, d])

    def wfp():
        once(WL, LATE, 1)
        for xx, d in ((xm, PREV), (xp, NEXT)):
            r = wblk(WL, xx, c)
            send(r, r, "pc", s_v.at[WL], r_v.at[WL, d])

    def wf2(k):
        once(k, ON, 1)
        for half in TWO:
            r = wblk(k, xq, c, half)
            send(r, r, "pc", s_v.at[k], r_v.at[k, OPP])

    def have(k, d, o):
        if o == 1:
            once(k, d, 1)
        elif d == OPP:
            once(k, ON, 1)
        elif d:
            once(k, FIRST, 1 if k == WL else 2)
            if k == WL:
                once(k, LATE, 1)

    xpos = {0: x, 1: xp, 2: xq, 3: xm}
    order = ((0, 0), (0, 1), (3, 0), (1, 0), (3, 1), (1, 1), (2, 0), (2, 1))

    def blk(t):
        d, o = order[t]
        return 2 * xpos[d] + (c if o == 0 else c1)

    def a_slot(t):
        s = t % RING
        return A.at[s // PAIR, s % PAIR]

    def ld_ab(t):
        d, o = order[t]
        s = t % RING
        ii = blk(t)
        out = [pltpu.make_async_copy(xd.at[0, :, pl.ds(pl.multiple_of(ii * CB, CB), CB)], a_slot(t), s_c.at[s, 0])]
        for k in TWO:
            src = w_in[k] if t == 0 else wblk(k, xpos[d], c if o == 0 else c1)
            out.append(pltpu.make_async_copy(src, WX.at[s % PAIR, k, pl.ds((s // PAIR) * CB, CB), :], s_c.at[s, 1]))
        return out

    def sab(t):
        for k in TWO:
            have(k, *order[t])
        for l in ld_ab(t):
            l.start()

    def ab(t):
        s = t % RING
        wait(a_slot(t), s_c.at[s, 0])
        wait(WX.at[s % PAIR, :, pl.ds((s // PAIR) * CB, CB), :], s_c.at[s, 1])

        def body(m, _):
            r = pl.ds(pl.multiple_of(m * QB, QB), QB)
            lhs = A[s // PAIR, s % PAIR, r, :]
            for k in TWO:
                v = jnp.dot(lhs, WX[s % PAIR, k, pl.ds((s // PAIR) * CB, CB), :], preferred_element_type=F32)
                if t == 0:
                    XB[2 * k + m // PAIR, m % PAIR] = v
                else:
                    XB[2 * k + m // PAIR, m % PAIR] += v
            return 0
        lax.fori_loop(0, 4, body, 0)

    def hp():
        def body(q, _):
            m = q // 8
            r = pl.ds(pl.multiple_of((q % 8) * RH, RH), RH)
            a = XB[m // PAIR, m % PAIR, r, :]
            b = XB[2 + m // PAIR, m % PAIR, r, :]
            sig = jax.nn.sigmoid(a)
            sa = a * sig
            XB[m // PAIR, m % PAIR, r, :] = b * sig * (1.0 + a * (1.0 - sig))
            XB[2 + m // PAIR, m % PAIR, r, :] = sa
            B[0, 0, pl.ds(pl.multiple_of(q * RH, RH), RH), :] = (sa * b).astype(BF)
            return 0
        lax.fori_loop(0, RH, body, 0)
        bp[0].start()
        uv_put.start()

    uv_put = pltpu.make_async_copy(XB, UV, s_one.at[0])

    def ld_g(t):
        d, o = order[t]
        s = t % RING
        ii = blk(t)
        src = wd_ref if t == 0 else wdf.at[ii]
        return [pltpu.make_async_copy(xd.at[1, :, pl.ds(pl.multiple_of(ii * CB, CB), CB)], a_slot(t), s_c.at[s, 0]),
                pltpu.make_async_copy(src, WX.at[s % PAIR, s // PAIR, pl.ds(0, FB), pl.ds(0, CB)], s_c.at[s, 1])]

    def sg(t):
        have(2, *order[t])
        for l in ld_g(t):
            l.start()

    def gg(t):
        for l in ld_g(t):
            l.wait()
        s = t % RING

        def body(m, _):
            r = pl.ds(pl.multiple_of(m * QB, QB), QB)
            v = lax.dot_general(A[s // PAIR, s % PAIR, r, :], WX[s % PAIR, s // PAIR, pl.ds(0, FB), pl.ds(0, CB)], NT, preferred_element_type=F32)
            if t == 0:
                XS[m] = v
            else:
                XS[m] += v
            return 0
        lax.fori_loop(0, 4, body, 0)

    def us_load(q, k):
        m = q // PAIR
        return pltpu.make_async_copy(UV.at[2 * k + m // PAIR, m % PAIR, pl.ds(pl.multiple_of((q % PAIR) * FOUR, FOUR), FOUR), :], XS.at[4 + q % PAIR, pl.ds(FOUR * k, FOUR), :], s_us.at[q % PAIR])

    def dadb():
        for k in TWO:
            us_load(0, k).start()

        def body(q, _):
            @pl.when(q < 7)
            def _():
                for k in TWO:
                    us_load(q + 1, k).start()
            wait(XS.at[4 + q % PAIR], s_us.at[q % PAIR])

            def inner(e, _):
                g = XS[q // PAIR, pl.ds(pl.multiple_of((q % PAIR) * FOUR + e * RH, RH), RH), :]
                o = pl.ds(pl.multiple_of(q * FOUR + e * RH, RH), RH)
                for k in TWO:
                    B[1 + k, 0, o, :] = (g * XS[4 + q % PAIR, pl.ds(pl.multiple_of(FOUR * k + e * RH, RH), RH), :]).astype(BF)
                return 0
            lax.fori_loop(0, 4, inner, 0)
            return 0
        lax.fori_loop(0, 8, body, 0)
        bp[1].start()
        bp[2].start()

    def chunk(idx):
        return (x + 6 - idx) % RING

    bp = [remote(B.at[k, 0], B.at[k, 1], s_b, r_b.at[k], "pc") for k in range(3)]

    def ap(arr, idx):
        return remote(xd.at[arr, :, pl.ds(pl.multiple_of(TG * chunk(idx) + CB * c1, CB), CB)], AP.at[arr, idx], s_ap, r_ap.at[arr, idx], "pc")

    seq = (0, 1, 3, 2)

    def load_a(k, n):
        arr = 1 - min(k, 1)
        idx = seq[n]
        return (pltpu.make_async_copy(xd.at[arr, :, pl.ds(pl.multiple_of(TG * chunk(idx) + CB * c, CB), CB)], A.at[n % PAIR, 0], s_a.at[n % PAIR]),
                pltpu.make_async_copy(AP.at[arr, idx], A.at[n % PAIR, 1], s_a.at[n % PAIR]))

    def start_a(k, n):
        if k < UP:
            ap(1 - k, seq[n]).wait_recv()
        for l in load_a(k, n):
            l.start()

    def dot_x(k, n, split=False):
        slot = n % PAIR
        wait(A.at[slot], s_a.at[slot])

        def body(m, _):
            cols = pl.ds(pl.multiple_of(m * QB, QB), QB)
            XB[seq[n], m] = (lax.dot_general(A[slot, 0, :, cols], B[k, 0], TN, preferred_element_type=F32)
                             + lax.dot_general(A[slot, 1, :, cols], B[k, 1], TN, preferred_element_type=F32))
            return 0

        if split:
            for m in TWO:
                body(m, 0)
                xmsg(k, m).start()
        else:
            lax.fori_loop(0, 2, body, 0)

    def xmsg(k, t):
        src = (XB.at[0, 0], XB.at[0, 1], XB.at[1, 1], XB.at[3, 0], XB.at[1, 0], XB.at[3, 1])[t]
        return remote(src, XR.at[k, t], s_xs.at[min(t // PAIR, 1)], r_xs.at[k, t // PAIR], ("xp", "xm")[t % PAIR])

    def xl(k, n):
        start_a(k, n)

    def x1(k):
        bp[k].wait_recv()
        if k == 0:
            uv_put.wait()
        else:
            wait(XB.at[0], s_xs.at[0])
        dot_x(k, 0, True)

    def x2(k):
        if k > 0:
            wait(XB.at[pl.ds(0, 2)], s_xs.at[1])
        dot_x(k, 1)
        start_a(k, 3)
        xmsg(k, 2).start()
        dot_x(k, 2)
        if k == 1:
            start_a(2, 0)
        xmsg(k, 3).start()

    def x2o(k):
        if k > 0:
            xout(k - 1).wait()
        dot_x(k, 3)
        if k == 1:
            start_a(2, 1)

    def xstage(k, t, slot):
        return pltpu.make_async_copy(XR.at[k, t], XS.at[4 + slot], s_one.at[1])

    def x3(k):
        wait(XS.at[pl.ds(4, 2)], r_xs.at[k, 0])
        for t in TWO:
            xstage(k, t, t).start()
        wait(XS.at[pl.ds(4, 2)], s_one.at[1])
        for t in TWO:
            add(XB.at[(1, 3)[t], t], XS.at[4 + t], QB)
            xmsg(k, 4 + t).start()

    def xout(k):
        return pltpu.make_async_copy(XB.at[2], dw.at[k], s_one.at[2])

    def xadd(k, ts):
        wait(XS.at[pl.ds(4, 2)], r_xs.at[k, ts[0] // PAIR])
        for h, t in enumerate(ts):
            xstage(k, t, h).start()
        wait(XS.at[pl.ds(4, 2)], s_one.at[1])
        for h, t in enumerate(ts):
            add(XB.at[2, h], XS.at[4 + h], QB)

    def xfa(k):
        xadd(k, (3, 2))
        if k == 2:
            xout(k).start()

    def xfb(k):
        xadd(k, (4, 5))
        xout(k).start()

    def pair(n, col):
        return ((0, 3), (1, 2))[col][n % PAIR]

    def lw(n):
        if n < 2:
            for col in TWO:
                have(2, pair(n, col), 0)
                have(2, pair(n, col), 1)
        out = []
        for col in TWO:
            d = pair(n, col)
            q = xpos[d]
            if n < 2:
                if d == 0:
                    out.append(pltpu.make_async_copy(wd_ref, WD.at[col, c], s_w.at[n // PAIR]))
                    out.append(pltpu.make_async_copy(wdf.at[2 * x + c1], WD.at[col, c1], s_w.at[n // PAIR]))
                else:
                    out.append(pltpu.make_async_copy(wdf.at[pl.ds(2 * q, 2)], WD.at[col], s_w.at[n // PAIR]))
            else:
                for k in TWO:
                    full = (wgf, wuf)[k]
                    if d == 0:
                        out.append(pltpu.make_async_copy(w_in[k], WX.at[col, k, pl.ds(pl.multiple_of(CB * c, CB), CB), :], s_w.at[n // PAIR]))
                        out.append(pltpu.make_async_copy(full.at[pl.ds(pl.multiple_of(TG * x + CB * c1, CB), CB), :],
                                                         WX.at[col, k, pl.ds(pl.multiple_of(CB * c1, CB), CB), :], s_w.at[n // PAIR]))
                    else:
                        out.append(pltpu.make_async_copy(full.at[pl.ds(pl.multiple_of(TG * q, TG), TG), :], WX.at[col, k], s_w.at[n // PAIR]))
        for o in out:
            o.start()

    def dots_z(n, lo, m):

        def body(q, _):
            col = q // m
            idx = lo + 2 * (q % m)
            p = z + col * (y - z)
            ch = (p + 6 - idx) % RING
            s1 = QB - 192 * col
            s2 = RW + 192 * col
            own = (idx // PAIR) * (1 - idx // 3)
            slot = idx + own * 2 * (n % PAIR)

            def lhs(k):
                return jnp.concatenate([B[k, 0, pl.ds(pl.multiple_of(ch * s1 + g * s2, RW), RW), :] for g in range(4)], axis=0)

            if n < 2:
                l = lhs(0)
                for h in TWO:
                    ZB[col, slot, h] = jnp.dot(l, WD[col, h], preferred_element_type=F32)
            else:
                l = lhs(1)
                u = lhs(2)
                for h in TWO:
                    r = pl.ds(CB * h, CB)
                    ZB[col, slot, h] = (lax.dot_general(l, WX[col, 0, r, :], NT, preferred_element_type=F32)
                                        + lax.dot_general(u, WX[col, 1, r, :], NT, preferred_element_type=F32))
            return 0
        lax.fori_loop(0, 2 * m, body, 0)

    def zmsg(n, col, t):
        src = ((0, 0), (0, 1), (1, 1), (3, 0), (1, 0), (3, 1))[t]
        return remote(ZB.at[col, src[0], src[1]], ZR.at[col, n, t], s_zs.at[min(t // PAIR, 1)], r_zs.at[n, t // PAIR], link[col][t % PAIR])

    def own(n, col, h):
        return ZB.at[col, 2 + 2 * (n % PAIR), h]

    def sub(n, col, h, d):
        s = (pos[col][1] + d) % RING
        return ZB.at[col, 2 + 2 * (n % PAIR), h, pl.ds(pl.multiple_of(s * RW, RW), RW), :]

    def msg2(n, col, t):
        h, d = ((0, 2), (1, 2), (1, 1), (0, 3), (0, 1), (1, 3))[t]
        return remote(sub(n, col, h, d), Z2.at[col, n, t], s_2.at[n % PAIR], r_2.at[n, min(t // PAIR, 1)], link[col][2 + t % PAIR])

    def p1(n):
        wait((WD, WX)[n // PAIR], s_w.at[n // PAIR])
        if n > 0:
            wait(ZB.at[0, pl.ds(0, 2)], s_zs.at[0])
        dots_z(n, 0, 1)
        for t in TWO:
            for col in TWO:
                zmsg(n, col, t).start()

    def p2(n):
        if n > 0:
            wait(ZB.at[0, pl.ds(0, 4)], s_zs.at[1])
        dots_z(n, 1, 2)
        for t in range(2, 4):
            for col in TWO:
                zmsg(n, col, t).start()

    def p2o(n):
        if n > 1:
            wait(Z2.at[0, pl.ds(0, 2)], s_2.at[n % PAIR])
        dots_z(n, 2, 1)

    def zstage(n, col, t, slot):
        return pltpu.make_async_copy(ZR.at[col, n, t], ZS.at[col, slot], s_one.at[3])

    def stage(n, ts):
        wait(ZS, r_zs.at[n, ts[0] // PAIR])
        for h, t in enumerate(ts):
            for col in TWO:
                zstage(n, col, t, h).start()
        wait(ZS, s_one.at[3])

    def p4(n):
        stage(n, (0, 1))
        for t in TWO:
            for col in TWO:
                add(ZB.at[col, (1, 3)[t], t], ZS.at[col, t], QB)
                zmsg(n, col, 4 + t).start()

    def zadd(n, ts):
        stage(n, ts)
        for h in TWO:
            for col in TWO:
                add(own(n, col, h), ZS.at[col, h], QB)

    def fa(n):
        zadd(n, (3, 2))

    def fb(n):
        zadd(n, (4, 5))
        for t in range(4):
            for col in TWO:
                msg2(n, col, t).start()

    def hh(n):
        wait(Z2.at[0, 0, pl.ds(0, 4)], r_2.at[n, 0])
        for t in TWO:
            for col in TWO:
                add(sub(n, col, t, (1, 3)[t]), Z2.at[col, n, t], RW)
                msg2(n, col, 4 + t).start()

    def zf(n):
        a = n // PAIR
        wait(Z2.at[:, 0, pl.ds(0, 4)], r_2.at[n, 1])
        for col in TWO:
            q = xpos[pair(n, col)]
            for h, ts in ((0, (3, 4)), (1, (2, 5))):
                cs = pl.ds(pl.multiple_of(TG * q + CB * h, CB), CB)
                v = sub(n, col, h, 0)[...] + Z2[col, n, ts[0]] + Z2[col, n, ts[1]]
                ov[a, :, cs] = (res[a, :, cs].astype(F32) + v).astype(BF)
        done.append(n)
        if len(done) == RING:
            out.start()

    def enter():
        for d in dev.values():
            pl.semaphore_signal(barrier, inc=1, device_id=d, device_id_type=MESH)
        pl.semaphore_wait(barrier, len(dev))

    own_ld = [pltpu.make_async_copy(r, res.at[k], s_one.at[4]) for k, r in enumerate((x_ref, dy_ref))]
    for l in own_ld:
        l.start()
    barrier = pltpu.get_barrier_semaphore()
    enter()
    wait(res, s_one.at[4])
    put = pltpu.make_async_copy(res, xd.at[:, pl.ds(pl.multiple_of(j * RW, RW), RW), :], s_one.at[5])
    put.start()
    out = pltpu.make_async_copy(ov, yo, s_one.at[6])
    done = []
    ga(AX)
    gb0(AX)
    ga(AD)
    wpc(WL)
    wpc(WU)
    wpc(WG)
    wown(WG)
    ga2(AX)
    gf(AX, OWN)
    gb31(AX)
    wown(WU)
    ga2(AD)
    gb2(AX)
    wf(WG)
    gf(AX, PREV)
    gf(AX, NEXT)
    gf(AX, OPP)
    ga(AE)
    gb31(AD)
    wf(WU)
    gb0(AD)
    gend(AX)
    sab(B2)
    sab(B1)
    sab(B0)
    ab(B0)
    wown(WL)
    ab(B1)
    gb2(AD)
    sab(B3)
    gf(AD, PREV)
    sab(B4)
    ga2(AE)
    wf2(WG)
    ab(B2)
    gb0(AE)
    wf2(WU)
    gf(AD, OWN)
    ab(B3)
    sab(B6)
    gf(AD, NEXT)
    gf(AD, OPP)
    sab(B5)
    ab(B4)
    sab(B7)
    gb2(AE)
    ab(B5)
    gb31(AE)
    gf(AE, OWN)
    ab(B6)
    wf(WL)
    ab(B7)
    gend(AD)
    hp()
    xl(DOWN, A0)
    gf(AE, PREV)
    wfp()
    gf(AE, NEXT)
    gf(AE, OPP)
    x1(DOWN)
    lw(Y0)
    gend(AE)
    p1(Y0)
    xl(DOWN, A2)
    xl(DOWN, A1)
    wf2(WL)
    p2(Y0)
    x2(DOWN)
    x2o(DOWN)
    sg(B1)
    sg(B0)
    p2o(Y0)
    lw(Y1)
    gg(B0)
    sg(B4)
    sg(B3)
    gg(B1)
    sg(B2)
    p4(Y0)
    gg(B2)
    gg(B3)
    gg(B4)
    sg(B5)
    p1(Y1)
    x3(DOWN)
    sg(B6)
    gg(B5)
    gg(B6)
    sg(B7)
    p2(Y1)
    gg(B7)
    xl(GATE, A0)
    lw(X0)
    dadb()
    xfa(DOWN)
    p2o(Y1)
    xl(GATE, A1)
    x1(GATE)
    p4(Y1)
    fa(Y0)
    p1(X0)
    xl(GATE, A2)
    x2(GATE)
    fb(Y0)
    xfb(DOWN)
    x3(GATE)
    fa(Y1)
    x1(UP)
    fb(Y1)
    hh(Y0)
    x2o(GATE)
    p2(X0)
    zf(Y0)
    xl(UP, A2)
    p4(X0)
    p2o(X0)
    lw(X1)
    hh(Y1)
    p1(X1)
    xfa(GATE)
    x2(UP)
    fa(X0)
    p2(X1)
    p4(X1)
    xfb(GATE)
    x3(UP)
    zf(Y1)
    fb(X0)
    p2o(X1)
    x2o(UP)
    fa(X1)
    fb(X1)
    hh(X0)
    xfa(UP)
    hh(X1)
    zf(X0)
    zf(X1)
    def end():
        for a in (AX, AD, AE):
            wait(some(a, 960), s_g.at[a])
        for k in (WG, WU, WL):
            wait(blocks(k, 7), s_v.at[k])
        wait(AP, s_ap)
        wait(B.at[:, 0], s_b)
        for q in TWO:
            wait(Z2.at[0, pl.ds(0, 2)], s_2.at[q])
            wait(ZB.at[0, pl.ds(0, 2 + 2 * q)], s_zs.at[q])
        xout(2).wait()
        out.wait()
        wait(XB.at[0], s_xs.at[0])
        wait(XB.at[pl.ds(0, 2)], s_xs.at[1])
        wait(XS.at[pl.ds(4, 2)], r_xs.at[2, 2])

    end()


def mlp(x, dy, wg, wu, wd):
    sd = jax.ShapeDtypeStruct
    dma = pltpu.SemaphoreType.DMA
    V = pltpu.VMEM
    o = pl.pallas_call(
        mlp_kernel,
        out_shape=(sd((3, 2, QB, FB), F32), sd((2, RW, DM), BF),
                   sd((2, TG, DM), BF), sd((DM, FB), BF), sd((DM, FB), BF), sd((8, FB, CB), BF), sd((4, 2, QB, FB), F32),
                   sd((3, 6, QB, FB), F32), sd((2, 4, 6, QB, CB), F32), sd((2, 4, TG, CB), BF)),
        in_specs=[HBM] * 5,
        out_specs=(HBM,) * 10,
        scratch_shapes=[
            V((3, 2, TG, FB), BF), V((2, 2, TG, CB), BF), V((4, 2, QB, FB), F32), V((6, QB, FB), F32),
            V((2, 2, FB, CB), BF), V((2, 2, TG, FB), BF), V((2, 5, 2, QB, CB), F32), V((2, 2, QB, CB), F32),
            V((2, 4, 6, RW, CB), F32), V((2, RW, DM), BF), V((2, RW, DM), BF),
            dma((3,)), dma((3, 7)), dma((3,)), dma((3, 7)), dma, dma((2, 4)), dma, dma((3,)), dma((2,)), dma((3, 3)),
            dma((2,)), dma((4, 3)), dma((2,)), dma((4, 2)), dma((4, 2)), dma((2,)), dma((2,)), dma((2,)), dma((7,)),
        ],
        compiler_params=pltpu.CompilerParams(collective_id=1, has_side_effects=True, vmem_limit_bytes=67043328),
        name="mlp",
    )(x, dy, wg, wu, wd)
    return o[0], o[1], o[7]


def place_kernel(dw, yo, xr, y, dx, dg, du, dd, bw, by, bt, br, s_in, s_out):
    w_in = [pltpu.make_async_copy(dw.at[k], bw.at[k], s_in.at[k]) for k in range(3)]
    y_in = [pltpu.make_async_copy(yo.at[k], by.at[k], s_in.at[3 + k]) for k in TWO]
    r_in = pltpu.make_async_copy(xr.at[2, pl.ds(4, 2)], br, s_in.at[5])
    for l in w_in + [r_in] + y_in:
        l.start()
    w_out = [pltpu.make_async_copy(bt, dd, s_out.at[0]), pltpu.make_async_copy(bw.at[1], dg, s_out.at[1]), pltpu.make_async_copy(bw.at[2], du, s_out.at[2])]
    y_out = [pltpu.make_async_copy(by.at[0], y, s_out.at[3]), pltpu.make_async_copy(by.at[1], dx, s_out.at[4])]
    w_in[0].wait()
    for h in TWO:
        bt[:, pl.ds(QB * h, QB)] = bw[0, pl.ds(QB * h, QB), :].T
    w_out[0].start()
    w_in[1].wait()
    w_out[1].start()
    w_in[2].wait()
    r_in.wait()
    for h in TWO:
        bw[2, pl.ds(QB * h, QB), :] += br[h]
    w_out[2].start()
    for l, e in zip(y_in, y_out):
        l.wait()
        e.start()
    for e in w_out + y_out:
        e.wait()


def place(dw, yo, xr):
    sd = jax.ShapeDtypeStruct
    V = pltpu.VMEM
    return pl.pallas_call(
        place_kernel,
        out_shape=(sd((RW, DM), BF), sd((RW, DM), BF), sd((CB, FB), F32), sd((CB, FB), F32), sd((FB, CB), F32)),
        in_specs=[HBM] * 3,
        out_specs=(HBM,) * 5,
        scratch_shapes=[V((3, CB, FB), F32), V((2, RW, DM), BF), V((FB, CB), F32), V((2, QB, FB), F32),
                        pltpu.SemaphoreType.DMA((6,)), pltpu.SemaphoreType.DMA((5,))],
        compiler_params=pltpu.CompilerParams(vmem_limit_bytes=60 * 2**20),
        name="place",
    )(dw.reshape(3, CB, FB), yo, xr)


def solution(mesh):
    rows = P(("dp", "tp"), None)
    wsp = P("dp", "tp")
    dsp = P("tp", "dp")

    def local(x, w_gate, w_up, w_down, dy):
        return place(*mlp(x, dy, w_gate, w_up, w_down))

    return jax.shard_map(local, mesh=mesh, in_specs=(rows, wsp, wsp, dsp, rows), out_specs=(rows, rows, wsp, wsp, dsp), check_vma=False)
```

time: 285 us -> 281 us (0.986)
  Pallas kernels: 283 us -> 279 us
    pallas_call x1, Pallas kernels: 278 us -> 274 us  [mlp(): pl.pallas_call(mlp_kernel, out_shape=(sd((3, 2, QB, FB), F32), sd((2, RW,...]
where the time goes in v7:
time: 281 us; the launch traced here: 280 us
  Pallas kernels  279 us (99%)
    pallas_call x1, Pallas kernels, mlp(): pl.pallas_call(mlp_kernel, out_shape=(sd((3, 2, QB, FB), F32), sd((2, RW,...  274 us

profile of v7, /device:TPU:1, one launch (start us, length us, event | category | flops | bytes accessed | tf_op | source)
XLA Modules:
  0.0 279.9 jit_solution(5198255358763199425)
XLA Ops:
  0.6 273.9 %mlp.1 = (f32[3,2,256,896]{3,2,1,0:T(8,128)}, bf16[2,64,4096]{2,1,0:T(8,128)(2,1)}, bf16[2,1024,4096]{2,1,0:T(8,128)(2,1)}, bf16[4096,896]{1,0:T(8,128)(2,1)}, b...) custom-call(bf16[64,4096]{1,0:T(8,128)(2,1)} %x_ref.1, ...), custom_call_target="tpu_custom_call" | custom-call | tf_op jit(solution)/shard_map/mlp/pallas_call | solution.py:746
  274.5 5.3 %place.1 = (bf16[64,4096]{1,0:T(8,128)(2,1)}, bf16[64,4096]{1,0:T(8,128)(2,1)}, f32[512,896]{1,0:T(8,128)}, f32[512,896]{1,0:T(8,128)}, f32[896,512]{1,0:T(8,128)}) custom-call(f32[3,512,896]{2,1,0:T(8,128)} %bitcast.1, bf16[2,64,4096]{2,1,0:T(8,128)(2,1)} %get-tuple-element.9.yo, f32[3,6,256,896]{3,2,1,0:T(8,128)} %get-tuple-element.10.xr), custom_call_target="tpu_custom_call" | custom-call | tf_op jit(solution)/shard_map/place/pallas_call | solution.py:795

commit v8 on v7

--- a/solution.py
+++ b/solution.py
@@ -7,6 +7,7 @@
 
 MESH = pl.DeviceIdType.MESH
 HBM = pl.BlockSpec(memory_space=pltpu.HBM)
+VMEM = pl.BlockSpec(memory_space=pltpu.VMEM)
 NT = (((1,), (1,)), ((), ()))
 TN = (((0,), (0,)), ((), ()))
 F32 = jnp.float32
@@ -26,8 +27,8 @@
 B0, B1, B2, B3, B4, B5, B6, B7 = range(8)
 
 
-def mlp_kernel(x_ref, dy_ref, wg_ref, wu_ref, wd_ref, dw, yo, xd, wgf, wuf, wdf, UV, XR, ZR, AP,
-               B, A, XB, XS, WD, WX, ZB, ZS, Z2, res, ov,
+def mlp_kernel(x_ref, dy_ref, wg_ref, wu_ref, wd_ref, dw, yo, du, xd, wgf, wuf, wdf, U, V, XR, ZR, AP,
+               B, A, XB, XS, WD, WX, ZB, ZS, Z2,
                s_g, r_g, s_v, r_v, s_ap, r_ap, s_b, r_b, s_xs, r_xs, s_zs, r_zs, s_2, r_2, s_c, s_a, s_w, s_us, s_one):
     i = lax.axis_index("dp")
     j = lax.axis_index("tp")
@@ -93,14 +94,14 @@
     def ga(a):
         for col in TWO:
             p, s, pp, pm, sp, sm = geo(col)
-            src = res.at[min(a, AD), pl.ds(col * RH, RH), cols(a)]
+            src = yo.at[min(a, AD), pl.ds(col * RH, RH), cols(a)]
             for to in (pp, pm):
                 send(src, rows(a, col, p, s), to, s_g.at[a], r_g.at[a, FIRST])
 
     def gb0(a):
         for col in TWO:
             p, s, pp, pm, sp, sm = geo(col)
-            src = res.at[min(a, AD), pl.ds(col * RH, RH), cols(a)]
+            src = yo.at[min(a, AD), pl.ds(col * RH, RH), cols(a)]
             for to in (sp, sm):
                 send(src, rows(a, col, p, s), to, s_g.at[a], r_g.at[a, OWN])
 
@@ -236,10 +237,8 @@
             lhs = A[s // PAIR, s % PAIR, r, :]
             for k in TWO:
                 v = jnp.dot(lhs, WX[s % PAIR, k, pl.ds((s // PAIR) * CB, CB), :], preferred_element_type=F32)
-                if t == 0:
-                    XB[2 * k + m // PAIR, m % PAIR] = v
-                else:
-                    XB[2 * k + m // PAIR, m % PAIR] += v
+                to = XB.at[m // PAIR, m % PAIR] if k == WG else XS.at[m]
+                to[...] = v if t == 0 else to[...] + v
             return 0
         lax.fori_loop(0, 4, body, 0)
 
@@ -248,18 +247,20 @@
             m = q // 8
             r = pl.ds(pl.multiple_of((q % 8) * RH, RH), RH)
             a = XB[m // PAIR, m % PAIR, r, :]
-            b = XB[2 + m // PAIR, m % PAIR, r, :]
+            b = XS[m, r, :]
             sig = jax.nn.sigmoid(a)
             sa = a * sig
             XB[m // PAIR, m % PAIR, r, :] = b * sig * (1.0 + a * (1.0 - sig))
-            XB[2 + m // PAIR, m % PAIR, r, :] = sa
+            XS[m, r, :] = sa
             B[0, 0, pl.ds(pl.multiple_of(q * RH, RH), RH), :] = (sa * b).astype(BF)
             return 0
         lax.fori_loop(0, RH, body, 0)
         bp[0].start()
-        uv_put.start()
-
-    uv_put = pltpu.make_async_copy(XB, UV, s_one.at[0])
+        u_put.start()
+        v_put.start()
+
+    u_put = pltpu.make_async_copy(XB.at[pl.ds(0, 2)], U, s_one.at[0])
+    v_put = pltpu.make_async_copy(XS.at[pl.ds(0, 4)], V, s_one.at[2])
 
     def ld_g(t):
         d, o = order[t]
@@ -275,6 +276,8 @@
             l.start()
 
     def gg(t):
+        if t == 0:
+            v_put.wait()
         for l in ld_g(t):
             l.wait()
         s = t % RING
@@ -291,7 +294,9 @@
 
     def us_load(q, k):
         m = q // PAIR
-        return pltpu.make_async_copy(UV.at[2 * k + m // PAIR, m % PAIR, pl.ds(pl.multiple_of((q % PAIR) * FOUR, FOUR), FOUR), :], XS.at[4 + q % PAIR, pl.ds(FOUR * k, FOUR), :], s_us.at[q % PAIR])
+        r = pl.ds(pl.multiple_of((q % PAIR) * FOUR, FOUR), FOUR)
+        src = U.at[m // PAIR, m % PAIR, r, :] if k == 0 else V.at[m, r, :]
+        return pltpu.make_async_copy(src, XS.at[4 + q % PAIR, pl.ds(FOUR * k, FOUR), :], s_us.at[q % PAIR])
 
     def dadb():
         for k in TWO:
@@ -344,7 +349,8 @@
 
         def body(m, _):
             cols = pl.ds(pl.multiple_of(m * QB, QB), QB)
-            XB[seq[n], m] = (lax.dot_general(A[slot, 0, :, cols], B[k, 0], TN, preferred_element_type=F32)
+            to = (XB.at[0, m], XB.at[1, m], XB.at[2, m], dw.at[k, m])[n]
+            to[...] = (lax.dot_general(A[slot, 0, :, cols], B[k, 0], TN, preferred_element_type=F32)
                              + lax.dot_general(A[slot, 1, :, cols], B[k, 1], TN, preferred_element_type=F32))
             return 0
 
@@ -356,8 +362,9 @@
             lax.fori_loop(0, 2, body, 0)
 
     def xmsg(k, t):
-        src = (XB.at[0, 0], XB.at[0, 1], XB.at[1, 1], XB.at[3, 0], XB.at[1, 0], XB.at[3, 1])[t]
-        return remote(src, XR.at[k, t], s_xs.at[min(t // PAIR, 1)], r_xs.at[k, t // PAIR], ("xp", "xm")[t % PAIR])
+        src = (XB.at[0, 0], XB.at[0, 1], XB.at[1, 1], XB.at[2, 0], XB.at[1, 0], XB.at[2, 1])[t]
+        dst = du.at[t - 4] if k == UP and t >= 4 else XR.at[k, t]
+        return remote(src, dst, s_xs.at[min(t // PAIR, 1)], r_xs.at[k, t // PAIR], ("xp", "xm")[t % PAIR])
 
     def xl(k, n):
         start_a(k, n)
@@ -365,7 +372,7 @@
     def x1(k):
         bp[k].wait_recv()
         if k == 0:
-            uv_put.wait()
+            u_put.wait()
         else:
             wait(XB.at[0], s_xs.at[0])
         dot_x(k, 0, True)
@@ -382,8 +389,6 @@
         xmsg(k, 3).start()
 
     def x2o(k):
-        if k > 0:
-            xout(k - 1).wait()
         dot_x(k, 3)
         if k == 1:
             start_a(2, 1)
@@ -397,11 +402,8 @@
             xstage(k, t, t).start()
         wait(XS.at[pl.ds(4, 2)], s_one.at[1])
         for t in TWO:
-            add(XB.at[(1, 3)[t], t], XS.at[4 + t], QB)
+            add(XB.at[1 + t, t], XS.at[4 + t], QB)
             xmsg(k, 4 + t).start()
-
-    def xout(k):
-        return pltpu.make_async_copy(XB.at[2], dw.at[k], s_one.at[2])
 
     def xadd(k, ts):
         wait(XS.at[pl.ds(4, 2)], r_xs.at[k, ts[0] // PAIR])
@@ -409,16 +411,13 @@
             xstage(k, t, h).start()
         wait(XS.at[pl.ds(4, 2)], s_one.at[1])
         for h, t in enumerate(ts):
-            add(XB.at[2, h], XS.at[4 + h], QB)
+            add(dw.at[k, h], XS.at[4 + h], QB)
 
     def xfa(k):
         xadd(k, (3, 2))
-        if k == 2:
-            xout(k).start()
 
     def xfb(k):
         xadd(k, (4, 5))
-        xout(k).start()
 
     def pair(n, col):
         return ((0, 3), (1, 2))[col][n % PAIR]
@@ -555,34 +554,35 @@
                 add(sub(n, col, t, (1, 3)[t]), Z2.at[col, n, t], RW)
                 msg2(n, col, 4 + t).start()
 
+    done = []
+
     def zf(n):
         a = n // PAIR
+        if not done:
+            for g in (AX, AD, AE):
+                wait(some(g, 960), s_g.at[g])
+        done.append(n)
         wait(Z2.at[:, 0, pl.ds(0, 4)], r_2.at[n, 1])
         for col in TWO:
             q = xpos[pair(n, col)]
             for h, ts in ((0, (3, 4)), (1, (2, 5))):
                 cs = pl.ds(pl.multiple_of(TG * q + CB * h, CB), CB)
                 v = sub(n, col, h, 0)[...] + Z2[col, n, ts[0]] + Z2[col, n, ts[1]]
-                ov[a, :, cs] = (res[a, :, cs].astype(F32) + v).astype(BF)
-        done.append(n)
-        if len(done) == RING:
-            out.start()
+                yo[a, :, cs] = (yo[a, :, cs].astype(F32) + v).astype(BF)
 
     def enter():
         for d in dev.values():
             pl.semaphore_signal(barrier, inc=1, device_id=d, device_id_type=MESH)
         pl.semaphore_wait(barrier, len(dev))
 
-    own_ld = [pltpu.make_async_copy(r, res.at[k], s_one.at[4]) for k, r in enumerate((x_ref, dy_ref))]
+    own_ld = [pltpu.make_async_copy(r, yo.at[k], s_one.at[4]) for k, r in enumerate((x_ref, dy_ref))]
     for l in own_ld:
         l.start()
     barrier = pltpu.get_barrier_semaphore()
     enter()
-    wait(res, s_one.at[4])
-    put = pltpu.make_async_copy(res, xd.at[:, pl.ds(pl.multiple_of(j * RW, RW), RW), :], s_one.at[5])
+    wait(yo, s_one.at[4])
+    put = pltpu.make_async_copy(yo, xd.at[:, pl.ds(pl.multiple_of(j * RW, RW), RW), :], s_one.at[5])
     put.start()
-    out = pltpu.make_async_copy(ov, yo, s_one.at[6])
-    done = []
     ga(AX)
     gb0(AX)
     ga(AD)
@@ -721,8 +721,6 @@
     zf(X0)
     zf(X1)
     def end():
-        for a in (AX, AD, AE):
-            wait(some(a, 960), s_g.at[a])
         for k in (WG, WU, WL):
             wait(blocks(k, 7), s_v.at[k])
         wait(AP, s_ap)
@@ -730,11 +728,9 @@
         for q in TWO:
             wait(Z2.at[0, pl.ds(0, 2)], s_2.at[q])
             wait(ZB.at[0, pl.ds(0, 2 + 2 * q)], s_zs.at[q])
-        xout(2).wait()
-        out.wait()
         wait(XB.at[0], s_xs.at[0])
         wait(XB.at[pl.ds(0, 2)], s_xs.at[1])
-        wait(XS.at[pl.ds(4, 2)], r_xs.at[2, 2])
+        wait(du, r_xs.at[2, 2])
 
     end()
 
@@ -745,63 +741,53 @@
     V = pltpu.VMEM
     o = pl.pallas_call(
         mlp_kernel,
-        out_shape=(sd((3, 2, QB, FB), F32), sd((2, RW, DM), BF),
-                   sd((2, TG, DM), BF), sd((DM, FB), BF), sd((DM, FB), BF), sd((8, FB, CB), BF), sd((4, 2, QB, FB), F32),
+        out_shape=(V((3, 2, QB, FB), F32), V((2, RW, DM), BF), V((2, QB, FB), F32),
+                   sd((2, TG, DM), BF), sd((DM, FB), BF), sd((DM, FB), BF), sd((8, FB, CB), BF), sd((2, 2, QB, FB), F32), sd((4, QB, FB), F32),
                    sd((3, 6, QB, FB), F32), sd((2, 4, 6, QB, CB), F32), sd((2, 4, TG, CB), BF)),
         in_specs=[HBM] * 5,
-        out_specs=(HBM,) * 10,
+        out_specs=(VMEM,) * 3 + (HBM,) * 9,
         scratch_shapes=[
-            V((3, 2, TG, FB), BF), V((2, 2, TG, CB), BF), V((4, 2, QB, FB), F32), V((6, QB, FB), F32),
+            V((3, 2, TG, FB), BF), V((2, 2, TG, CB), BF), V((3, 2, QB, FB), F32), V((6, QB, FB), F32),
             V((2, 2, FB, CB), BF), V((2, 2, TG, FB), BF), V((2, 5, 2, QB, CB), F32), V((2, 2, QB, CB), F32),
-            V((2, 4, 6, RW, CB), F32), V((2, RW, DM), BF), V((2, RW, DM), BF),
+            V((2, 4, 6, RW, CB), F32),
             dma((3,)), dma((3, 7)), dma((3,)), dma((3, 7)), dma, dma((2, 4)), dma, dma((3,)), dma((2,)), dma((3, 3)),
             dma((2,)), dma((4, 3)), dma((2,)), dma((4, 2)), dma((4, 2)), dma((2,)), dma((2,)), dma((2,)), dma((7,)),
         ],
-        compiler_params=pltpu.CompilerParams(collective_id=1, has_side_effects=True, vmem_limit_bytes=67043328),
+        compiler_params=pltpu.CompilerParams(collective_id=1, has_side_effects=True, vmem_limit_bytes=58600000),
         name="mlp",
     )(x, dy, wg, wu, wd)
-    return o[0], o[1], o[7]
-
-
-def place_kernel(dw, yo, xr, y, dx, dg, du, dd, bw, by, bt, br, s_in, s_out):
-    w_in = [pltpu.make_async_copy(dw.at[k], bw.at[k], s_in.at[k]) for k in range(3)]
-    y_in = [pltpu.make_async_copy(yo.at[k], by.at[k], s_in.at[3 + k]) for k in TWO]
-    r_in = pltpu.make_async_copy(xr.at[2, pl.ds(4, 2)], br, s_in.at[5])
-    for l in w_in + [r_in] + y_in:
-        l.start()
-    w_out = [pltpu.make_async_copy(bt, dd, s_out.at[0]), pltpu.make_async_copy(bw.at[1], dg, s_out.at[1]), pltpu.make_async_copy(bw.at[2], du, s_out.at[2])]
-    y_out = [pltpu.make_async_copy(by.at[0], y, s_out.at[3]), pltpu.make_async_copy(by.at[1], dx, s_out.at[4])]
-    w_in[0].wait()
+    return o[:3]
+
+
+def place_kernel(dw, yo, du, y, dx, og, ou, od, bu, bt, sem):
+    outs = [pltpu.make_async_copy(dw.at[1], og, sem.at[0]), pltpu.make_async_copy(yo.at[0], y, sem.at[1]), pltpu.make_async_copy(yo.at[1], dx, sem.at[2]),
+            pltpu.make_async_copy(bu, ou, sem.at[3]), pltpu.make_async_copy(bt, od, sem.at[4])]
+    for o in outs[:3]:
+        o.start()
     for h in TWO:
-        bt[:, pl.ds(QB * h, QB)] = bw[0, pl.ds(QB * h, QB), :].T
-    w_out[0].start()
-    w_in[1].wait()
-    w_out[1].start()
-    w_in[2].wait()
-    r_in.wait()
+        r = pl.ds(QB * h, QB)
+        bu[r, :] = dw[2, r, :] + du[h]
+    outs[3].start()
     for h in TWO:
-        bw[2, pl.ds(QB * h, QB), :] += br[h]
-    w_out[2].start()
-    for l, e in zip(y_in, y_out):
-        l.wait()
-        e.start()
-    for e in w_out + y_out:
-        e.wait()
-
-
-def place(dw, yo, xr):
+        r = pl.ds(QB * h, QB)
+        bt[:, r] = dw[0, r, :].T
+    outs[4].start()
+    for o in outs:
+        o.wait()
+
+
+def place(dw, yo, du):
     sd = jax.ShapeDtypeStruct
     V = pltpu.VMEM
     return pl.pallas_call(
         place_kernel,
         out_shape=(sd((RW, DM), BF), sd((RW, DM), BF), sd((CB, FB), F32), sd((CB, FB), F32), sd((FB, CB), F32)),
-        in_specs=[HBM] * 3,
+        in_specs=[VMEM] * 3,
         out_specs=(HBM,) * 5,
-        scratch_shapes=[V((3, CB, FB), F32), V((2, RW, DM), BF), V((FB, CB), F32), V((2, QB, FB), F32),
-                        pltpu.SemaphoreType.DMA((6,)), pltpu.SemaphoreType.DMA((5,))],
-        compiler_params=pltpu.CompilerParams(vmem_limit_bytes=60 * 2**20),
+        scratch_shapes=[V((CB, FB), F32), V((FB, CB), F32), pltpu.SemaphoreType.DMA((5,))],
+        compiler_params=pltpu.CompilerParams(vmem_limit_bytes=24 * 2**20),
         name="place",
-    )(dw.reshape(3, CB, FB), yo, xr)
+    )(dw.reshape(3, CB, FB), yo, du)
 
 
 def solution(mesh):

time: 281 us -> 278 us (0.989)
  no operation moved by 1% of the time
where the time goes in v8:
time: 278 us; the launch traced here: 277 us
  Pallas kernels  277 us (100%)
    pallas_call x1, Pallas kernels, mlp(): pl.pallas_call(mlp_kernel, out_shape=(V((3, 2, QB, FB), F32), V((2, RW, D...  274 us

profile of v8, /device:TPU:1, one launch (start us, length us, event | category | flops | bytes accessed | tf_op | source)
XLA Modules:
  0.0 277.4 jit_solution(10726196065589407363)
XLA Ops:
  0.6 273.8 %mlp.1 = (f32[3,2,256,896]{3,2,1,0:T(8,128)S(1)}, bf16[2,64,4096]{2,1,0:T(8,128)(2,1)S(1)}, f32[2,256,896]{2,1,0:T(8,128)S(1)}, bf16[2,1024,4096]{2,1,0:T(8,128)...) custom-call(bf16[64,4096]{1,0:T(8,128)(2,1)} %x_ref.1, ...), custom_call_target="tpu_custom_call" | custom-call | tf_op jit(solution)/shard_map/mlp/pallas_call | solution.py:742
  274.4 2.8 %place.1 = (bf16[64,4096]{1,0:T(8,128)(2,1)}, bf16[64,4096]{1,0:T(8,128)(2,1)}, f32[512,896]{1,0:T(8,128)}, f32[512,896]{1,0:T(8,128)}, f32[896,512]{1,0:T(8,128)}) custom-call(f32[3,512,896]{2,1,0:T(8,128)S(1)} %bitcast.1, bf16[2,64,4096]{2,1,0:T(8,128)(2,1)S(1)} %get-tuple-element.9.yo, f32[2,256,896]{2,1,0:T(8,128)S(1)} %get-tuple-element.10.du), custom_call_target="tpu_custom_call" | custom-call | tf_op jit(solution)/shard_map/place/pallas_call | solution.py:782

commit v9 on v8

--- a/solution.py
+++ b/solution.py
@@ -29,7 +29,7 @@
 
 def mlp_kernel(x_ref, dy_ref, wg_ref, wu_ref, wd_ref, dw, yo, du, xd, wgf, wuf, wdf, U, V, XR, ZR, AP,
                B, A, XB, XS, WD, WX, ZB, ZS, Z2,
-               s_g, r_g, s_v, r_v, s_ap, r_ap, s_b, r_b, s_xs, r_xs, s_zs, r_zs, s_2, r_2, s_c, s_a, s_w, s_us, s_one):
+               s_g, r_g, s_v, r_v, s_ap, r_ap, s_b, r_b, s_xs, r_xs, s_zs, r_zs, s_2, r_2, s_c, s_a, s_w, s_us, s_one, in_x, in_zy):
     i = lax.axis_index("dp")
     j = lax.axis_index("tp")
     x, c, z, y = i // PAIR, i % PAIR, j // 4, j % RING
@@ -570,30 +570,56 @@
                 v = sub(n, col, h, 0)[...] + Z2[col, n, ts[0]] + Z2[col, n, ts[1]]
                 yo[a, :, cs] = (yo[a, :, cs].astype(F32) + v).astype(BF)
 
+    odd = (x + c + y + z) % PAIR
+    along = ("xp", "xm", "pc")
+    across = ("yp", "ym", "zp", "zm")
+
+    def tell(sem, names):
+        for d in names:
+            pl.semaphore_signal(sem, inc=1, device_id=dev[d], device_id_type=MESH)
+
     def enter():
-        for d in dev.values():
-            pl.semaphore_signal(barrier, inc=1, device_id=d, device_id_type=MESH)
-        pl.semaphore_wait(barrier, len(dev))
+        @pl.when(odd == 0)
+        def _():
+            tell(barrier, across)
+            pl.semaphore_wait(barrier, len(along))
+            tell(in_x, along)
+
+        @pl.when(odd == 1)
+        def _():
+            tell(barrier, along)
+            pl.semaphore_wait(in_x, len(along))
+
+    def enter_zy():
+        @pl.when(odd == 0)
+        def _():
+            pl.semaphore_wait(in_zy, len(across))
+
+        @pl.when(odd == 1)
+        def _():
+            pl.semaphore_wait(barrier, len(across))
+            tell(in_zy, across)
 
     own_ld = [pltpu.make_async_copy(r, yo.at[k], s_one.at[4]) for k, r in enumerate((x_ref, dy_ref))]
     for l in own_ld:
         l.start()
     barrier = pltpu.get_barrier_semaphore()
     enter()
+    put = pltpu.make_async_copy(yo, xd.at[:, pl.ds(pl.multiple_of(j * RW, RW), RW), :], s_one.at[5])
+    wown(WG)
+    wown(WU)
+    wpc(WG)
+    wpc(WU)
+    wpc(WL)
     wait(yo, s_one.at[4])
-    put = pltpu.make_async_copy(yo, xd.at[:, pl.ds(pl.multiple_of(j * RW, RW), RW), :], s_one.at[5])
     put.start()
+    enter_zy()
     ga(AX)
     gb0(AX)
     ga(AD)
-    wpc(WL)
-    wpc(WU)
-    wpc(WG)
-    wown(WG)
     ga2(AX)
     gf(AX, OWN)
     gb31(AX)
-    wown(WU)
     ga2(AD)
     gb2(AX)
     wf(WG)
@@ -752,6 +778,7 @@
             V((2, 4, 6, RW, CB), F32),
             dma((3,)), dma((3, 7)), dma((3,)), dma((3, 7)), dma, dma((2, 4)), dma, dma((3,)), dma((2,)), dma((3, 3)),
             dma((2,)), dma((4, 3)), dma((2,)), dma((4, 2)), dma((4, 2)), dma((2,)), dma((2,)), dma((2,)), dma((7,)),
+            pltpu.SemaphoreType.REGULAR, pltpu.SemaphoreType.REGULAR,
         ],
         compiler_params=pltpu.CompilerParams(collective_id=1, has_side_effects=True, vmem_limit_bytes=58600000),
         name="mlp",

time: 278 us -> 277 us (level)
  no operation moved by 1% of the time
where the time goes in v9:
time: 277 us
  Pallas kernels  276 us (100%)
    pallas_call x1, Pallas kernels, mlp(): pl.pallas_call(mlp_kernel, out_shape=(V((3, 2, QB, FB), F32), V((2, RW, D...  273 us

profile of v9, /device:TPU:1, one launch (start us, length us, event | category | flops | bytes accessed | tf_op | source)
XLA Modules:
  0.0 276.5 jit_solution(2078111325546855572)
XLA Ops:
  0.6 272.9 %mlp.1 = (f32[3,2,256,896]{3,2,1,0:T(8,128)S(1)}, bf16[2,64,4096]{2,1,0:T(8,128)(2,1)S(1)}, f32[2,256,896]{2,1,0:T(8,128)S(1)}, bf16[2,1024,4096]{2,1,0:T(8,128)...) custom-call(bf16[64,4096]{1,0:T(8,128)(2,1)} %x_ref.1, ...), custom_call_target="tpu_custom_call" | custom-call | tf_op jit(solution)/shard_map/mlp/pallas_call | solution.py:768
  273.5 2.8 %place.1 = (bf16[64,4096]{1,0:T(8,128)(2,1)}, bf16[64,4096]{1,0:T(8,128)(2,1)}, f32[512,896]{1,0:T(8,128)}, f32[512,896]{1,0:T(8,128)}, f32[896,512]{1,0:T(8,128)}) custom-call(f32[3,512,896]{2,1,0:T(8,128)S(1)} %bitcast.1, bf16[2,64,4096]{2,1,0:T(8,128)(2,1)S(1)} %get-tuple-element.9.yo, f32[2,256,896]{2,1,0:T(8,128)S(1)} %get-tuple-element.10.du), custom_call_target="tpu_custom_call" | custom-call | tf_op jit(solution)/shard_map/place/pallas_call | solution.py:809

commit v10 on v9

--- a/solution.py
+++ b/solution.py
@@ -29,7 +29,7 @@
 
 def mlp_kernel(x_ref, dy_ref, wg_ref, wu_ref, wd_ref, dw, yo, du, xd, wgf, wuf, wdf, U, V, XR, ZR, AP,
                B, A, XB, XS, WD, WX, ZB, ZS, Z2,
-               s_g, r_g, s_v, r_v, s_ap, r_ap, s_b, r_b, s_xs, r_xs, s_zs, r_zs, s_2, r_2, s_c, s_a, s_w, s_us, s_one, in_x, in_zy):
+               s_g, r_g, s_v, r_v, s_ap, r_ap, s_b, r_b, s_xs, s_zs, s_2, s_c, s_a, s_w, s_us, s_one, in_x, in_zy):
     i = lax.axis_index("dp")
     j = lax.axis_index("tp")
     x, c, z, y = i // PAIR, i % PAIR, j // 4, j % RING
@@ -48,6 +48,12 @@
     def wait(ref, sem):
         pltpu.make_async_copy(ref, ref, sem).wait()
 
+    def r_x(k, t):
+        return r_v.at[k, 4 + t // PAIR]
+
+    def r_z(i):
+        return r_g.at[i // 7, i % 7]
+
     def add(dst, src, n):
         def body(r, _):
             s = pl.ds(pl.multiple_of(r * RH, RH), RH)
@@ -215,10 +221,10 @@
         d, o = order[t]
         s = t % RING
         ii = blk(t)
-        out = [pltpu.make_async_copy(xd.at[0, :, pl.ds(pl.multiple_of(ii * CB, CB), CB)], a_slot(t), s_c.at[s, 0])]
+        out = [pltpu.make_async_copy(xd.at[0, :, pl.ds(pl.multiple_of(ii * CB, CB), CB)], a_slot(t), s_c.at[s])]
         for k in TWO:
             src = w_in[k] if t == 0 else wblk(k, xpos[d], c if o == 0 else c1)
-            out.append(pltpu.make_async_copy(src, WX.at[s % PAIR, k, pl.ds((s // PAIR) * CB, CB), :], s_c.at[s, 1]))
+            out.append(pltpu.make_async_copy(src, WX.at[s % PAIR, k, pl.ds((s // PAIR) * CB, CB), :], s_c.at[s]))
         return out
 
     def sab(t):
@@ -229,8 +235,7 @@
 
     def ab(t):
         s = t % RING
-        wait(a_slot(t), s_c.at[s, 0])
-        wait(WX.at[s % PAIR, :, pl.ds((s // PAIR) * CB, CB), :], s_c.at[s, 1])
+        wait(xd.at[0, pl.ds(0, 352)], s_c.at[s])
 
         def body(m, _):
             r = pl.ds(pl.multiple_of(m * QB, QB), QB)
@@ -267,8 +272,8 @@
         s = t % RING
         ii = blk(t)
         src = wd_ref if t == 0 else wdf.at[ii]
-        return [pltpu.make_async_copy(xd.at[1, :, pl.ds(pl.multiple_of(ii * CB, CB), CB)], a_slot(t), s_c.at[s, 0]),
-                pltpu.make_async_copy(src, WX.at[s % PAIR, s // PAIR, pl.ds(0, FB), pl.ds(0, CB)], s_c.at[s, 1])]
+        return [pltpu.make_async_copy(xd.at[1, :, pl.ds(pl.multiple_of(ii * CB, CB), CB)], a_slot(t), s_c.at[s]),
+                pltpu.make_async_copy(src, WX.at[s % PAIR, s // PAIR, pl.ds(0, FB), pl.ds(0, CB)], s_c.at[s])]
 
     def sg(t):
         have(2, *order[t])
@@ -278,9 +283,8 @@
     def gg(t):
         if t == 0:
             v_put.wait()
-        for l in ld_g(t):
-            l.wait()
         s = t % RING
+        wait(xd.at[1, pl.ds(0, 240)], s_c.at[s])
 
         def body(m, _):
             r = pl.ds(pl.multiple_of(m * QB, QB), QB)
@@ -327,7 +331,7 @@
     bp = [remote(B.at[k, 0], B.at[k, 1], s_b, r_b.at[k], "pc") for k in range(3)]
 
     def ap(arr, idx):
-        return remote(xd.at[arr, :, pl.ds(pl.multiple_of(TG * chunk(idx) + CB * c1, CB), CB)], AP.at[arr, idx], s_ap, r_ap.at[arr, idx], "pc")
+        return remote(xd.at[arr, :, pl.ds(pl.multiple_of(TG * chunk(idx) + CB * c1, CB), CB)], AP.at[arr, idx], s_ap, r_ap.at[arr * min(idx + 1, 2)], "pc")
 
     seq = (0, 1, 3, 2)
 
@@ -337,9 +341,17 @@
         return (pltpu.make_async_copy(xd.at[arr, :, pl.ds(pl.multiple_of(TG * chunk(idx) + CB * c, CB), CB)], A.at[n % PAIR, 0], s_a.at[n % PAIR]),
                 pltpu.make_async_copy(AP.at[arr, idx], A.at[n % PAIR, 1], s_a.at[n % PAIR]))
 
+    served = set()
+
     def start_a(k, n):
-        if k < UP:
-            ap(1 - k, seq[n]).wait_recv()
+        if k == DOWN and n == 0:
+            wait(AP.at[1, 0], r_ap.at[1])
+        elif k == DOWN and 2 not in served:
+            served.add(2)
+            wait(AP.at[1, pl.ds(0, 3)], r_ap.at[2])
+        elif k == GATE and 0 not in served:
+            served.add(0)
+            wait(AP.at[0], r_ap.at[0])
         for l in load_a(k, n):
             l.start()
 
@@ -364,7 +376,7 @@
     def xmsg(k, t):
         src = (XB.at[0, 0], XB.at[0, 1], XB.at[1, 1], XB.at[2, 0], XB.at[1, 0], XB.at[2, 1])[t]
         dst = du.at[t - 4] if k == UP and t >= 4 else XR.at[k, t]
-        return remote(src, dst, s_xs.at[min(t // PAIR, 1)], r_xs.at[k, t // PAIR], ("xp", "xm")[t % PAIR])
+        return remote(src, dst, s_xs.at[min(t // PAIR, 1)], r_x(k, t), ("xp", "xm")[t % PAIR])
 
     def xl(k, n):
         start_a(k, n)
@@ -397,7 +409,7 @@
         return pltpu.make_async_copy(XR.at[k, t], XS.at[4 + slot], s_one.at[1])
 
     def x3(k):
-        wait(XS.at[pl.ds(4, 2)], r_xs.at[k, 0])
+        wait(XS.at[pl.ds(4, 2)], r_x(k, 0))
         for t in TWO:
             xstage(k, t, t).start()
         wait(XS.at[pl.ds(4, 2)], s_one.at[1])
@@ -406,7 +418,7 @@
             xmsg(k, 4 + t).start()
 
     def xadd(k, ts):
-        wait(XS.at[pl.ds(4, 2)], r_xs.at[k, ts[0] // PAIR])
+        wait(XS.at[pl.ds(4, 2)], r_x(k, ts[0]))
         for h, t in enumerate(ts):
             xstage(k, t, h).start()
         wait(XS.at[pl.ds(4, 2)], s_one.at[1])
@@ -480,7 +492,7 @@
 
     def zmsg(n, col, t):
         src = ((0, 0), (0, 1), (1, 1), (3, 0), (1, 0), (3, 1))[t]
-        return remote(ZB.at[col, src[0], src[1]], ZR.at[col, n, t], s_zs.at[min(t // PAIR, 1)], r_zs.at[n, t // PAIR], link[col][t % PAIR])
+        return remote(ZB.at[col, src[0], src[1]], ZR.at[col, n, t], s_zs.at[min(t // PAIR, 1)], r_z(3 * n + t // PAIR), link[col][t % PAIR])
 
     def own(n, col, h):
         return ZB.at[col, 2 + 2 * (n % PAIR), h]
@@ -491,7 +503,7 @@
 
     def msg2(n, col, t):
         h, d = ((0, 2), (1, 2), (1, 1), (0, 3), (0, 1), (1, 3))[t]
-        return remote(sub(n, col, h, d), Z2.at[col, n, t], s_2.at[n % PAIR], r_2.at[n, min(t // PAIR, 1)], link[col][2 + t % PAIR])
+        return remote(sub(n, col, h, d), Z2.at[col, n, t], s_2.at[n % PAIR], r_z(12 + PAIR * n + min(t // PAIR, 1)), link[col][2 + t % PAIR])
 
     def p1(n):
         wait((WD, WX)[n // PAIR], s_w.at[n // PAIR])
@@ -519,7 +531,7 @@
         return pltpu.make_async_copy(ZR.at[col, n, t], ZS.at[col, slot], s_one.at[3])
 
     def stage(n, ts):
-        wait(ZS, r_zs.at[n, ts[0] // PAIR])
+        wait(ZS, r_z(3 * n + ts[0] // PAIR))
         for h, t in enumerate(ts):
             for col in TWO:
                 zstage(n, col, t, h).start()
@@ -548,7 +560,7 @@
                 msg2(n, col, t).start()
 
     def hh(n):
-        wait(Z2.at[0, 0, pl.ds(0, 4)], r_2.at[n, 0])
+        wait(Z2.at[0, 0, pl.ds(0, 4)], r_z(12 + PAIR * n))
         for t in TWO:
             for col in TWO:
                 add(sub(n, col, t, (1, 3)[t]), Z2.at[col, n, t], RW)
@@ -562,7 +574,7 @@
             for g in (AX, AD, AE):
                 wait(some(g, 960), s_g.at[g])
         done.append(n)
-        wait(Z2.at[:, 0, pl.ds(0, 4)], r_2.at[n, 1])
+        wait(Z2.at[:, 0, pl.ds(0, 4)], r_z(13 + PAIR * n))
         for col in TWO:
             q = xpos[pair(n, col)]
             for h, ts in ((0, (3, 4)), (1, (2, 5))):
@@ -756,7 +768,7 @@
             wait(ZB.at[0, pl.ds(0, 2 + 2 * q)], s_zs.at[q])
         wait(XB.at[0], s_xs.at[0])
         wait(XB.at[pl.ds(0, 2)], s_xs.at[1])
-        wait(du, r_xs.at[2, 2])
+        wait(du, r_x(UP, 4))
 
     end()
 
@@ -776,8 +788,8 @@
             V((3, 2, TG, FB), BF), V((2, 2, TG, CB), BF), V((3, 2, QB, FB), F32), V((6, QB, FB), F32),
             V((2, 2, FB, CB), BF), V((2, 2, TG, FB), BF), V((2, 5, 2, QB, CB), F32), V((2, 2, QB, CB), F32),
             V((2, 4, 6, RW, CB), F32),
-            dma((3,)), dma((3, 7)), dma((3,)), dma((3, 7)), dma, dma((2, 4)), dma, dma((3,)), dma((2,)), dma((3, 3)),
-            dma((2,)), dma((4, 3)), dma((2,)), dma((4, 2)), dma((4, 2)), dma((2,)), dma((2,)), dma((2,)), dma((7,)),
+            dma((3,)), dma((3, 7)), dma((3,)), dma((3, 7)), dma, dma((3,)), dma, dma((3,)), dma((2,)), dma((2,)), dma((2,)),
+            dma((4,)), dma((2,)), dma((2,)), dma((2,)), dma((7,)),
             pltpu.SemaphoreType.REGULAR, pltpu.SemaphoreType.REGULAR,
         ],
         compiler_params=pltpu.CompilerParams(collective_id=1, has_side_effects=True, vmem_limit_bytes=58600000),

time: 277 us -> 277 us (level)
  no operation moved by 1% of the time
where the time goes in v10:
time: 277 us; the launch traced here: 276 us
  Pallas kernels  275 us (99%)
    pallas_call x1, Pallas kernels, mlp(): pl.pallas_call(mlp_kernel, out_shape=(V((3, 2, QB, FB), F32), V((2, RW, D...  272 us

profile of v10, /device:TPU:1, one launch (start us, length us, event | category | flops | bytes accessed | tf_op | source)
XLA Modules:
  0.0 276.1 jit_solution(2931333339819189632)
XLA Ops:
  0.6 272.5 %mlp.1 = (f32[3,2,256,896]{3,2,1,0:T(8,128)S(1)}, bf16[2,64,4096]{2,1,0:T(8,128)(2,1)S(1)}, f32[2,256,896]{2,1,0:T(8,128)S(1)}, bf16[2,1024,4096]{2,1,0:T(8,128)...) custom-call(bf16[64,4096]{1,0:T(8,128)(2,1)} %x_ref.1, ...), custom_call_target="tpu_custom_call" | custom-call | tf_op jit(solution)/shard_map/mlp/pallas_call | solution.py:780
  273.1 2.8 %place.1 = (bf16[64,4096]{1,0:T(8,128)(2,1)}, bf16[64,4096]{1,0:T(8,128)(2,1)}, f32[512,896]{1,0:T(8,128)}, f32[512,896]{1,0:T(8,128)}, f32[896,512]{1,0:T(8,128)}) custom-call(f32[3,512,896]{2,1,0:T(8,128)S(1)} %bitcast.1, bf16[2,64,4096]{2,1,0:T(8,128)(2,1)S(1)} %get-tuple-element.9.yo, f32[2,256,896]{2,1,0:T(8,128)S(1)} %get-tuple-element.10.du), custom_call_target="tpu_custom_call" | custom-call | tf_op jit(solution)/shard_map/place/pallas_call | solution.py:821

commit v11 on v10

--- a/solution.py
+++ b/solution.py
@@ -29,7 +29,7 @@
 
 def mlp_kernel(x_ref, dy_ref, wg_ref, wu_ref, wd_ref, dw, yo, du, xd, wgf, wuf, wdf, U, V, XR, ZR, AP,
                B, A, XB, XS, WD, WX, ZB, ZS, Z2,
-               s_g, r_g, s_v, r_v, s_ap, r_ap, s_b, r_b, s_xs, s_zs, s_2, s_c, s_a, s_w, s_us, s_one, in_x, in_zy):
+               s_g, r_g, s_v, r_v, s_ap, r_ap, s_b, r_b, s_xs, s_zs, s_2, s_c, s_w, s_us, s_one, in_x, in_zy):
     i = lax.axis_index("dp")
     j = lax.axis_index("tp")
     x, c, z, y = i // PAIR, i % PAIR, j // 4, j % RING
@@ -265,7 +265,7 @@
         v_put.start()
 
     u_put = pltpu.make_async_copy(XB.at[pl.ds(0, 2)], U, s_one.at[0])
-    v_put = pltpu.make_async_copy(XS.at[pl.ds(0, 4)], V, s_one.at[2])
+    v_put = pltpu.make_async_copy(XS.at[pl.ds(0, 4)], V, s_one.at[1])
 
     def ld_g(t):
         d, o = order[t]
@@ -338,8 +338,8 @@
     def load_a(k, n):
         arr = 1 - min(k, 1)
         idx = seq[n]
-        return (pltpu.make_async_copy(xd.at[arr, :, pl.ds(pl.multiple_of(TG * chunk(idx) + CB * c, CB), CB)], A.at[n % PAIR, 0], s_a.at[n % PAIR]),
-                pltpu.make_async_copy(AP.at[arr, idx], A.at[n % PAIR, 1], s_a.at[n % PAIR]))
+        return (pltpu.make_async_copy(xd.at[arr, :, pl.ds(pl.multiple_of(TG * chunk(idx) + CB * c, CB), CB)], A.at[n % PAIR, 0], s_c.at[n % PAIR]),
+                pltpu.make_async_copy(AP.at[arr, idx], A.at[n % PAIR, 1], s_c.at[n % PAIR]))
 
     served = set()
 
@@ -357,7 +357,7 @@
 
     def dot_x(k, n, split=False):
         slot = n % PAIR
-        wait(A.at[slot], s_a.at[slot])
+        wait(A.at[slot], s_c.at[slot])
 
         def body(m, _):
             cols = pl.ds(pl.multiple_of(m * QB, QB), QB)
@@ -406,13 +406,13 @@
             start_a(2, 1)
 
     def xstage(k, t, slot):
-        return pltpu.make_async_copy(XR.at[k, t], XS.at[4 + slot], s_one.at[1])
+        return pltpu.make_async_copy(XR.at[k, t], XS.at[4 + slot], s_one.at[3])
 
     def x3(k):
         wait(XS.at[pl.ds(4, 2)], r_x(k, 0))
         for t in TWO:
             xstage(k, t, t).start()
-        wait(XS.at[pl.ds(4, 2)], s_one.at[1])
+        wait(XS.at[pl.ds(4, 2)], s_one.at[3])
         for t in TWO:
             add(XB.at[1 + t, t], XS.at[4 + t], QB)
             xmsg(k, 4 + t).start()
@@ -421,7 +421,7 @@
         wait(XS.at[pl.ds(4, 2)], r_x(k, ts[0]))
         for h, t in enumerate(ts):
             xstage(k, t, h).start()
-        wait(XS.at[pl.ds(4, 2)], s_one.at[1])
+        wait(XS.at[pl.ds(4, 2)], s_one.at[3])
         for h, t in enumerate(ts):
             add(dw.at[k, h], XS.at[4 + h], QB)
 
@@ -528,14 +528,14 @@
         dots_z(n, 2, 1)
 
     def zstage(n, col, t, slot):
-        return pltpu.make_async_copy(ZR.at[col, n, t], ZS.at[col, slot], s_one.at[3])
+        return pltpu.make_async_copy(ZR.at[col, n, t], ZS.at[col, slot], s_one.at[2])
 
     def stage(n, ts):
         wait(ZS, r_z(3 * n + ts[0] // PAIR))
         for h, t in enumerate(ts):
             for col in TWO:
                 zstage(n, col, t, h).start()
-        wait(ZS, s_one.at[3])
+        wait(ZS, s_one.at[2])
 
     def p4(n):
         stage(n, (0, 1))
@@ -612,18 +612,18 @@
             pl.semaphore_wait(barrier, len(across))
             tell(in_zy, across)
 
-    own_ld = [pltpu.make_async_copy(r, yo.at[k], s_one.at[4]) for k, r in enumerate((x_ref, dy_ref))]
+    own_ld = [pltpu.make_async_copy(r, yo.at[k], s_one.at[2]) for k, r in enumerate((x_ref, dy_ref))]
     for l in own_ld:
         l.start()
     barrier = pltpu.get_barrier_semaphore()
     enter()
-    put = pltpu.make_async_copy(yo, xd.at[:, pl.ds(pl.multiple_of(j * RW, RW), RW), :], s_one.at[5])
+    put = pltpu.make_async_copy(yo, xd.at[:, pl.ds(pl.multiple_of(j * RW, RW), RW), :], s_one.at[3])
     wown(WG)
     wown(WU)
     wpc(WG)
     wpc(WU)
     wpc(WL)
-    wait(yo, s_one.at[4])
+    wait(yo, s_one.at[2])
     put.start()
     enter_zy()
     ga(AX)
@@ -641,13 +641,13 @@
     ga(AE)
     gb31(AD)
     wf(WU)
+    wown(WL)
     gb0(AD)
     gend(AX)
     sab(B2)
     sab(B1)
     sab(B0)
     ab(B0)
-    wown(WL)
     ab(B1)
     gb2(AD)
     sab(B3)
@@ -789,7 +789,7 @@
             V((2, 2, FB, CB), BF), V((2, 2, TG, FB), BF), V((2, 5, 2, QB, CB), F32), V((2, 2, QB, CB), F32),
             V((2, 4, 6, RW, CB), F32),
             dma((3,)), dma((3, 7)), dma((3,)), dma((3, 7)), dma, dma((3,)), dma, dma((3,)), dma((2,)), dma((2,)), dma((2,)),
-            dma((4,)), dma((2,)), dma((2,)), dma((2,)), dma((7,)),
+            dma((4,)), dma((2,)), dma((2,)), dma((4,)),
             pltpu.SemaphoreType.REGULAR, pltpu.SemaphoreType.REGULAR,
         ],
         compiler_params=pltpu.CompilerParams(collective_id=1, has_side_effects=True, vmem_limit_bytes=58600000),
@@ -799,18 +799,20 @@
 
 
 def place_kernel(dw, yo, du, y, dx, og, ou, od, bu, bt, sem):
-    outs = [pltpu.make_async_copy(dw.at[1], og, sem.at[0]), pltpu.make_async_copy(yo.at[0], y, sem.at[1]), pltpu.make_async_copy(yo.at[1], dx, sem.at[2]),
-            pltpu.make_async_copy(bu, ou, sem.at[3]), pltpu.make_async_copy(bt, od, sem.at[4])]
-    for o in outs[:3]:
+    def put(src, dst, k):
+        o = pltpu.make_async_copy(src, dst, sem.at[k])
         o.start()
+        return o
+
+    outs = [put(dw.at[1], og, 0)]
     for h in TWO:
         r = pl.ds(QB * h, QB)
         bu[r, :] = dw[2, r, :] + du[h]
-    outs[3].start()
-    for h in TWO:
-        r = pl.ds(QB * h, QB)
-        bt[:, r] = dw[0, r, :].T
-    outs[4].start()
+        outs.append(put(bu.at[r], ou.at[r], 1 + h))
+    outs += [put(yo.at[0], y, 3), put(yo.at[1], dx, 4)]
+    for h, q in enumerate((pl.ds(0, CB), pl.ds(CB, FB - CB))):
+        bt[q, :] = dw[0, :, q].T
+        outs.append(put(bt.at[q], od.at[q], 5 + h))
     for o in outs:
         o.wait()
 
@@ -823,7 +825,7 @@
         out_shape=(sd((RW, DM), BF), sd((RW, DM), BF), sd((CB, FB), F32), sd((CB, FB), F32), sd((FB, CB), F32)),
         in_specs=[VMEM] * 3,
         out_specs=(HBM,) * 5,
-        scratch_shapes=[V((CB, FB), F32), V((FB, CB), F32), pltpu.SemaphoreType.DMA((5,))],
+        scratch_shapes=[V((CB, FB), F32), V((FB, CB), F32), pltpu.SemaphoreType.DMA((7,))],
         compiler_params=pltpu.CompilerParams(vmem_limit_bytes=24 * 2**20),
         name="place",
     )(dw.reshape(3, CB, FB), yo, du)

time: 277 us -> 277 us (level)
  no operation moved by 1% of the time
where the time goes in v11:
time: 277 us; the launch traced here: 276 us
  Pallas kernels  275 us (99%)
    pallas_call x1, Pallas kernels, mlp(): pl.pallas_call(mlp_kernel, out_shape=(V((3, 2, QB, FB), F32), V((2, RW, D...  272 us

profile of v11, /device:TPU:1, one launch (start us, length us, event | category | flops | bytes accessed | tf_op | source)
XLA Modules:
  0.0 276.1 jit_solution(15218578479983667584)
XLA Ops:
  0.6 272.4 %mlp.1 = (f32[3,2,256,896]{3,2,1,0:T(8,128)S(1)}, bf16[2,64,4096]{2,1,0:T(8,128)(2,1)S(1)}, f32[2,256,896]{2,1,0:T(8,128)S(1)}, bf16[2,1024,4096]{2,1,0:T(8,128)...) custom-call(bf16[64,4096]{1,0:T(8,128)(2,1)} %x_ref.1, ...), custom_call_target="tpu_custom_call" | custom-call | tf_op jit(solution)/shard_map/mlp/pallas_call | solution.py:780
  273.1 2.8 %place.1 = (bf16[64,4096]{1,0:T(8,128)(2,1)}, bf16[64,4096]{1,0:T(8,128)(2,1)}, f32[512,896]{1,0:T(8,128)}, f32[512,896]{1,0:T(8,128)}, f32[896,512]{1,0:T(8,128)}) custom-call(f32[3,512,896]{2,1,0:T(8,128)S(1)} %bitcast.1, bf16[2,64,4096]{2,1,0:T(8,128)(2,1)S(1)} %get-tuple-element.9.yo, f32[2,256,896]{2,1,0:T(8,128)S(1)} %get-tuple-element.10.du), custom_call_target="tpu_custom_call" | custom-call | tf_op jit(solution)/shard_map/place/pallas_call | solution.py:823

commit v12 on v11

--- a/solution.py
+++ b/solution.py
@@ -29,7 +29,7 @@
 
 def mlp_kernel(x_ref, dy_ref, wg_ref, wu_ref, wd_ref, dw, yo, du, xd, wgf, wuf, wdf, U, V, XR, ZR, AP,
                B, A, XB, XS, WD, WX, ZB, ZS, Z2,
-               s_g, r_g, s_v, r_v, s_ap, r_ap, s_b, r_b, s_xs, s_zs, s_2, s_c, s_w, s_us, s_one, in_x, in_zy):
+               s_g, r_g, s_v, r_v, s_ap, r_ap, s_b, r_b, s_xs, s_zs, s_2, s_c, s_w, s_one, in_x, in_zy):
     i = lax.axis_index("dp")
     j = lax.axis_index("tp")
     x, c, z, y = i // PAIR, i % PAIR, j // 4, j % RING
@@ -300,7 +300,7 @@
         m = q // PAIR
         r = pl.ds(pl.multiple_of((q % PAIR) * FOUR, FOUR), FOUR)
         src = U.at[m // PAIR, m % PAIR, r, :] if k == 0 else V.at[m, r, :]
-        return pltpu.make_async_copy(src, XS.at[4 + q % PAIR, pl.ds(FOUR * k, FOUR), :], s_us.at[q % PAIR])
+        return pltpu.make_async_copy(src, XS.at[4 + q % PAIR, pl.ds(FOUR * k, FOUR), :], s_c.at[2 + q % PAIR])
 
     def dadb():
         for k in TWO:
@@ -311,7 +311,7 @@
             def _():
                 for k in TWO:
                     us_load(q + 1, k).start()
-            wait(XS.at[4 + q % PAIR], s_us.at[q % PAIR])
+            wait(XS.at[4 + q % PAIR], s_c.at[2 + q % PAIR])
 
             def inner(e, _):
                 g = XS[q // PAIR, pl.ds(pl.multiple_of((q % PAIR) * FOUR + e * RH, RH), RH), :]
@@ -789,7 +789,7 @@
             V((2, 2, FB, CB), BF), V((2, 2, TG, FB), BF), V((2, 5, 2, QB, CB), F32), V((2, 2, QB, CB), F32),
             V((2, 4, 6, RW, CB), F32),
             dma((3,)), dma((3, 7)), dma((3,)), dma((3, 7)), dma, dma((3,)), dma, dma((3,)), dma((2,)), dma((2,)), dma((2,)),
-            dma((4,)), dma((2,)), dma((2,)), dma((4,)),
+            dma((4,)), dma((2,)), dma((4,)),
             pltpu.SemaphoreType.REGULAR, pltpu.SemaphoreType.REGULAR,
         ],
         compiler_params=pltpu.CompilerParams(collective_id=1, has_side_effects=True, vmem_limit_bytes=58600000),

time: 277 us -> 277 us (level)
  no operation moved by 1% of the time
where the time goes in v12:
time: 277 us; the launch traced here: 276 us
  Pallas kernels  275 us (99%)
    pallas_call x1, Pallas kernels, mlp(): pl.pallas_call(mlp_kernel, out_shape=(V((3, 2, QB, FB), F32), V((2, RW, D...  272 us

profile of v12, /device:TPU:1, one launch (start us, length us, event | category | flops | bytes accessed | tf_op | source)
XLA Modules:
  0.0 276.1 jit_solution(1026821089454919742)
XLA Ops:
  0.6 272.4 %mlp.1 = (f32[3,2,256,896]{3,2,1,0:T(8,128)S(1)}, bf16[2,64,4096]{2,1,0:T(8,128)(2,1)S(1)}, f32[2,256,896]{2,1,0:T(8,128)S(1)}, bf16[2,1024,4096]{2,1,0:T(8,128)...) custom-call(bf16[64,4096]{1,0:T(8,128)(2,1)} %x_ref.1, ...), custom_call_target="tpu_custom_call" | custom-call | tf_op jit(solution)/shard_map/mlp/pallas_call | solution.py:780
  273.1 2.8 %place.1 = (bf16[64,4096]{1,0:T(8,128)(2,1)}, bf16[64,4096]{1,0:T(8,128)(2,1)}, f32[512,896]{1,0:T(8,128)}, f32[512,896]{1,0:T(8,128)}, f32[896,512]{1,0:T(8,128)}) custom-call(f32[3,512,896]{2,1,0:T(8,128)S(1)} %bitcast.1, bf16[2,64,4096]{2,1,0:T(8,128)(2,1)S(1)} %get-tuple-element.9.yo, f32[2,256,896]{2,1,0:T(8,128)S(1)} %get-tuple-element.10.du), custom_call_target="tpu_custom_call" | custom-call | tf_op jit(solution)/shard_map/place/pallas_call | solution.py:823
